TPU v7x, 768 devices: a whole 4x8x12 slice. The times are simulated.
768 devices in a mesh: dp: 3 (over z_lo), context: 16 (over x, z_hi), tensor: 16 (over y, core).
Axes of the slice: x: 4, y: 8, z: 12 (z_hi: 4, z_lo: 3; z = z_hi * 3 + z_lo), core: 2. Of those that a mesh axis runs over, the one named last changes fastest.
Arguments:
- queries: bfloat16 [3, 4096, 8192], P('dp', 'context', 'tensor'), may hold values from -45 to 45
- keys: bfloat16 [3, 4096, 1024], P('dp', 'context'), may hold values from -20 to 20
- values: bfloat16 [3, 4096, 1024], P('dp', 'context'), may hold values from -6 to 6
- out_weight: bfloat16 [8192, 8192], P('tensor'), may hold values from -0.0625 to 0.0625
- segment_ids: int32 [3, 4096], P('dp'), may hold values from 0 to 7, as said below
- loss_mask: int32 [3, 4096], P('dp', 'context'), may hold values from 0 to 1, as said below
- span_order: int32 [32], replicated, may hold values from 0 to 31, as said below
Outputs:
- weighted_out: bfloat16 [3, 4096, 8192], P('dp', 'context', 'tensor')
Inputs may be any that keep to these rules, and one draw needn't show every extreme that they name: `span_order`: a permutation of 0 .. 31. `segment_ids`: taken in order of sequence position pos (see the steps), a sequence's document numbers never fall; each sequence holds 8 documents. `loss_mask`: the first row of every sequence is 1.
All inputs are finite; a program needn't handle non-finite values.
Results may differ from a plain program's by a relative error of at most 0.018.
Values may be sent and summed in bfloat16 or wider, within the bound.
No kernel may reach another device: no remote copies, remote signals or barrier semaphores. Data moves between devices by JAX's collectives and lax.ppermute only.
A program may use at most 64 MiB of HBM per device.

v0:
```python
import jax
import jax.numpy as jnp
import numpy as np
from jax import lax
from jax.experimental import pallas as pl
from jax.experimental.pallas import tpu as pltpu
from jax.sharding import PartitionSpec as P


HD = 128
SPAN = 128
TALLY = 8
BLOCK = SPAN + TALLY
COLS = 512
LOG2E = 1.4426950408889634
LOW = -1e30


NX, NZ, NY, NC = 4, 4, 8, 2


def inner(i, c, n):
    return ((((i - c) % n) ^ 1) + c) % n


def outer(i, c, n):
    v = (i - c) % n
    return (v + (1 if v % 2 else -1) + c) % n


def perm_context(axis, partner):
    out = []
    for x in range(NX):
        for z in range(NZ):
            for y in range(NY):
                for c in range(NC):
                    px = partner(x, c, NX) if axis == "x" else x
                    pz = partner(z, c, NZ) if axis == "z" else z
                    tensor = y * NC + c
                    out.append(((x * NZ + z) * 16 + tensor, (px * NZ + pz) * 16 + tensor))
    return out


def perm_tensor(partner):
    return [
        (y * NC + c, partner(y, c, NY) * NC + c) for y in range(NY) for c in range(NC)
    ]


SWAP = [(t, t ^ 1) for t in range(16)]


def slot_table():
    table = np.zeros((16, NC, 16), np.int32)
    for x in range(NX):
        for z in range(NZ):
            for c in range(NC):
                far = outer(z, c, NZ)
                rows = []
                for zs in ((z, inner(z, c, NZ)), (far, inner(far, c, NZ))):
                    rows += [2 * (xx * NZ + zz) + c for xx in range(NX) for zz in zs]
                table[x * NZ + z, c] = rows
    return table


def block_table():
    table = np.zeros((16, 8), np.int32)
    for y in range(NY):
        for c in range(NC):
            v = (y - c) % NY
            k, s = v // 2, v % 2
            far = (k + 2) % 4
            mid = (k + 1 - 2 * s) % 4
            near = (k - 1 + 2 * s) % 4
            order = [2 * far + s, 2 * far + 1 - s]
            order += [2 * mid + 1 - s, 2 * mid + s]
            order += [2 * near + s, 2 * near + 1 - s]
            order += [2 * k + 1 - s, 2 * k + s]
            table[y * NC + c] = [2 * ((b + c) % NY) + c for b in order]
    return table


SMEM = pl.BlockSpec(memory_space=pltpu.SMEM)
VMEM = pl.BlockSpec(memory_space=pltpu.VMEM)
HBM = pl.BlockSpec(memory_space=pltpu.HBM)


def grant(mib):
    return pltpu.CompilerParams(vmem_limit_bytes=mib * 2**20)


def prepare_kernel(k_ref, v_ref, mask_hbm, out_ref, mask_ref, sems):
    counted = pltpu.make_async_copy(mask_hbm, mask_ref, sems.at[2])
    counted.start()
    tensor = lax.axis_index("tensor")
    rows = pl.ds(pl.multiple_of(lax.rem(tensor, NC) * SPAN, SPAN), SPAN)
    cols = pl.ds(pl.multiple_of(lax.div(tensor, NC) * HD, HD), HD)
    copies = []
    for i, ref in enumerate((k_ref, v_ref)):
        into = out_ref.at[pl.ds(0, SPAN), pl.ds(i * HD, HD)]
        copies.append(pltpu.make_async_copy(ref.at[0, rows, cols], into, sems.at[i]))
        copies[-1].start()
    counted.wait()
    total = jnp.sum(mask_ref[...].astype(jnp.float32), axis=1, keepdims=True)
    out_ref[SPAN:, :] = jnp.broadcast_to(total, (TALLY, 2 * HD)).astype(jnp.bfloat16)
    for copy in copies:
        copy.wait()


def prepare(keys, values, loss_mask):
    return pl.pallas_call(
        prepare_kernel,
        out_shape=jax.ShapeDtypeStruct((BLOCK, 2 * HD), jnp.bfloat16),
        in_specs=[HBM] * 3,
        out_specs=VMEM,
        scratch_shapes=[pltpu.VMEM(loss_mask.shape, loss_mask.dtype), pltpu.SemaphoreType.DMA((3,))],
        compiler_params=grant(2),
        name="prepare",
    )(keys, values, loss_mask)


def pack_kernel(order, w_ref, out_ref, sems):
    other = (lax.axis_index("tensor") ^ 1) * 8
    copies = []
    for g in range(8):
        at = pl.multiple_of(order[other + g] * COLS, COLS)
        copies.append(pltpu.make_async_copy(w_ref.at[:, pl.ds(at, COLS)], out_ref.at[g], sems.at[g]))
        copies[-1].start()
    for copy in copies:
        copy.wait()


def pack(order, w):
    return pl.pallas_call(
        pack_kernel,
        out_shape=jax.ShapeDtypeStruct((8, w.shape[0], COLS), w.dtype),
        in_specs=[SMEM, HBM],
        out_specs=HBM,
        scratch_shapes=[pltpu.SemaphoreType.DMA((8,))],
        compiler_params=grant(2),
        name="pack",
    )(order, w)


def attention_kernel(
    slots, spans, seg_ref, q_ref, q_other_ref, a_ref, b_ref, out_ref, tally_ref, kv, q8, items, lo_ref, m_ref, l_ref, acc
):
    f32 = jnp.float32
    context = lax.axis_index("context")
    core = lax.rem(lax.axis_index("tensor"), NC)
    heads = 2 * q_ref.shape[1] // HD
    half = heads // 2
    width = heads * SPAN
    tally = jnp.zeros((TALLY, HD), f32)
    for which, ref in enumerate((a_ref, b_ref)):
        for i in range(8):
            kv[which * 8 + i] = ref[i * BLOCK : i * BLOCK + SPAN, :]
            tally += ref[i * BLOCK + SPAN : (i + 1) * BLOCK, :HD].astype(f32)
    tally_ref[...] = tally
    seg = seg_ref[...]
    starts = [jnp.sum((seg < d).astype(f32), keepdims=True) for d in range(1, 8)]
    base = (context * NC + core) * 16
    count = jnp.int32(0)
    for i in range(2):
        for h in range(heads):
            ref = q_ref if h < half else q_other_ref
            q8[i, h * SPAN : (h + 1) * SPAN, :] = ref[i * SPAN : (i + 1) * SPAN, h % half * HD : (h % half + 1) * HD]
        q_seg = seg_ref[pl.ds(2 * context + i, 1), :]
        lo = jnp.zeros((1, SPAN), f32)
        for d in range(1, 8):
            lo = jnp.where(q_seg == d, starts[d - 1], lo)
        lo_ref[i] = lo
        first = jnp.min(lo).astype(jnp.int32)
        q_pos = spans[2 * context + i]
        m_ref[i] = jnp.full((1, width), LOW, f32)
        l_ref[i] = jnp.zeros((1, width), f32)
        acc[i] = jnp.zeros((HD, width), f32)
        for b in range(16):
            pos = spans[slots[base + b]]
            items[count] = i * 16 + b
            seen = (pos <= q_pos) & ((pos + 1) * SPAN > first)
            count = count + seen.astype(jnp.int32)

    def step(j, carry):
        item = items[j]
        i, b = lax.shift_right_logical(item, 4), item & 15
        pos = lax.broadcasted_iota(jnp.int32, (SPAN, SPAN), 0) + spans[slots[base + b]] * SPAN
        hi = lax.broadcasted_iota(jnp.int32, (SPAN, SPAN), 1) + spans[2 * context + i] * SPAN
        bias = jnp.where((pos.astype(f32) >= lo_ref[i]) & (pos <= hi), 0.0, LOW)
        s = lax.dot_general(kv[b, :, :HD], q8[i], (((1,), (1,)), ((), ())), preferred_element_type=f32)
        s = s * (HD ** (-0.5) * LOG2E) + jnp.concatenate([bias] * heads, axis=1)
        old = m_ref[i]
        new = jnp.maximum(old, jnp.max(s, axis=0, keepdims=True))
        alpha = jnp.exp2(old - new)
        p = jnp.exp2(s - new)
        m_ref[i] = new
        l_ref[i] = l_ref[i] * alpha + jnp.sum(p, axis=0, keepdims=True)
        add = lax.dot_general(
            kv[b, :, HD:], p.astype(jnp.bfloat16), (((0,), (0,)), ((), ())), preferred_element_type=f32
        )
        acc[i] = acc[i] * alpha + add
        return carry

    lax.fori_loop(0, count, step, 0)
    row = lax.broadcasted_iota(jnp.int32, (TALLY, width), 0)
    for i in range(2):
        cols = slice(i * width, (i + 1) * width)
        total = l_ref[i]
        total = jnp.where(total > 0, total, 1.0)
        out_ref[:SPAN, cols] = (acc[i] / total).astype(jnp.bfloat16)
        log = m_ref[i] + jnp.log(total) * LOG2E
        high = log.astype(jnp.bfloat16).astype(f32)
        mid = (log - high).astype(jnp.bfloat16).astype(f32)
        tail = log - high - mid
        parts = jnp.where(row == 0, high, jnp.where(row == 1, mid, jnp.where(row == 2, tail, 0.0)))
        out_ref[SPAN:, cols] = parts.astype(jnp.bfloat16)


def attention(slots, spans, seg, q, q_other, a, b):
    heads = 2 * q.shape[1] // HD
    width = heads * SPAN
    return pl.pallas_call(
        attention_kernel,
        out_shape=(
            jax.ShapeDtypeStruct((BLOCK, 2 * width), jnp.bfloat16),
            jax.ShapeDtypeStruct((TALLY, HD), jnp.float32),
        ),
        in_specs=[SMEM, SMEM] + [VMEM] * 5,
        out_specs=(VMEM, VMEM),
        scratch_shapes=[
            pltpu.VMEM((16, SPAN, 2 * HD), jnp.bfloat16),
            pltpu.VMEM((2, width, HD), jnp.bfloat16),
            pltpu.SMEM((33,), jnp.int32),
            pltpu.VMEM((2, 1, SPAN), jnp.float32),
            pltpu.VMEM((2, 1, width), jnp.float32),
            pltpu.VMEM((2, 1, width), jnp.float32),
            pltpu.VMEM((2, HD, width), jnp.float32),
        ],
        compiler_params=grant(12),
        name="attend",
    )(slots, spans, seg, q, q_other, a, b)


def multiply(order, first, heads_ref, w_ref, other_ref, out_ref):
    depth = w_ref.shape[0]
    mine = lax.axis_index("tensor") * 8
    for g in range(out_ref.shape[0]):
        at = pl.multiple_of(order[mine + first + g] * COLS, COLS)
        total = jnp.dot(heads_ref[:, :depth], w_ref[:, pl.ds(at, COLS)], preferred_element_type=jnp.float32)
        total += jnp.dot(heads_ref[:, depth:], other_ref[first + g], preferred_element_type=jnp.float32)
        out_ref[g] = total.astype(jnp.bfloat16)


def join_kernel(order, mine_ref, theirs_ref, w_ref, other_ref, heads_ref, out_ref):
    f32 = jnp.float32
    width = mine_ref.shape[1] // 2
    heads = width // SPAN

    def log(ref, at):
        rows = ref[SPAN:, at : at + SPAN].astype(f32)
        return rows[0:1] + rows[1:2] + rows[2:3]

    for i in range(2):
        for h in range(heads):
            a = i * width + h * SPAN
            b = i * width + (h + heads // 2) % heads * SPAN
            log_a, log_b = log(mine_ref, a), log(theirs_ref, b)
            top = jnp.maximum(log_a, log_b)
            part_a, part_b = jnp.exp2(log_a - top), jnp.exp2(log_b - top)
            total = part_a + part_b
            joined = mine_ref[:SPAN, a : a + SPAN].astype(f32) * (part_a / total)
            joined += theirs_ref[:SPAN, b : b + SPAN].astype(f32) * (part_b / total)
            heads_ref[i * SPAN : (i + 1) * SPAN, h * HD : (h + 1) * HD] = joined.T.astype(jnp.bfloat16)
    multiply(order, 0, heads_ref, w_ref, other_ref, out_ref)


def join(order, mine, theirs, w, other):
    rows, depth = 2 * SPAN, 2 * w.shape[0]
    return pl.pallas_call(
        join_kernel,
        out_shape=(
            jax.ShapeDtypeStruct((rows, depth), jnp.bfloat16),
            jax.ShapeDtypeStruct((2, rows, COLS), jnp.bfloat16),
        ),
        in_specs=[SMEM] + [VMEM] * 4,
        out_specs=(VMEM, VMEM),
        compiler_params=grant(20),
        name="join",
    )(order, mine, theirs, w, other)


def project_kernel(order, heads_ref, w_ref, other_ref, out_ref):
    multiply(order, 2, heads_ref, w_ref, other_ref, out_ref)


def project(order, heads, w, other):
    rows = heads.shape[0]
    return pl.pallas_call(
        project_kernel,
        out_shape=jax.ShapeDtypeStruct((6, rows, COLS), jnp.bfloat16),
        in_specs=[SMEM] + [VMEM] * 3,
        out_specs=VMEM,
        compiler_params=grant(20),
        name="project",
    )(order, heads, w, other)


def add(a, b):
    return (a.astype(jnp.float32) + b.astype(jnp.float32)).astype(jnp.bfloat16)


def per_device(queries, keys, values, out_weight, segment_ids, loss_mask, span_order):
    both = ("context", "tensor")
    f32 = jnp.float32
    cat = lambda *a: jnp.concatenate(a, axis=0)
    order = jnp.asarray(block_table().reshape(-1))
    slots = jnp.asarray(slot_table().reshape(-1))
    along_x = [[x * NZ + z for x in range(NX)] for z in range(NZ)]
    gather = lambda a: lax.all_gather(a, "context", axis=0, tiled=True, axis_index_groups=along_x)

    in_hbm = lambda a: pltpu.with_memory_space_constraint(a, pltpu.HBM)

    kv1 = prepare(in_hbm(keys), in_hbm(values), in_hbm(loss_mask))
    r1 = lax.ppermute(kv1, both, perm_context("z", inner))
    q_other = lax.ppermute(queries[0], "tensor", SWAP)
    packed = pack(order, in_hbm(out_weight))
    weight_other = lax.ppermute(packed, "tensor", SWAP)
    kv2 = cat(kv1, r1)
    r2 = lax.ppermute(kv2, both, perm_context("z", outer))
    near = gather(kv2)
    far = gather(r2)
    mine, tally = attention(slots, span_order, segment_ids.reshape(32, SPAN), queries[0], q_other, near, far)
    theirs = lax.ppermute(mine, "tensor", SWAP)

    inward, outward = perm_tensor(inner), perm_tensor(outer)
    heads, far = join(order, mine, theirs, out_weight, weight_other)
    far = lax.ppermute(far, "tensor", outward)
    rest = project(order, heads, out_weight, weight_other)
    around = [(d * 16 + t, (d + 1 + t % 2) % 3 * 16 + t) for d in range(3) for t in range(16)]
    one = lax.ppermute(tally, ("dp", "tensor"), around)
    two = lax.ppermute(one, "tensor", SWAP)
    mid = lax.ppermute(add(rest[0:2], far), "tensor", inward)
    near = lax.ppermute(add(rest[2:4], mid), "tensor", outward)
    last = lax.ppermute(add(rest[4], near[0]), "tensor", inward)
    count = (tally + one + two)[0, 0]
    scale_all = lax.axis_size("dp") * lax.axis_size("context") * queries.shape[1]
    weight = loss_mask[0].astype(f32) * scale_all / count
    summed = rest[5].astype(f32) + near[1].astype(f32) + last.astype(f32)
    return (summed * weight[:, None]).astype(jnp.bfloat16)[None]


def solution(mesh):
    in_specs = (
        P("dp", "context", "tensor"),
        P("dp", "context", None),
        P("dp", "context", None),
        P("tensor", None),
        P("dp", None),
        P("dp", "context"),
        P(),
    )
    out_specs = P("dp", "context", "tensor")
    return jax.shard_map(
        per_device, mesh=mesh, in_specs=in_specs, out_specs=out_specs, check_vma=False
    )
```

profile of v0, /device:TPU:1, one launch (start us, length us, event | category | flops | bytes accessed | tf_op | source)
XLA Modules:
  0.0 118.1 jit_solution(12727752471997302973)
XLA Ops:
  0.7 3.0 %pack.1 = bf16[8,512,512]{2,1,0:T(8,128)(2,1)S(1)} custom-call(s32[128]{0:T(128)S(1)} %copy-done.3, bf16[512,8192]{1,0:T(8,128)(2,1)} %w_ref.5), custom_call_target="tpu_custom_call" | custom-call | tf_op jit(solution)/shard_map/pack/pallas_call | solution.py:134
  3.8 12.5 %collective-permute-start.4 = (bf16[8,512,512]{2,1,0:T(8,128)(2,1)S(1)}, bf16[8,512,512]{2,1,0:T(8,128)(2,1)S(1)}, u32[]{:S(2)}, u32[]{:S(2)}) collective-permute-start(bf16[8,512,512]{2,1,0:T(8,128)(2,1)S(1)} %pack.1), channel_id=1, source_target_pairs={{0,1},{1,0},{2,3},{3,2},{4,5},{5,4},{6,7},{7,6},{8,9},{9,8},{10,11... | collective-permute-start | bytes 12582920 | tf_op jit(solution)/shard_map/ppermute | solution.py:327
  16.3 0.8 prepare.1
  17.1 5.3 %collective-permute-start.1 = (bf16[136,256]{1,0:T(8,128)(2,1)S(1)}, bf16[136,256]{1,0:T(8,128)(2,1)S(1)}, u32[]{:S(2)}, u32[]{:S(2)}) collective-permute-start(bf16[136,256]{1,0:T(8,128)(2,1)S(1)} %prepare.1), channel_id=1, source_target_pairs={{0,16},{1,49},{2,18},{3,51},{4,20},{5,53},{6,22},{7,55},{8,24},{9,... | collective-permute-start | bytes 208904 | tf_op jit(solution)/shard_map/ppermute | solution.py:324
  22.4 1.9 %collective-permute-start = (bf16[256,512]{1,0:T(8,128)(2,1)S(1)}, bf16[256,512]{1,0:T(8,128)(2,1)S(1)}, u32[]{:S(2)}, u32[]{:S(2)}) collective-permute-start(bf16[256,512]{1,0:T(8,128)(2,1)S(1)} %bitcast.16), channel_id=1, source_target_pairs={{0,1},{1,0},{2,3},{3,2},{4,5},{5,4},{6,7},{7,6},{8,9},{9,8},{10,11... | collective-permute-start | bytes 786440 | tf_op jit(solution)/shard_map/ppermute | solution.py:325
  25.2 1.9 %collective-permute-start.2 = (bf16[272,256]{1,0:T(8,128)(2,1)S(1)}, bf16[272,256]{1,0:T(8,128)(2,1)S(1)}, u32[]{:S(2)}, u32[]{:S(2)}) collective-permute-start(bf16[272,256]{1,0:T(8,128)(2,1)S(1)} %pad_maximum_fusion), channel_id=1, source_target_pairs={{0,48},{1,17},{2,50},{3,19},{4,52},{5,21},{6,54},{7,23},{8,56},{9,... | collective-permute-start | bytes 417800 | tf_op jit(solution)/shard_map/ppermute | solution.py:329
  27.1 10.3 %all_gather.6.a_ref = bf16[1088,256]{1,0:T(8,128)(2,1)S(1)} all-gather(bf16[272,256]{1,0:T(8,128)(2,1)S(1)} %pad_maximum_fusion), channel_id=1, replica_groups={{0,64,128,192},{16,80,144,208},{32,96,160,224},{48,112,176,240},{1,65,1..., dimensions={0}, use_global_device_ids=true | all-gather | bytes 696320 | tf_op jit(solution)/shard_map/all_gather | solution.py:319
  37.4 11.3 %all_gather.7.b_ref = bf16[1088,256]{1,0:T(8,128)(2,1)S(1)} all-gather(bf16[272,256]{1,0:T(8,128)(2,1)S(1)} %collective-permute-done.2), channel_id=1, replica_groups={{0,64,128,192},{16,80,144,208},{32,96,160,224},{48,112,176,240},{1,65,1..., dimensions={0}, use_global_device_ids=true | all-gather | bytes 696320 | tf_op jit(solution)/shard_map/all_gather | solution.py:319
  48.7 5.6 %attend.1 = (bf16[136,2048]{1,0:T(8,128)(2,1)S(1)}, f32[8,128]{1,0:T(8,128)S(1)}) custom-call(s32[512]{0:T(512)S(1)} %copy-done.5, s32[32]{0:T(128)S(1)} %copy-done.6, s32[32,128]{1,0:T(8,128)S(1)} %bitcast.18, bf16[256,512]{1,0:T(8,128)(2,1)S(1)} %bitcast.17, bf16[256,512]{1,0:T(8,128)(2,1)S(1)} %collective-permute-done.q_other_ref, ...), custom_call_target="tpu_custom_call" | custom-call | tf_op jit(solution)/shard_map/attend/pallas_call | solution.py:222
  54.3 13.8 %collective-permute-start.3 = (bf16[136,2048]{1,0:T(8,128)(2,1)S(1)}, bf16[136,2048]{1,0:T(8,128)(2,1)S(1)}, u32[]{:S(2)}, u32[]{:S(2)}) collective-permute-start(bf16[136,2048]{1,0:T(8,128)(2,1)S(1)} %get-tuple-element.9.mine_ref), channel_id=1, source_target_pairs={{0,1},{1,0},{2,3},{3,2},{4,5},{5,4},{6,7},{7,6},{8,9},{9,8},{10,11... | collective-permute-start | bytes 1671176 | tf_op jit(solution)/shard_map/ppermute | solution.py:333
  68.2 1.6 %collective-permute-done.3.theirs_ref = bf16[136,2048]{1,0:T(8,128)(2,1)S(1)} collective-permute-done((bf16[136,2048]{1,0:T(8,128)(2,1)S(1)}, bf16[136,2048]{1,0:T(8,128)(2,1)S(1)}, u32[]{:S(2)}, u32[]{:S(2)}) %collective-permute-start.3) | collective-permute-done | bytes 557088 | tf_op jit(solution)/shard_map/ppermute | solution.py:333
  69.7 1.5 %join.1 = (bf16[256,1024]{1,0:T(8,128)(2,1)S(1)}, bf16[2,256,512]{2,1,0:T(8,128)(2,1)S(1)}) custom-call(s32[128]{0:T(128)S(1)} %copy-done.4, bf16[136,2048]{1,0:T(8,128)(2,1)S(1)} %get-tuple-element.9.mine_ref, bf16[136,2048]{1,0:T(8,128)(2,1)S(1)} %collective-permute-done.3.theirs_ref, bf16[512,8192]{1,0:T(8,128)(2,1)S(1)} %copy-done, ...), custom_call_target="tpu_custom_call" | custom-call | tf_op jit(solution)/shard_map/join/pallas_call | solution.py:279
  71.3 3.1 %collective-permute-start.5 = (bf16[2,256,512]{2,1,0:T(8,128)(2,1)S(1)}, bf16[2,256,512]{2,1,0:T(8,128)(2,1)S(1)}, u32[]{:S(2)}, u32[]{:S(2)}) collective-permute-start(bf16[2,256,512]{2,1,0:T(8,128)(2,1)S(1)} %get-tuple-element.11), channel_id=1, source_target_pairs={{0,14},{1,3},{2,4},{3,1},{4,2},{5,7},{6,8},{7,5},{8,6},{9,11},{10,... | collective-permute-start | bytes 1572872 | tf_op jit(solution)/shard_map/ppermute | solution.py:337
  74.4 2.3 %project.1 = bf16[6,256,512]{2,1,0:T(8,128)(2,1)S(1)} custom-call(s32[128]{0:T(128)S(1)} %copy-done.4, bf16[256,1024]{1,0:T(8,128)(2,1)S(1)} %get-tuple-element.10.heads_ref, bf16[512,8192]{1,0:T(8,128)(2,1)S(1)} %copy-done, bf16[8,512,512]{2,1,0:T(8,128)(2,1)S(1)} %collective-permute-done.4.other_ref), custom_call_target="tpu_custom_call" | custom-call | tf_op jit(solution)/shard_map/project/pallas_call | solution.py:298
  76.7 4.8 %collective-permute-done.5 = bf16[2,256,512]{2,1,0:T(8,128)(2,1)S(1)} collective-permute-done((bf16[2,256,512]{2,1,0:T(8,128)(2,1)S(1)}, bf16[2,256,512]{2,1,0:T(8,128)(2,1)S(1)}, u32[]{:S(2)}, u32[]{:S(2)}) %collective-permute-start.5) | collective-permute-done | bytes 524320 | tf_op jit(solution)/shard_map/ppermute | solution.py:337
  81.6 5.0 %collective-permute-start.6 = (bf16[2,256,512]{2,1,0:T(8,128)(2,1)S(1)}, bf16[2,256,512]{2,1,0:T(8,128)(2,1)S(1)}, u32[]{:S(2)}, u32[]{:S(2)}) collective-permute-start(bf16[2,256,512]{2,1,0:T(8,128)(2,1)S(1)} %add_convert_fusion.1), channel_id=1, source_target_pairs={{0,2},{1,15},{2,0},{3,5},{4,6},{5,3},{6,4},{7,9},{8,10},{9,7},{10,... | collective-permute-start | bytes 1572872 | tf_op jit(solution)/shard_map/ppermute | solution.py:342
  86.6 6.6 %collective-permute-done.6 = bf16[2,256,512]{2,1,0:T(8,128)(2,1)S(1)} collective-permute-done((bf16[2,256,512]{2,1,0:T(8,128)(2,1)S(1)}, bf16[2,256,512]{2,1,0:T(8,128)(2,1)S(1)}, u32[]{:S(2)}, u32[]{:S(2)}) %collective-permute-start.6) | collective-permute-done | bytes 524320 | tf_op jit(solution)/shard_map/ppermute | solution.py:342
  93.3 1.9 %collective-permute-start.7 = (bf16[2,256,512]{2,1,0:T(8,128)(2,1)S(1)}, bf16[2,256,512]{2,1,0:T(8,128)(2,1)S(1)}, u32[]{:S(2)}, u32[]{:S(2)}) collective-permute-start(bf16[2,256,512]{2,1,0:T(8,128)(2,1)S(1)} %add_convert_fusion), channel_id=1, source_target_pairs={{0,14},{1,3},{2,4},{3,1},{4,2},{5,7},{6,8},{7,5},{8,6},{9,11},{10,... | collective-permute-start | bytes 1572872 | tf_op jit(solution)/shard_map/ppermute | solution.py:343
  95.2 1.9 %collective-permute-start.9 = (f32[8,128]{1,0:T(8,128)S(1)}, f32[8,128]{1,0:T(8,128)S(1)}, u32[]{:S(2)}, u32[]{:S(2)}) collective-permute-start(f32[8,128]{1,0:T(8,128)S(1)} %get-tuple-element.12), channel_id=1, source_target_pairs={{0,256},{1,513},{2,258},{3,515},{4,260},{5,517},{6,262},{7,519},{8... | collective-permute-start | bytes 12296 | tf_op jit(solution)/shard_map/ppermute | solution.py:340
  97.2 2.4 %collective-permute-done.9 = f32[8,128]{1,0:T(8,128)S(1)} collective-permute-done((f32[8,128]{1,0:T(8,128)S(1)}, f32[8,128]{1,0:T(8,128)S(1)}, u32[]{:S(2)}, u32[]{:S(2)}) %collective-permute-start.9) | collective-permute-done | bytes 4128 | tf_op jit(solution)/shard_map/ppermute | solution.py:340
  99.6 9.2 %collective-permute-start.10 = (f32[8,128]{1,0:T(8,128)S(1)}, f32[8,128]{1,0:T(8,128)S(1)}, u32[]{:S(2)}, u32[]{:S(2)}) collective-permute-start(f32[8,128]{1,0:T(8,128)S(1)} %collective-permute-done.9), channel_id=1, source_target_pairs={{0,1},{1,0},{2,3},{3,2},{4,5},{5,4},{6,7},{7,6},{8,9},{9,8},{10,11... | collective-permute-start | bytes 12296 | tf_op jit(solution)/shard_map/ppermute | solution.py:341
  108.9 1.9 %collective-permute-start.8 = (bf16[256,512]{1,0:T(8,128)(2,1)S(1)}, bf16[256,512]{1,0:T(8,128)(2,1)S(1)}, u32[]{:S(2)}, u32[]{:S(2)}) collective-permute-start(bf16[256,512]{1,0:T(8,128)(2,1)S(1)} %fusion.2), channel_id=1, source_target_pairs={{0,2},{1,15},{2,0},{3,5},{4,6},{5,3},{6,4},{7,9},{8,10},{9,7},{10,... | collective-permute-start | bytes 786440 | tf_op jit(solution)/shard_map/ppermute | solution.py:344
  112.1 5.2 %collective-permute-done.8 = bf16[256,512]{1,0:T(8,128)(2,1)S(1)} collective-permute-done((bf16[256,512]{1,0:T(8,128)(2,1)S(1)}, bf16[256,512]{1,0:T(8,128)(2,1)S(1)}, u32[]{:S(2)}, u32[]{:S(2)}) %collective-permute-start.8) | collective-permute-done | bytes 262176 | tf_op jit(solution)/shard_map/ppermute | solution.py:344
  117.3 0.8 fusion.3
  (29 shorter events, 3.1 us)
Async XLA Ops:
  0.0 22.4 %copy-start.1 = (bf16[1,256,512]{2,1,0:T(8,128)(2,1)S(1)}, bf16[1,256,512]{2,1,0:T(8,128)(2,1)}, u32[]{:S(2)}) copy-start(bf16[1,256,512]{2,1,0:T(8,128)(2,1)} %param.9) | copy-start | bytes 786436
  0.0 0.7 copy-start.3
  0.7 69.0 %copy-start = (bf16[512,8192]{1,0:T(8,128)(2,1)S(1)}, bf16[512,8192]{1,0:T(8,128)(2,1)}, u32[]{:S(2)}) copy-start(bf16[512,8192]{1,0:T(8,128)(2,1)} %w_ref.5) | copy-start | bytes 25165828
  3.7 45.0 %copy-start.2 = (s32[1,4096]{1,0:T(1,128)S(1)}, s32[1,4096]{1,0:T(1,128)}, u32[]{:S(2)}) copy-start(s32[1,4096]{1,0:T(1,128)} %param.13) | copy-start | bytes 49156
  3.8 45.0 %copy-start.5 = (s32[512]{0:T(512)S(1)}, s32[512]{0:T(512)}, u32[]{:S(2)}) copy-start(s32[512]{0:T(512)} %constant.7.clone.slots) | copy-start | bytes 6148
  3.8 44.9 %copy-start.6 = (s32[32]{0:T(128)S(1)}, s32[32]{0:T(128)}, u32[]{:S(2)}) copy-start(s32[32]{0:T(128)} %spans.1) | copy-start | bytes 388
  3.8 66.0 %collective-permute-start.4 = (bf16[8,512,512]{2,1,0:T(8,128)(2,1)S(1)}, bf16[8,512,512]{2,1,0:T(8,128)(2,1)S(1)}, u32[]{:S(2)}, u32[]{:S(2)}) collective-permute-start(bf16[8,512,512]{2,1,0:T(8,128)(2,1)S(1)} %pack.1), channel_id=1, source_target_pairs={{0,1},{1,0},{2,3},{3,2},{4,5},{5,4},{6,7},{7,6},{8,9},{9,8},{10,11... | collective-permute-start | bytes 12582920 | tf_op jit(solution)/shard_map/ppermute | solution.py:327
  17.1 8.1 %collective-permute-start.1 = (bf16[136,256]{1,0:T(8,128)(2,1)S(1)}, bf16[136,256]{1,0:T(8,128)(2,1)S(1)}, u32[]{:S(2)}, u32[]{:S(2)}) collective-permute-start(bf16[136,256]{1,0:T(8,128)(2,1)S(1)} %prepare.1), channel_id=1, source_target_pairs={{0,16},{1,49},{2,18},{3,51},{4,20},{5,53},{6,22},{7,55},{8,24},{9,... | collective-permute-start | bytes 208904 | tf_op jit(solution)/shard_map/ppermute | solution.py:324
  22.4 26.3 %collective-permute-start = (bf16[256,512]{1,0:T(8,128)(2,1)S(1)}, bf16[256,512]{1,0:T(8,128)(2,1)S(1)}, u32[]{:S(2)}, u32[]{:S(2)}) collective-permute-start(bf16[256,512]{1,0:T(8,128)(2,1)S(1)} %bitcast.16), channel_id=1, source_target_pairs={{0,1},{1,0},{2,3},{3,2},{4,5},{5,4},{6,7},{7,6},{8,9},{9,8},{10,11... | collective-permute-start | bytes 786440 | tf_op jit(solution)/shard_map/ppermute | solution.py:325
  25.2 44.5 %copy-start.4 = (s32[128]{0:T(128)S(1)}, s32[128]{0:T(128)}, u32[]{:S(2)}) copy-start(s32[128]{0:T(128)} %constant.6.clone.order) | copy-start | bytes 1540
  25.2 12.2 %collective-permute-start.2 = (bf16[272,256]{1,0:T(8,128)(2,1)S(1)}, bf16[272,256]{1,0:T(8,128)(2,1)S(1)}, u32[]{:S(2)}, u32[]{:S(2)}) collective-permute-start(bf16[272,256]{1,0:T(8,128)(2,1)S(1)} %pad_maximum_fusion), channel_id=1, source_target_pairs={{0,48},{1,17},{2,50},{3,19},{4,52},{5,21},{6,54},{7,23},{8,56},{9,... | collective-permute-start | bytes 417800 | tf_op jit(solution)/shard_map/ppermute | solution.py:329
  54.3 15.4 %collective-permute-start.3 = (bf16[136,2048]{1,0:T(8,128)(2,1)S(1)}, bf16[136,2048]{1,0:T(8,128)(2,1)S(1)}, u32[]{:S(2)}, u32[]{:S(2)}) collective-permute-start(bf16[136,2048]{1,0:T(8,128)(2,1)S(1)} %get-tuple-element.9.mine_ref), channel_id=1, source_target_pairs={{0,1},{1,0},{2,3},{3,2},{4,5},{5,4},{6,7},{7,6},{8,9},{9,8},{10,11... | collective-permute-start | bytes 1671176 | tf_op jit(solution)/shard_map/ppermute | solution.py:333
  71.3 10.2 %collective-permute-start.5 = (bf16[2,256,512]{2,1,0:T(8,128)(2,1)S(1)}, bf16[2,256,512]{2,1,0:T(8,128)(2,1)S(1)}, u32[]{:S(2)}, u32[]{:S(2)}) collective-permute-start(bf16[2,256,512]{2,1,0:T(8,128)(2,1)S(1)} %get-tuple-element.11), channel_id=1, source_target_pairs={{0,14},{1,3},{2,4},{3,1},{4,2},{5,7},{6,8},{7,5},{8,6},{9,11},{10,... | collective-permute-start | bytes 1572872 | tf_op jit(solution)/shard_map/ppermute | solution.py:337
  81.6 29.8 %copy-start.7 = (s32[1,256]{1,0:T(1,128)S(1)}, s32[1,256]{1,0:T(1,128)}, u32[]{:S(2)}) copy-start(s32[1,256]{1,0:T(1,128)} %mask_hbm.1) | copy-start | bytes 3076
  81.6 11.5 %collective-permute-start.6 = (bf16[2,256,512]{2,1,0:T(8,128)(2,1)S(1)}, bf16[2,256,512]{2,1,0:T(8,128)(2,1)S(1)}, u32[]{:S(2)}, u32[]{:S(2)}) collective-permute-start(bf16[2,256,512]{2,1,0:T(8,128)(2,1)S(1)} %add_convert_fusion.1), channel_id=1, source_target_pairs={{0,2},{1,15},{2,0},{3,5},{4,6},{5,3},{6,4},{7,9},{8,10},{9,7},{10,... | collective-permute-start | bytes 1572872 | tf_op jit(solution)/shard_map/ppermute | solution.py:342
  93.3 15.5 %collective-permute-start.7 = (bf16[2,256,512]{2,1,0:T(8,128)(2,1)S(1)}, bf16[2,256,512]{2,1,0:T(8,128)(2,1)S(1)}, u32[]{:S(2)}, u32[]{:S(2)}) collective-permute-start(bf16[2,256,512]{2,1,0:T(8,128)(2,1)S(1)} %add_convert_fusion), channel_id=1, source_target_pairs={{0,14},{1,3},{2,4},{3,1},{4,2},{5,7},{6,8},{7,5},{8,6},{9,11},{10,... | collective-permute-start | bytes 1572872 | tf_op jit(solution)/shard_map/ppermute | solution.py:343
  95.2 4.4 %collective-permute-start.9 = (f32[8,128]{1,0:T(8,128)S(1)}, f32[8,128]{1,0:T(8,128)S(1)}, u32[]{:S(2)}, u32[]{:S(2)}) collective-permute-start(f32[8,128]{1,0:T(8,128)S(1)} %get-tuple-element.12), channel_id=1, source_target_pairs={{0,256},{1,513},{2,258},{3,515},{4,260},{5,517},{6,262},{7,519},{8... | collective-permute-start | bytes 12296 | tf_op jit(solution)/shard_map/ppermute | solution.py:340
  99.6 11.3 %collective-permute-start.10 = (f32[8,128]{1,0:T(8,128)S(1)}, f32[8,128]{1,0:T(8,128)S(1)}, u32[]{:S(2)}, u32[]{:S(2)}) collective-permute-start(f32[8,128]{1,0:T(8,128)S(1)} %collective-permute-done.9), channel_id=1, source_target_pairs={{0,1},{1,0},{2,3},{3,2},{4,5},{5,4},{6,7},{7,6},{8,9},{9,8},{10,11... | collective-permute-start | bytes 12296 | tf_op jit(solution)/shard_map/ppermute | solution.py:341
  108.9 8.3 %collective-permute-start.8 = (bf16[256,512]{1,0:T(8,128)(2,1)S(1)}, bf16[256,512]{1,0:T(8,128)(2,1)S(1)}, u32[]{:S(2)}, u32[]{:S(2)}) collective-permute-start(bf16[256,512]{1,0:T(8,128)(2,1)S(1)} %fusion.2), channel_id=1, source_target_pairs={{0,2},{1,15},{2,0},{3,5},{4,6},{5,3},{6,4},{7,9},{8,10},{9,7},{10,... | collective-permute-start | bytes 786440 | tf_op jit(solution)/shard_map/ppermute | solution.py:344
where the time goes:
time: 119 us; the launch traced here: 118 us
  starting transfers between devices  58.6 us (49%)
  blocking collectives  21.5 us (18%)
  waiting for transfers between devices  21.3 us (18%)
  Pallas kernels  13.3 us (11%)
  other arithmetic  1.83 us (2%)
  local copies, waits for them, and re-layouts  1.25 us (1%)
    all_gather x2, blocking collectives, per_device(): lax.all_gather(a, 'context', axis=0, tiled=True, axis_index_groups=along_x)  21.5 us
    ppermute x1, starting transfers between devices, per_device(): theirs = lax.ppermute(mine, 'tensor', SWAP)  13.8 us
    ppermute x1, starting transfers between devices, per_device(): weight_other = lax.ppermute(packed, 'tensor', SWAP)  12.5 us
    ppermute x1, starting transfers between devices, per_device(): two = lax.ppermute(one, 'tensor', SWAP)  9.25 us
    ppermute x1, waiting for transfers between devices, per_device(): mid = lax.ppermute(add(rest[0:2], far), 'tensor', inward)  6.56 us
    pallas_call x1, Pallas kernels, attention(): pl.pallas_call(attention_kernel, out_shape=(jax.ShapeDtypeStruct((BLOCK,...  5.61 us
    ppermute x1, starting transfers between devices, per_device(): r1 = lax.ppermute(kv1, both, perm_context('z', inner))  5.3 us
    ppermute x1, waiting for transfers between devices, per_device(): last = lax.ppermute(add(rest[4], near[0]), 'tensor', inward)  5.2 us
  transfers between devices with their start and end apart: 11, of which 6 were waited for; matrix products, arithmetic and copies ran while one was open for 1% of the time, Pallas kernels for 7%

commit v1 on v0

--- a/solution.py
+++ b/solution.py
@@ -57,7 +57,7 @@
             for c in range(NC):
                 far = outer(z, c, NZ)
                 rows = []
-                for zs in ((z, inner(z, c, NZ)), (far, inner(far, c, NZ))):
+                for zs in ((z,), (inner(z, c, NZ), far, inner(far, c, NZ))):
                     rows += [2 * (xx * NZ + zz) + c for xx in range(NX) for zz in zs]
                 table[x * NZ + z, c] = rows
     return table
@@ -152,10 +152,12 @@
     half = heads // 2
     width = heads * SPAN
     tally = jnp.zeros((TALLY, HD), f32)
-    for which, ref in enumerate((a_ref, b_ref)):
-        for i in range(8):
-            kv[which * 8 + i] = ref[i * BLOCK : i * BLOCK + SPAN, :]
+    at = 0
+    for ref in (a_ref, b_ref):
+        for i in range(ref.shape[0] // BLOCK):
+            kv[at] = ref[i * BLOCK : i * BLOCK + SPAN, :]
             tally += ref[i * BLOCK + SPAN : (i + 1) * BLOCK, :HD].astype(f32)
+            at += 1
     tally_ref[...] = tally
     seg = seg_ref[...]
     starts = [jnp.sum((seg < d).astype(f32), keepdims=True) for d in range(1, 8)]
@@ -322,13 +324,12 @@
 
     kv1 = prepare(in_hbm(keys), in_hbm(values), in_hbm(loss_mask))
     r1 = lax.ppermute(kv1, both, perm_context("z", inner))
+    near = gather(kv1)
+    r2 = lax.ppermute(cat(kv1, r1), both, perm_context("z", outer))
     q_other = lax.ppermute(queries[0], "tensor", SWAP)
     packed = pack(order, in_hbm(out_weight))
     weight_other = lax.ppermute(packed, "tensor", SWAP)
-    kv2 = cat(kv1, r1)
-    r2 = lax.ppermute(kv2, both, perm_context("z", outer))
-    near = gather(kv2)
-    far = gather(r2)
+    far = gather(cat(r1, r2))
     mine, tally = attention(slots, span_order, segment_ids.reshape(32, SPAN), queries[0], q_other, near, far)
     theirs = lax.ppermute(mine, "tensor", SWAP)
 

time: 119 us -> 121 us (1.017)
  starting transfers between devices: 58.6 us -> 60.5 us
  waiting for transfers between devices: 21.3 us -> 23.2 us
    ppermute x1, starting transfers between devices: 1.92 us -> 7.75 us  [per_device(): q_other = lax.ppermute(queries[0], 'tensor', SWAP)]
    ppermute x1, starting transfers between devices: 13.8 us -> 9.85 us  [per_device(): theirs = lax.ppermute(mine, 'tensor', SWAP)]
    ppermute x1, waiting for transfers between devices: 0.81 us -> 2.75 us  [per_device(): r1 = lax.ppermute(kv1, both, perm_context('z', inner))]
where the time goes in v1:
time: 121 us
  starting transfers between devices  60.5 us (50%)
  waiting for transfers between devices  23.2 us (19%)
  blocking collectives  20.4 us (17%)
  Pallas kernels  13.3 us (11%)
  other arithmetic  1.85 us (2%)
  local copies, waits for them, and re-layouts  1.25 us (1%)
    all_gather x2, blocking collectives, per_device(): lax.all_gather(a, 'context', axis=0, tiled=True, axis_index_groups=along_x)  20.4 us
    ppermute x1, starting transfers between devices, per_device(): weight_other = lax.ppermute(packed, 'tensor', SWAP)  12.5 us
    ppermute x1, starting transfers between devices, per_device(): theirs = lax.ppermute(mine, 'tensor', SWAP)  9.85 us
    ppermute x1, starting transfers between devices, per_device(): two = lax.ppermute(one, 'tensor', SWAP)  9.25 us
    ppermute x1, starting transfers between devices, per_device(): q_other = lax.ppermute(queries[0], 'tensor', SWAP)  7.75 us
    ppermute x1, waiting for transfers between devices, per_device(): mid = lax.ppermute(add(rest[0:2], far), 'tensor', inward)  6.56 us
    pallas_call x1, Pallas kernels, attention(): pl.pallas_call(attention_kernel, out_shape=(jax.ShapeDtypeStruct((BLOCK,...  5.62 us
    ppermute x1, starting transfers between devices, per_device(): r1 = lax.ppermute(kv1, both, perm_context('z', inner))  5.3 us
  transfers between devices with their start and end apart: 11, of which 6 were waited for; matrix products, arithmetic and copies ran while one was open for 1% of the time, Pallas kernels for 7%

profile of v1, /device:TPU:1, one launch (start us, length us, event | category | flops | bytes accessed | tf_op | source)
XLA Modules:
  0.0 120.8 jit_solution(3268230625875080591)
XLA Ops:
  0.7 3.0 %pack.1 = bf16[8,512,512]{2,1,0:T(8,128)(2,1)S(1)} custom-call(s32[128]{0:T(128)S(1)} %copy-done.3, bf16[512,8192]{1,0:T(8,128)(2,1)} %w_ref.5), custom_call_target="tpu_custom_call" | custom-call | tf_op jit(solution)/shard_map/pack/pallas_call | solution.py:134
  3.8 12.5 %collective-permute-start.4 = (bf16[8,512,512]{2,1,0:T(8,128)(2,1)S(1)}, bf16[8,512,512]{2,1,0:T(8,128)(2,1)S(1)}, u32[]{:S(2)}, u32[]{:S(2)}) collective-permute-start(bf16[8,512,512]{2,1,0:T(8,128)(2,1)S(1)} %pack.1), channel_id=1, source_target_pairs={{0,1},{1,0},{2,3},{3,2},{4,5},{5,4},{6,7},{7,6},{8,9},{9,8},{10,11... | collective-permute-start | bytes 12582920 | tf_op jit(solution)/shard_map/ppermute | solution.py:331
  17.1 5.3 %collective-permute-start.1 = (bf16[136,256]{1,0:T(8,128)(2,1)S(1)}, bf16[136,256]{1,0:T(8,128)(2,1)S(1)}, u32[]{:S(2)}, u32[]{:S(2)}) collective-permute-start(bf16[136,256]{1,0:T(8,128)(2,1)S(1)} %prepare.1), channel_id=1, source_target_pairs={{0,16},{1,49},{2,18},{3,51},{4,20},{5,53},{6,22},{7,55},{8,24},{9,... | collective-permute-start | bytes 208904 | tf_op jit(solution)/shard_map/ppermute | solution.py:326
  22.4 2.8 %collective-permute-done.1 = bf16[136,256]{1,0:T(8,128)(2,1)S(1)} collective-permute-done((bf16[136,256]{1,0:T(8,128)(2,1)S(1)}, bf16[136,256]{1,0:T(8,128)(2,1)S(1)}, u32[]{:S(2)}, u32[]{:S(2)}) %collective-permute-start.1) | collective-permute-done | bytes 69664 | tf_op jit(solution)/shard_map/ppermute | solution.py:326
  25.2 1.9 %collective-permute-start.2 = (bf16[272,256]{1,0:T(8,128)(2,1)S(1)}, bf16[272,256]{1,0:T(8,128)(2,1)S(1)}, u32[]{:S(2)}, u32[]{:S(2)}) collective-permute-start(bf16[272,256]{1,0:T(8,128)(2,1)S(1)} %pad_maximum_fusion.1), channel_id=1, source_target_pairs={{0,48},{1,17},{2,50},{3,19},{4,52},{5,21},{6,54},{7,23},{8,56},{9,... | collective-permute-start | bytes 417800 | tf_op jit(solution)/shard_map/ppermute | solution.py:328
  27.1 7.7 %collective-permute-start = (bf16[256,512]{1,0:T(8,128)(2,1)S(1)}, bf16[256,512]{1,0:T(8,128)(2,1)S(1)}, u32[]{:S(2)}, u32[]{:S(2)}) collective-permute-start(bf16[256,512]{1,0:T(8,128)(2,1)S(1)} %bitcast.16), channel_id=1, source_target_pairs={{0,1},{1,0},{2,3},{3,2},{4,5},{5,4},{6,7},{7,6},{8,9},{9,8},{10,11... | collective-permute-start | bytes 786440 | tf_op jit(solution)/shard_map/ppermute | solution.py:329
  34.9 9.5 %all_gather.6.a_ref = bf16[544,256]{1,0:T(8,128)(2,1)S(1)} all-gather(bf16[136,256]{1,0:T(8,128)(2,1)S(1)} %prepare.1), channel_id=1, replica_groups={{0,64,128,192},{16,80,144,208},{32,96,160,224},{48,112,176,240},{1,65,1..., dimensions={0}, use_global_device_ids=true | all-gather | bytes 348160 | tf_op jit(solution)/shard_map/all_gather | solution.py:321
  44.4 10.9 %all_gather.7.b_ref = bf16[1632,256]{1,0:T(8,128)(2,1)S(1)} all-gather(bf16[408,256]{1,0:T(8,128)(2,1)S(1)} %pad_maximum_fusion), channel_id=1, replica_groups={{0,64,128,192},{16,80,144,208},{32,96,160,224},{48,112,176,240},{1,65,1..., dimensions={0}, use_global_device_ids=true | all-gather | bytes 1044480 | tf_op jit(solution)/shard_map/all_gather | solution.py:321
  55.3 5.6 %attend.1 = (bf16[136,2048]{1,0:T(8,128)(2,1)S(1)}, f32[8,128]{1,0:T(8,128)S(1)}) custom-call(s32[512]{0:T(512)S(1)} %copy-done.5, s32[32]{0:T(128)S(1)} %copy-done.6, s32[32,128]{1,0:T(8,128)S(1)} %bitcast.18, bf16[256,512]{1,0:T(8,128)(2,1)S(1)} %bitcast.17, bf16[256,512]{1,0:T(8,128)(2,1)S(1)} %collective-permute-done.q_other_ref, ...), custom_call_target="tpu_custom_call" | custom-call | tf_op jit(solution)/shard_map/attend/pallas_call | solution.py:224
  61.0 9.9 %collective-permute-start.3 = (bf16[136,2048]{1,0:T(8,128)(2,1)S(1)}, bf16[136,2048]{1,0:T(8,128)(2,1)S(1)}, u32[]{:S(2)}, u32[]{:S(2)}) collective-permute-start(bf16[136,2048]{1,0:T(8,128)(2,1)S(1)} %get-tuple-element.9.mine_ref), channel_id=1, source_target_pairs={{0,1},{1,0},{2,3},{3,2},{4,5},{5,4},{6,7},{7,6},{8,9},{9,8},{10,11... | collective-permute-start | bytes 1671176 | tf_op jit(solution)/shard_map/ppermute | solution.py:334
  70.8 1.6 %collective-permute-done.3.theirs_ref = bf16[136,2048]{1,0:T(8,128)(2,1)S(1)} collective-permute-done((bf16[136,2048]{1,0:T(8,128)(2,1)S(1)}, bf16[136,2048]{1,0:T(8,128)(2,1)S(1)}, u32[]{:S(2)}, u32[]{:S(2)}) %collective-permute-start.3) | collective-permute-done | bytes 557088 | tf_op jit(solution)/shard_map/ppermute | solution.py:334
  72.4 1.5 %join.1 = (bf16[256,1024]{1,0:T(8,128)(2,1)S(1)}, bf16[2,256,512]{2,1,0:T(8,128)(2,1)S(1)}) custom-call(s32[128]{0:T(128)S(1)} %copy-done.4, bf16[136,2048]{1,0:T(8,128)(2,1)S(1)} %get-tuple-element.9.mine_ref, bf16[136,2048]{1,0:T(8,128)(2,1)S(1)} %collective-permute-done.3.theirs_ref, bf16[512,8192]{1,0:T(8,128)(2,1)S(1)} %copy-done, ...), custom_call_target="tpu_custom_call" | custom-call | tf_op jit(solution)/shard_map/join/pallas_call | solution.py:281
  73.9 3.1 %collective-permute-start.5 = (bf16[2,256,512]{2,1,0:T(8,128)(2,1)S(1)}, bf16[2,256,512]{2,1,0:T(8,128)(2,1)S(1)}, u32[]{:S(2)}, u32[]{:S(2)}) collective-permute-start(bf16[2,256,512]{2,1,0:T(8,128)(2,1)S(1)} %get-tuple-element.11), channel_id=1, source_target_pairs={{0,14},{1,3},{2,4},{3,1},{4,2},{5,7},{6,8},{7,5},{8,6},{9,11},{10,... | collective-permute-start | bytes 1572872 | tf_op jit(solution)/shard_map/ppermute | solution.py:338
  77.1 2.3 %project.1 = bf16[6,256,512]{2,1,0:T(8,128)(2,1)S(1)} custom-call(s32[128]{0:T(128)S(1)} %copy-done.4, bf16[256,1024]{1,0:T(8,128)(2,1)S(1)} %get-tuple-element.10.heads_ref, bf16[512,8192]{1,0:T(8,128)(2,1)S(1)} %copy-done, bf16[8,512,512]{2,1,0:T(8,128)(2,1)S(1)} %collective-permute-done.4.other_ref), custom_call_target="tpu_custom_call" | custom-call | tf_op jit(solution)/shard_map/project/pallas_call | solution.py:300
  79.4 4.7 %collective-permute-done.5 = bf16[2,256,512]{2,1,0:T(8,128)(2,1)S(1)} collective-permute-done((bf16[2,256,512]{2,1,0:T(8,128)(2,1)S(1)}, bf16[2,256,512]{2,1,0:T(8,128)(2,1)S(1)}, u32[]{:S(2)}, u32[]{:S(2)}) %collective-permute-start.5) | collective-permute-done | bytes 524320 | tf_op jit(solution)/shard_map/ppermute | solution.py:338
  84.3 5.0 %collective-permute-start.6 = (bf16[2,256,512]{2,1,0:T(8,128)(2,1)S(1)}, bf16[2,256,512]{2,1,0:T(8,128)(2,1)S(1)}, u32[]{:S(2)}, u32[]{:S(2)}) collective-permute-start(bf16[2,256,512]{2,1,0:T(8,128)(2,1)S(1)} %add_convert_fusion.1), channel_id=1, source_target_pairs={{0,2},{1,15},{2,0},{3,5},{4,6},{5,3},{6,4},{7,9},{8,10},{9,7},{10,... | collective-permute-start | bytes 1572872 | tf_op jit(solution)/shard_map/ppermute | solution.py:343
  89.3 6.6 %collective-permute-done.6 = bf16[2,256,512]{2,1,0:T(8,128)(2,1)S(1)} collective-permute-done((bf16[2,256,512]{2,1,0:T(8,128)(2,1)S(1)}, bf16[2,256,512]{2,1,0:T(8,128)(2,1)S(1)}, u32[]{:S(2)}, u32[]{:S(2)}) %collective-permute-start.6) | collective-permute-done | bytes 524320 | tf_op jit(solution)/shard_map/ppermute | solution.py:343
  96.0 1.9 %collective-permute-start.7 = (bf16[2,256,512]{2,1,0:T(8,128)(2,1)S(1)}, bf16[2,256,512]{2,1,0:T(8,128)(2,1)S(1)}, u32[]{:S(2)}, u32[]{:S(2)}) collective-permute-start(bf16[2,256,512]{2,1,0:T(8,128)(2,1)S(1)} %add_convert_fusion), channel_id=1, source_target_pairs={{0,14},{1,3},{2,4},{3,1},{4,2},{5,7},{6,8},{7,5},{8,6},{9,11},{10,... | collective-permute-start | bytes 1572872 | tf_op jit(solution)/shard_map/ppermute | solution.py:344
  97.9 1.9 %collective-permute-start.9 = (f32[8,128]{1,0:T(8,128)S(1)}, f32[8,128]{1,0:T(8,128)S(1)}, u32[]{:S(2)}, u32[]{:S(2)}) collective-permute-start(f32[8,128]{1,0:T(8,128)S(1)} %get-tuple-element.12), channel_id=1, source_target_pairs={{0,256},{1,513},{2,258},{3,515},{4,260},{5,517},{6,262},{7,519},{8... | collective-permute-start | bytes 12296 | tf_op jit(solution)/shard_map/ppermute | solution.py:341
  99.9 2.4 %collective-permute-done.9 = f32[8,128]{1,0:T(8,128)S(1)} collective-permute-done((f32[8,128]{1,0:T(8,128)S(1)}, f32[8,128]{1,0:T(8,128)S(1)}, u32[]{:S(2)}, u32[]{:S(2)}) %collective-permute-start.9) | collective-permute-done | bytes 4128 | tf_op jit(solution)/shard_map/ppermute | solution.py:341
  102.3 9.3 %collective-permute-start.10 = (f32[8,128]{1,0:T(8,128)S(1)}, f32[8,128]{1,0:T(8,128)S(1)}, u32[]{:S(2)}, u32[]{:S(2)}) collective-permute-start(f32[8,128]{1,0:T(8,128)S(1)} %collective-permute-done.9), channel_id=1, source_target_pairs={{0,1},{1,0},{2,3},{3,2},{4,5},{5,4},{6,7},{7,6},{8,9},{9,8},{10,11... | collective-permute-start | bytes 12296 | tf_op jit(solution)/shard_map/ppermute | solution.py:342
  111.6 1.9 %collective-permute-start.8 = (bf16[256,512]{1,0:T(8,128)(2,1)S(1)}, bf16[256,512]{1,0:T(8,128)(2,1)S(1)}, u32[]{:S(2)}, u32[]{:S(2)}) collective-permute-start(bf16[256,512]{1,0:T(8,128)(2,1)S(1)} %fusion.2), channel_id=1, source_target_pairs={{0,2},{1,15},{2,0},{3,5},{4,6},{5,3},{6,4},{7,9},{8,10},{9,7},{10,... | collective-permute-start | bytes 786440 | tf_op jit(solution)/shard_map/ppermute | solution.py:345
  114.8 5.2 %collective-permute-done.8 = bf16[256,512]{1,0:T(8,128)(2,1)S(1)} collective-permute-done((bf16[256,512]{1,0:T(8,128)(2,1)S(1)}, bf16[256,512]{1,0:T(8,128)(2,1)S(1)}, u32[]{:S(2)}, u32[]{:S(2)}) %collective-permute-start.8) | collective-permute-done | bytes 262176 | tf_op jit(solution)/shard_map/ppermute | solution.py:345
  120.0 0.8 fusion.3
  (30 shorter events, 3.1 us)
Async XLA Ops:
  0.0 27.1 %copy-start.1 = (bf16[1,256,512]{2,1,0:T(8,128)(2,1)S(1)}, bf16[1,256,512]{2,1,0:T(8,128)(2,1)}, u32[]{:S(2)}) copy-start(bf16[1,256,512]{2,1,0:T(8,128)(2,1)} %param.9) | copy-start | bytes 786436
  0.0 0.7 copy-start.3
  0.7 71.7 %copy-start = (bf16[512,8192]{1,0:T(8,128)(2,1)S(1)}, bf16[512,8192]{1,0:T(8,128)(2,1)}, u32[]{:S(2)}) copy-start(bf16[512,8192]{1,0:T(8,128)(2,1)} %w_ref.5) | copy-start | bytes 25165828
  3.7 51.6 %copy-start.2 = (s32[1,4096]{1,0:T(1,128)S(1)}, s32[1,4096]{1,0:T(1,128)}, u32[]{:S(2)}) copy-start(s32[1,4096]{1,0:T(1,128)} %param.13) | copy-start | bytes 49156
  3.8 51.6 %copy-start.5 = (s32[512]{0:T(512)S(1)}, s32[512]{0:T(512)}, u32[]{:S(2)}) copy-start(s32[512]{0:T(512)} %constant.7.clone.slots) | copy-start | bytes 6148
  3.8 51.6 %copy-start.6 = (s32[32]{0:T(128)S(1)}, s32[32]{0:T(128)}, u32[]{:S(2)}) copy-start(s32[32]{0:T(128)} %spans.1) | copy-start | bytes 388
  3.8 68.6 %collective-permute-start.4 = (bf16[8,512,512]{2,1,0:T(8,128)(2,1)S(1)}, bf16[8,512,512]{2,1,0:T(8,128)(2,1)S(1)}, u32[]{:S(2)}, u32[]{:S(2)}) collective-permute-start(bf16[8,512,512]{2,1,0:T(8,128)(2,1)S(1)} %pack.1), channel_id=1, source_target_pairs={{0,1},{1,0},{2,3},{3,2},{4,5},{5,4},{6,7},{7,6},{8,9},{9,8},{10,11... | collective-permute-start | bytes 12582920 | tf_op jit(solution)/shard_map/ppermute | solution.py:331
  17.1 8.1 %collective-permute-start.1 = (bf16[136,256]{1,0:T(8,128)(2,1)S(1)}, bf16[136,256]{1,0:T(8,128)(2,1)S(1)}, u32[]{:S(2)}, u32[]{:S(2)}) collective-permute-start(bf16[136,256]{1,0:T(8,128)(2,1)S(1)} %prepare.1), channel_id=1, source_target_pairs={{0,16},{1,49},{2,18},{3,51},{4,20},{5,53},{6,22},{7,55},{8,24},{9,... | collective-permute-start | bytes 208904 | tf_op jit(solution)/shard_map/ppermute | solution.py:326
  25.2 19.2 %collective-permute-start.2 = (bf16[272,256]{1,0:T(8,128)(2,1)S(1)}, bf16[272,256]{1,0:T(8,128)(2,1)S(1)}, u32[]{:S(2)}, u32[]{:S(2)}) collective-permute-start(bf16[272,256]{1,0:T(8,128)(2,1)S(1)} %pad_maximum_fusion.1), channel_id=1, source_target_pairs={{0,48},{1,17},{2,50},{3,19},{4,52},{5,21},{6,54},{7,23},{8,56},{9,... | collective-permute-start | bytes 417800 | tf_op jit(solution)/shard_map/ppermute | solution.py:328
  27.1 28.2 %collective-permute-start = (bf16[256,512]{1,0:T(8,128)(2,1)S(1)}, bf16[256,512]{1,0:T(8,128)(2,1)S(1)}, u32[]{:S(2)}, u32[]{:S(2)}) collective-permute-start(bf16[256,512]{1,0:T(8,128)(2,1)S(1)} %bitcast.16), channel_id=1, source_target_pairs={{0,1},{1,0},{2,3},{3,2},{4,5},{5,4},{6,7},{7,6},{8,9},{9,8},{10,11... | collective-permute-start | bytes 786440 | tf_op jit(solution)/shard_map/ppermute | solution.py:329
  44.4 28.0 %copy-start.4 = (s32[128]{0:T(128)S(1)}, s32[128]{0:T(128)}, u32[]{:S(2)}) copy-start(s32[128]{0:T(128)} %constant.6.clone.order) | copy-start | bytes 1540
  61.0 11.4 %collective-permute-start.3 = (bf16[136,2048]{1,0:T(8,128)(2,1)S(1)}, bf16[136,2048]{1,0:T(8,128)(2,1)S(1)}, u32[]{:S(2)}, u32[]{:S(2)}) collective-permute-start(bf16[136,2048]{1,0:T(8,128)(2,1)S(1)} %get-tuple-element.9.mine_ref), channel_id=1, source_target_pairs={{0,1},{1,0},{2,3},{3,2},{4,5},{5,4},{6,7},{7,6},{8,9},{9,8},{10,11... | collective-permute-start | bytes 1671176 | tf_op jit(solution)/shard_map/ppermute | solution.py:334
  73.9 10.2 %collective-permute-start.5 = (bf16[2,256,512]{2,1,0:T(8,128)(2,1)S(1)}, bf16[2,256,512]{2,1,0:T(8,128)(2,1)S(1)}, u32[]{:S(2)}, u32[]{:S(2)}) collective-permute-start(bf16[2,256,512]{2,1,0:T(8,128)(2,1)S(1)} %get-tuple-element.11), channel_id=1, source_target_pairs={{0,14},{1,3},{2,4},{3,1},{4,2},{5,7},{6,8},{7,5},{8,6},{9,11},{10,... | collective-permute-start | bytes 1572872 | tf_op jit(solution)/shard_map/ppermute | solution.py:338
  84.3 29.8 %copy-start.7 = (s32[1,256]{1,0:T(1,128)S(1)}, s32[1,256]{1,0:T(1,128)}, u32[]{:S(2)}) copy-start(s32[1,256]{1,0:T(1,128)} %mask_hbm.1) | copy-start | bytes 3076
  84.3 11.6 %collective-permute-start.6 = (bf16[2,256,512]{2,1,0:T(8,128)(2,1)S(1)}, bf16[2,256,512]{2,1,0:T(8,128)(2,1)S(1)}, u32[]{:S(2)}, u32[]{:S(2)}) collective-permute-start(bf16[2,256,512]{2,1,0:T(8,128)(2,1)S(1)} %add_convert_fusion.1), channel_id=1, source_target_pairs={{0,2},{1,15},{2,0},{3,5},{4,6},{5,3},{6,4},{7,9},{8,10},{9,7},{10,... | collective-permute-start | bytes 1572872 | tf_op jit(solution)/shard_map/ppermute | solution.py:343
  96.0 15.5 %collective-permute-start.7 = (bf16[2,256,512]{2,1,0:T(8,128)(2,1)S(1)}, bf16[2,256,512]{2,1,0:T(8,128)(2,1)S(1)}, u32[]{:S(2)}, u32[]{:S(2)}) collective-permute-start(bf16[2,256,512]{2,1,0:T(8,128)(2,1)S(1)} %add_convert_fusion), channel_id=1, source_target_pairs={{0,14},{1,3},{2,4},{3,1},{4,2},{5,7},{6,8},{7,5},{8,6},{9,11},{10,... | collective-permute-start | bytes 1572872 | tf_op jit(solution)/shard_map/ppermute | solution.py:344
  97.9 4.4 %collective-permute-start.9 = (f32[8,128]{1,0:T(8,128)S(1)}, f32[8,128]{1,0:T(8,128)S(1)}, u32[]{:S(2)}, u32[]{:S(2)}) collective-permute-start(f32[8,128]{1,0:T(8,128)S(1)} %get-tuple-element.12), channel_id=1, source_target_pairs={{0,256},{1,513},{2,258},{3,515},{4,260},{5,517},{6,262},{7,519},{8... | collective-permute-start | bytes 12296 | tf_op jit(solution)/shard_map/ppermute | solution.py:341
  102.3 11.3 %collective-permute-start.10 = (f32[8,128]{1,0:T(8,128)S(1)}, f32[8,128]{1,0:T(8,128)S(1)}, u32[]{:S(2)}, u32[]{:S(2)}) collective-permute-start(f32[8,128]{1,0:T(8,128)S(1)} %collective-permute-done.9), channel_id=1, source_target_pairs={{0,1},{1,0},{2,3},{3,2},{4,5},{5,4},{6,7},{7,6},{8,9},{9,8},{10,11... | collective-permute-start | bytes 12296 | tf_op jit(solution)/shard_map/ppermute | solution.py:342
  111.6 8.3 %collective-permute-start.8 = (bf16[256,512]{1,0:T(8,128)(2,1)S(1)}, bf16[256,512]{1,0:T(8,128)(2,1)S(1)}, u32[]{:S(2)}, u32[]{:S(2)}) collective-permute-start(bf16[256,512]{1,0:T(8,128)(2,1)S(1)} %fusion.2), channel_id=1, source_target_pairs={{0,2},{1,15},{2,0},{3,5},{4,6},{5,3},{6,4},{7,9},{8,10},{9,7},{10,... | collective-permute-start | bytes 786440 | tf_op jit(solution)/shard_map/ppermute | solution.py:345

commit v2 on v1

--- a/solution.py
+++ b/solution.py
@@ -1,6 +1,5 @@
 import jax
 import jax.numpy as jnp
-import numpy as np
 from jax import lax
 from jax.experimental import pallas as pl
 from jax.experimental.pallas import tpu as pltpu
@@ -20,12 +19,12 @@
 
 
 def inner(i, c, n):
-    return ((((i - c) % n) ^ 1) + c) % n
+    return ((((i - c) & (n - 1)) ^ 1) + c) & (n - 1)
 
 
 def outer(i, c, n):
-    v = (i - c) % n
-    return (v + (1 if v % 2 else -1) + c) % n
+    v = (i - c) & (n - 1)
+    return (v + 2 * (v & 1) - 1 + c) & (n - 1)
 
 
 def perm_context(axis, partner):
@@ -50,34 +49,24 @@
 SWAP = [(t, t ^ 1) for t in range(16)]
 
 
-def slot_table():
-    table = np.zeros((16, NC, 16), np.int32)
-    for x in range(NX):
-        for z in range(NZ):
-            for c in range(NC):
-                far = outer(z, c, NZ)
-                rows = []
-                for zs in ((z,), (inner(z, c, NZ), far, inner(far, c, NZ))):
-                    rows += [2 * (xx * NZ + zz) + c for xx in range(NX) for zz in zs]
-                table[x * NZ + z, c] = rows
-    return table
-
-
-def block_table():
-    table = np.zeros((16, 8), np.int32)
-    for y in range(NY):
-        for c in range(NC):
-            v = (y - c) % NY
-            k, s = v // 2, v % 2
-            far = (k + 2) % 4
-            mid = (k + 1 - 2 * s) % 4
-            near = (k - 1 + 2 * s) % 4
-            order = [2 * far + s, 2 * far + 1 - s]
-            order += [2 * mid + 1 - s, 2 * mid + s]
-            order += [2 * near + s, 2 * near + 1 - s]
-            order += [2 * k + 1 - s, 2 * k + s]
-            table[y * NC + c] = [2 * ((b + c) % NY) + c for b in order]
-    return table
+def gathered_slot(context, core, i):
+    z = context & (NZ - 1)
+    far = outer(z, core, NZ)
+    if i < NX:
+        return 2 * (i * NZ + z) + core
+    x, which = divmod(i - NX, NZ - 1)
+    zs = (inner(z, core, NZ), far, inner(far, core, NZ))
+    return 2 * (x * NZ + zs[which]) + core
+
+
+def column_blocks(tensor):
+    y, core = tensor >> 1, tensor & 1
+    v = (y - core) & (NY - 1)
+    k, s = v >> 1, v & 1
+    far, mid, near = (k + 2) & 3, (k + 1 - 2 * s) & 3, (k - 1 + 2 * s) & 3
+    order = (2 * far + s, 2 * far + 1 - s, 2 * mid + 1 - s, 2 * mid + s)
+    order += (2 * near + s, 2 * near + 1 - s, 2 * k + 1 - s, 2 * k + s)
+    return [2 * ((b + core) & (NY - 1)) + core for b in order]
 
 
 SMEM = pl.BlockSpec(memory_space=pltpu.SMEM)
@@ -119,31 +108,30 @@
     )(keys, values, loss_mask)
 
 
-def pack_kernel(order, w_ref, out_ref, sems):
-    other = (lax.axis_index("tensor") ^ 1) * 8
+def pack_kernel(w_ref, out_ref, sems):
     copies = []
-    for g in range(8):
-        at = pl.multiple_of(order[other + g] * COLS, COLS)
+    for g, block in enumerate(column_blocks(lax.axis_index("tensor") ^ 1)):
+        at = pl.multiple_of(block * COLS, COLS)
         copies.append(pltpu.make_async_copy(w_ref.at[:, pl.ds(at, COLS)], out_ref.at[g], sems.at[g]))
         copies[-1].start()
     for copy in copies:
         copy.wait()
 
 
-def pack(order, w):
+def pack(w):
     return pl.pallas_call(
         pack_kernel,
         out_shape=jax.ShapeDtypeStruct((8, w.shape[0], COLS), w.dtype),
-        in_specs=[SMEM, HBM],
+        in_specs=[HBM],
         out_specs=HBM,
         scratch_shapes=[pltpu.SemaphoreType.DMA((8,))],
         compiler_params=grant(2),
         name="pack",
-    )(order, w)
+    )(w)
 
 
 def attention_kernel(
-    slots, spans, seg_ref, q_ref, q_other_ref, a_ref, b_ref, out_ref, tally_ref, kv, q8, items, lo_ref, m_ref, l_ref, acc
+    spans, seg_ref, q_ref, q_other_ref, a_ref, b_ref, out_ref, tally_ref, kv, q8, places, items, lo_ref, m_ref, l_ref, acc
 ):
     f32 = jnp.float32
     context = lax.axis_index("context")
@@ -161,8 +149,9 @@
     tally_ref[...] = tally
     seg = seg_ref[...]
     starts = [jnp.sum((seg < d).astype(f32), keepdims=True) for d in range(1, 8)]
-    base = (context * NC + core) * 16
     count = jnp.int32(0)
+    for b in range(16):
+        places[b] = spans[gathered_slot(context, core, b)]
     for i in range(2):
         for h in range(heads):
             ref = q_ref if h < half else q_other_ref
@@ -178,7 +167,7 @@
         l_ref[i] = jnp.zeros((1, width), f32)
         acc[i] = jnp.zeros((HD, width), f32)
         for b in range(16):
-            pos = spans[slots[base + b]]
+            pos = places[b]
             items[count] = i * 16 + b
             seen = (pos <= q_pos) & ((pos + 1) * SPAN > first)
             count = count + seen.astype(jnp.int32)
@@ -186,7 +175,7 @@
     def step(j, carry):
         item = items[j]
         i, b = lax.shift_right_logical(item, 4), item & 15
-        pos = lax.broadcasted_iota(jnp.int32, (SPAN, SPAN), 0) + spans[slots[base + b]] * SPAN
+        pos = lax.broadcasted_iota(jnp.int32, (SPAN, SPAN), 0) + places[b] * SPAN
         hi = lax.broadcasted_iota(jnp.int32, (SPAN, SPAN), 1) + spans[2 * context + i] * SPAN
         bias = jnp.where((pos.astype(f32) >= lo_ref[i]) & (pos <= hi), 0.0, LOW)
         s = lax.dot_general(kv[b, :, :HD], q8[i], (((1,), (1,)), ((), ())), preferred_element_type=f32)
@@ -218,7 +207,7 @@
         out_ref[SPAN:, cols] = parts.astype(jnp.bfloat16)
 
 
-def attention(slots, spans, seg, q, q_other, a, b):
+def attention(spans, seg, q, q_other, a, b):
     heads = 2 * q.shape[1] // HD
     width = heads * SPAN
     return pl.pallas_call(
@@ -227,11 +216,12 @@
             jax.ShapeDtypeStruct((BLOCK, 2 * width), jnp.bfloat16),
             jax.ShapeDtypeStruct((TALLY, HD), jnp.float32),
         ),
-        in_specs=[SMEM, SMEM] + [VMEM] * 5,
+        in_specs=[SMEM] + [VMEM] * 5,
         out_specs=(VMEM, VMEM),
         scratch_shapes=[
             pltpu.VMEM((16, SPAN, 2 * HD), jnp.bfloat16),
             pltpu.VMEM((2, width, HD), jnp.bfloat16),
+            pltpu.SMEM((16,), jnp.int32),
             pltpu.SMEM((33,), jnp.int32),
             pltpu.VMEM((2, 1, SPAN), jnp.float32),
             pltpu.VMEM((2, 1, width), jnp.float32),
@@ -240,20 +230,20 @@
         ],
         compiler_params=grant(12),
         name="attend",
-    )(slots, spans, seg, q, q_other, a, b)
-
-
-def multiply(order, first, heads_ref, w_ref, other_ref, out_ref):
+    )(spans, seg, q, q_other, a, b)
+
+
+def multiply(first, heads_ref, w_ref, other_ref, out_ref):
     depth = w_ref.shape[0]
-    mine = lax.axis_index("tensor") * 8
+    blocks = column_blocks(lax.axis_index("tensor"))
     for g in range(out_ref.shape[0]):
-        at = pl.multiple_of(order[mine + first + g] * COLS, COLS)
+        at = pl.multiple_of(blocks[first + g] * COLS, COLS)
         total = jnp.dot(heads_ref[:, :depth], w_ref[:, pl.ds(at, COLS)], preferred_element_type=jnp.float32)
         total += jnp.dot(heads_ref[:, depth:], other_ref[first + g], preferred_element_type=jnp.float32)
         out_ref[g] = total.astype(jnp.bfloat16)
 
 
-def join_kernel(order, mine_ref, theirs_ref, w_ref, other_ref, heads_ref, out_ref):
+def join_kernel(mine_ref, theirs_ref, w_ref, other_ref, heads_ref, out_ref):
     f32 = jnp.float32
     width = mine_ref.shape[1] // 2
     heads = width // SPAN
@@ -273,10 +263,10 @@
             joined = mine_ref[:SPAN, a : a + SPAN].astype(f32) * (part_a / total)
             joined += theirs_ref[:SPAN, b : b + SPAN].astype(f32) * (part_b / total)
             heads_ref[i * SPAN : (i + 1) * SPAN, h * HD : (h + 1) * HD] = joined.T.astype(jnp.bfloat16)
-    multiply(order, 0, heads_ref, w_ref, other_ref, out_ref)
-
-
-def join(order, mine, theirs, w, other):
+    multiply(0, heads_ref, w_ref, other_ref, out_ref)
+
+
+def join(mine, theirs, w, other):
     rows, depth = 2 * SPAN, 2 * w.shape[0]
     return pl.pallas_call(
         join_kernel,
@@ -284,27 +274,27 @@
             jax.ShapeDtypeStruct((rows, depth), jnp.bfloat16),
             jax.ShapeDtypeStruct((2, rows, COLS), jnp.bfloat16),
         ),
-        in_specs=[SMEM] + [VMEM] * 4,
+        in_specs=[VMEM] * 4,
         out_specs=(VMEM, VMEM),
         compiler_params=grant(20),
         name="join",
-    )(order, mine, theirs, w, other)
-
-
-def project_kernel(order, heads_ref, w_ref, other_ref, out_ref):
-    multiply(order, 2, heads_ref, w_ref, other_ref, out_ref)
-
-
-def project(order, heads, w, other):
+    )(mine, theirs, w, other)
+
+
+def project_kernel(heads_ref, w_ref, other_ref, out_ref):
+    multiply(2, heads_ref, w_ref, other_ref, out_ref)
+
+
+def project(heads, w, other):
     rows = heads.shape[0]
     return pl.pallas_call(
         project_kernel,
         out_shape=jax.ShapeDtypeStruct((6, rows, COLS), jnp.bfloat16),
-        in_specs=[SMEM] + [VMEM] * 3,
+        in_specs=[VMEM] * 3,
         out_specs=VMEM,
         compiler_params=grant(20),
         name="project",
-    )(order, heads, w, other)
+    )(heads, w, other)
 
 
 def add(a, b):
@@ -315,8 +305,6 @@
     both = ("context", "tensor")
     f32 = jnp.float32
     cat = lambda *a: jnp.concatenate(a, axis=0)
-    order = jnp.asarray(block_table().reshape(-1))
-    slots = jnp.asarray(slot_table().reshape(-1))
     along_x = [[x * NZ + z for x in range(NX)] for z in range(NZ)]
     gather = lambda a: lax.all_gather(a, "context", axis=0, tiled=True, axis_index_groups=along_x)
 
@@ -327,16 +315,16 @@
     near = gather(kv1)
     r2 = lax.ppermute(cat(kv1, r1), both, perm_context("z", outer))
     q_other = lax.ppermute(queries[0], "tensor", SWAP)
-    packed = pack(order, in_hbm(out_weight))
+    packed = pack(in_hbm(out_weight))
     weight_other = lax.ppermute(packed, "tensor", SWAP)
     far = gather(cat(r1, r2))
-    mine, tally = attention(slots, span_order, segment_ids.reshape(32, SPAN), queries[0], q_other, near, far)
+    mine, tally = attention(span_order, segment_ids.reshape(32, SPAN), queries[0], q_other, near, far)
     theirs = lax.ppermute(mine, "tensor", SWAP)
 
     inward, outward = perm_tensor(inner), perm_tensor(outer)
-    heads, far = join(order, mine, theirs, out_weight, weight_other)
+    heads, far = join(mine, theirs, out_weight, weight_other)
     far = lax.ppermute(far, "tensor", outward)
-    rest = project(order, heads, out_weight, weight_other)
+    rest = project(heads, out_weight, weight_other)
     around = [(d * 16 + t, (d + 1 + t % 2) % 3 * 16 + t) for d in range(3) for t in range(16)]
     one = lax.ppermute(tally, ("dp", "tensor"), around)
     two = lax.ppermute(one, "tensor", SWAP)

time: 121 us -> 119 us (0.983)
  Pallas kernels: 13.3 us -> 11.5 us
where the time goes in v2:
time: 119 us
  starting transfers between devices  60.7 us (51%)
  waiting for transfers between devices  23.8 us (20%)
  blocking collectives  20.4 us (17%)
  Pallas kernels  11.5 us (10%)
  other arithmetic  1.84 us (2%)
    all_gather x2, blocking collectives, per_device(): lax.all_gather(a, 'context', axis=0, tiled=True, axis_index_groups=along_x)  20.4 us
    ppermute x1, starting transfers between devices, per_device(): weight_other = lax.ppermute(packed, 'tensor', SWAP)  12.6 us
    ppermute x1, starting transfers between devices, per_device(): theirs = lax.ppermute(mine, 'tensor', SWAP)  9.86 us
    ppermute x1, starting transfers between devices, per_device(): two = lax.ppermute(one, 'tensor', SWAP)  9.25 us
    ppermute x1, starting transfers between devices, per_device(): q_other = lax.ppermute(queries[0], 'tensor', SWAP)  7.75 us
    ppermute x1, waiting for transfers between devices, per_device(): mid = lax.ppermute(add(rest[0:2], far), 'tensor', inward)  6.56 us
    pallas_call x1, Pallas kernels, attention(): pl.pallas_call(attention_kernel, out_shape=(jax.ShapeDtypeStruct((BLOCK,...  5.57 us
    ppermute x1, starting transfers between devices, per_device(): r1 = lax.ppermute(kv1, both, perm_context('z', inner))  5.3 us
  transfers between devices with their start and end apart: 11, of which 6 were waited for; matrix products, arithmetic and copies ran while one was open for 1% of the time, Pallas kernels for 7%

profile of v2, /device:TPU:1, one launch (start us, length us, event | category | flops | bytes accessed | tf_op | source)
XLA Modules:
  0.0 119.0 jit_solution(14980296999796559600)
XLA Ops:
  0.0 2.4 %pack.1 = bf16[8,512,512]{2,1,0:T(8,128)(2,1)S(1)} custom-call(bf16[512,8192]{1,0:T(8,128)(2,1)} %w_ref.5), custom_call_target="tpu_custom_call" | custom-call | tf_op jit(solution)/shard_map/pack/pallas_call | solution.py:122
  2.4 12.6 %collective-permute-start.4 = (bf16[8,512,512]{2,1,0:T(8,128)(2,1)S(1)}, bf16[8,512,512]{2,1,0:T(8,128)(2,1)S(1)}, u32[]{:S(2)}, u32[]{:S(2)}) collective-permute-start(bf16[8,512,512]{2,1,0:T(8,128)(2,1)S(1)} %pack.1), channel_id=1, source_target_pairs={{0,1},{1,0},{2,3},{3,2},{4,5},{5,4},{6,7},{7,6},{8,9},{9,8},{10,11... | collective-permute-start | bytes 12582920 | tf_op jit(solution)/shard_map/ppermute | solution.py:319
  15.9 5.3 %collective-permute-start.1 = (bf16[136,256]{1,0:T(8,128)(2,1)S(1)}, bf16[136,256]{1,0:T(8,128)(2,1)S(1)}, u32[]{:S(2)}, u32[]{:S(2)}) collective-permute-start(bf16[136,256]{1,0:T(8,128)(2,1)S(1)} %prepare.1), channel_id=1, source_target_pairs={{0,16},{1,49},{2,18},{3,51},{4,20},{5,53},{6,22},{7,55},{8,24},{9,... | collective-permute-start | bytes 208904 | tf_op jit(solution)/shard_map/ppermute | solution.py:314
  21.2 2.8 %collective-permute-done.1 = bf16[136,256]{1,0:T(8,128)(2,1)S(1)} collective-permute-done((bf16[136,256]{1,0:T(8,128)(2,1)S(1)}, bf16[136,256]{1,0:T(8,128)(2,1)S(1)}, u32[]{:S(2)}, u32[]{:S(2)}) %collective-permute-start.1) | collective-permute-done | bytes 69664 | tf_op jit(solution)/shard_map/ppermute | solution.py:314
  24.0 1.9 %collective-permute-start.2 = (bf16[272,256]{1,0:T(8,128)(2,1)S(1)}, bf16[272,256]{1,0:T(8,128)(2,1)S(1)}, u32[]{:S(2)}, u32[]{:S(2)}) collective-permute-start(bf16[272,256]{1,0:T(8,128)(2,1)S(1)} %pad_maximum_fusion.1), channel_id=1, source_target_pairs={{0,48},{1,17},{2,50},{3,19},{4,52},{5,21},{6,54},{7,23},{8,56},{9,... | collective-permute-start | bytes 417800 | tf_op jit(solution)/shard_map/ppermute | solution.py:316
  25.9 7.7 %collective-permute-start = (bf16[256,512]{1,0:T(8,128)(2,1)S(1)}, bf16[256,512]{1,0:T(8,128)(2,1)S(1)}, u32[]{:S(2)}, u32[]{:S(2)}) collective-permute-start(bf16[256,512]{1,0:T(8,128)(2,1)S(1)} %bitcast.16), channel_id=1, source_target_pairs={{0,1},{1,0},{2,3},{3,2},{4,5},{5,4},{6,7},{7,6},{8,9},{9,8},{10,11... | collective-permute-start | bytes 786440 | tf_op jit(solution)/shard_map/ppermute | solution.py:317
  33.7 9.5 %all_gather.6.a_ref = bf16[544,256]{1,0:T(8,128)(2,1)S(1)} all-gather(bf16[136,256]{1,0:T(8,128)(2,1)S(1)} %prepare.1), channel_id=1, replica_groups={{0,64,128,192},{16,80,144,208},{32,96,160,224},{48,112,176,240},{1,65,1..., dimensions={0}, use_global_device_ids=true | all-gather | bytes 348160 | tf_op jit(solution)/shard_map/all_gather | solution.py:309
  43.2 10.9 %all_gather.7.b_ref = bf16[1632,256]{1,0:T(8,128)(2,1)S(1)} all-gather(bf16[408,256]{1,0:T(8,128)(2,1)S(1)} %pad_maximum_fusion), channel_id=1, replica_groups={{0,64,128,192},{16,80,144,208},{32,96,160,224},{48,112,176,240},{1,65,1..., dimensions={0}, use_global_device_ids=true | all-gather | bytes 1044480 | tf_op jit(solution)/shard_map/all_gather | solution.py:309
  54.1 5.6 %attend.1 = (bf16[136,2048]{1,0:T(8,128)(2,1)S(1)}, f32[8,128]{1,0:T(8,128)S(1)}) custom-call(s32[32]{0:T(128)S(1)} %copy-done.3, s32[32,128]{1,0:T(8,128)S(1)} %bitcast.18, bf16[256,512]{1,0:T(8,128)(2,1)S(1)} %bitcast.17, bf16[256,512]{1,0:T(8,128)(2,1)S(1)} %collective-permute-done.q_other_ref, bf16[544,256]{1,0:T(8,128)(2,1)S(1)} %all_gather.6.a_ref, ...), custom_call_target="tpu_custom_call" | custom-call | tf_op jit(solution)/shard_map/attend/pallas_call | solution.py:213
  59.7 9.9 %collective-permute-start.3 = (bf16[136,2048]{1,0:T(8,128)(2,1)S(1)}, bf16[136,2048]{1,0:T(8,128)(2,1)S(1)}, u32[]{:S(2)}, u32[]{:S(2)}) collective-permute-start(bf16[136,2048]{1,0:T(8,128)(2,1)S(1)} %get-tuple-element.9.mine_ref), channel_id=1, source_target_pairs={{0,1},{1,0},{2,3},{3,2},{4,5},{5,4},{6,7},{7,6},{8,9},{9,8},{10,11... | collective-permute-start | bytes 1671176 | tf_op jit(solution)/shard_map/ppermute | solution.py:322
  69.6 1.6 %collective-permute-done.3.theirs_ref = bf16[136,2048]{1,0:T(8,128)(2,1)S(1)} collective-permute-done((bf16[136,2048]{1,0:T(8,128)(2,1)S(1)}, bf16[136,2048]{1,0:T(8,128)(2,1)S(1)}, u32[]{:S(2)}, u32[]{:S(2)}) %collective-permute-start.3) | collective-permute-done | bytes 557088 | tf_op jit(solution)/shard_map/ppermute | solution.py:322
  71.1 1.0 join.1
  72.1 3.2 %collective-permute-start.5 = (bf16[2,256,512]{2,1,0:T(8,128)(2,1)S(1)}, bf16[2,256,512]{2,1,0:T(8,128)(2,1)S(1)}, u32[]{:S(2)}, u32[]{:S(2)}) collective-permute-start(bf16[2,256,512]{2,1,0:T(8,128)(2,1)S(1)} %get-tuple-element.11), channel_id=1, source_target_pairs={{0,14},{1,3},{2,4},{3,1},{4,2},{5,7},{6,8},{7,5},{8,6},{9,11},{10,... | collective-permute-start | bytes 1572872 | tf_op jit(solution)/shard_map/ppermute | solution.py:326
  75.3 1.8 %project.1 = bf16[6,256,512]{2,1,0:T(8,128)(2,1)S(1)} custom-call(bf16[256,1024]{1,0:T(8,128)(2,1)S(1)} %get-tuple-element.10.heads_ref, bf16[512,8192]{1,0:T(8,128)(2,1)S(1)} %copy-done, bf16[8,512,512]{2,1,0:T(8,128)(2,1)S(1)} %collective-permute-done.4.other_ref), custom_call_target="tpu_custom_call" | custom-call | tf_op jit(solution)/shard_map/project/pallas_call | solution.py:290
  77.1 5.2 %collective-permute-done.5 = bf16[2,256,512]{2,1,0:T(8,128)(2,1)S(1)} collective-permute-done((bf16[2,256,512]{2,1,0:T(8,128)(2,1)S(1)}, bf16[2,256,512]{2,1,0:T(8,128)(2,1)S(1)}, u32[]{:S(2)}, u32[]{:S(2)}) %collective-permute-start.5) | collective-permute-done | bytes 524320 | tf_op jit(solution)/shard_map/ppermute | solution.py:326
  82.5 5.0 %collective-permute-start.6 = (bf16[2,256,512]{2,1,0:T(8,128)(2,1)S(1)}, bf16[2,256,512]{2,1,0:T(8,128)(2,1)S(1)}, u32[]{:S(2)}, u32[]{:S(2)}) collective-permute-start(bf16[2,256,512]{2,1,0:T(8,128)(2,1)S(1)} %add_convert_fusion.1), channel_id=1, source_target_pairs={{0,2},{1,15},{2,0},{3,5},{4,6},{5,3},{6,4},{7,9},{8,10},{9,7},{10,... | collective-permute-start | bytes 1572872 | tf_op jit(solution)/shard_map/ppermute | solution.py:331
  87.5 6.6 %collective-permute-done.6 = bf16[2,256,512]{2,1,0:T(8,128)(2,1)S(1)} collective-permute-done((bf16[2,256,512]{2,1,0:T(8,128)(2,1)S(1)}, bf16[2,256,512]{2,1,0:T(8,128)(2,1)S(1)}, u32[]{:S(2)}, u32[]{:S(2)}) %collective-permute-start.6) | collective-permute-done | bytes 524320 | tf_op jit(solution)/shard_map/ppermute | solution.py:331
  94.2 1.9 %collective-permute-start.7 = (bf16[2,256,512]{2,1,0:T(8,128)(2,1)S(1)}, bf16[2,256,512]{2,1,0:T(8,128)(2,1)S(1)}, u32[]{:S(2)}, u32[]{:S(2)}) collective-permute-start(bf16[2,256,512]{2,1,0:T(8,128)(2,1)S(1)} %add_convert_fusion), channel_id=1, source_target_pairs={{0,14},{1,3},{2,4},{3,1},{4,2},{5,7},{6,8},{7,5},{8,6},{9,11},{10,... | collective-permute-start | bytes 1572872 | tf_op jit(solution)/shard_map/ppermute | solution.py:332
  96.1 1.9 %collective-permute-start.9 = (f32[8,128]{1,0:T(8,128)S(1)}, f32[8,128]{1,0:T(8,128)S(1)}, u32[]{:S(2)}, u32[]{:S(2)}) collective-permute-start(f32[8,128]{1,0:T(8,128)S(1)} %get-tuple-element.12), channel_id=1, source_target_pairs={{0,256},{1,513},{2,258},{3,515},{4,260},{5,517},{6,262},{7,519},{8... | collective-permute-start | bytes 12296 | tf_op jit(solution)/shard_map/ppermute | solution.py:329
  98.1 2.4 %collective-permute-done.9 = f32[8,128]{1,0:T(8,128)S(1)} collective-permute-done((f32[8,128]{1,0:T(8,128)S(1)}, f32[8,128]{1,0:T(8,128)S(1)}, u32[]{:S(2)}, u32[]{:S(2)}) %collective-permute-start.9) | collective-permute-done | bytes 4128 | tf_op jit(solution)/shard_map/ppermute | solution.py:329
  100.5 9.3 %collective-permute-start.10 = (f32[8,128]{1,0:T(8,128)S(1)}, f32[8,128]{1,0:T(8,128)S(1)}, u32[]{:S(2)}, u32[]{:S(2)}) collective-permute-start(f32[8,128]{1,0:T(8,128)S(1)} %collective-permute-done.9), channel_id=1, source_target_pairs={{0,1},{1,0},{2,3},{3,2},{4,5},{5,4},{6,7},{7,6},{8,9},{9,8},{10,11... | collective-permute-start | bytes 12296 | tf_op jit(solution)/shard_map/ppermute | solution.py:330
  109.8 1.9 %collective-permute-start.8 = (bf16[256,512]{1,0:T(8,128)(2,1)S(1)}, bf16[256,512]{1,0:T(8,128)(2,1)S(1)}, u32[]{:S(2)}, u32[]{:S(2)}) collective-permute-start(bf16[256,512]{1,0:T(8,128)(2,1)S(1)} %fusion.2), channel_id=1, source_target_pairs={{0,2},{1,15},{2,0},{3,5},{4,6},{5,3},{6,4},{7,9},{8,10},{9,7},{10,... | collective-permute-start | bytes 786440 | tf_op jit(solution)/shard_map/ppermute | solution.py:333
  113.0 5.2 %collective-permute-done.8 = bf16[256,512]{1,0:T(8,128)(2,1)S(1)} collective-permute-done((bf16[256,512]{1,0:T(8,128)(2,1)S(1)}, bf16[256,512]{1,0:T(8,128)(2,1)S(1)}, u32[]{:S(2)}, u32[]{:S(2)}) %collective-permute-start.8) | collective-permute-done | bytes 262176 | tf_op jit(solution)/shard_map/ppermute | solution.py:333
  118.2 0.8 fusion.3
  (24 shorter events, 2.4 us)
Async XLA Ops:
  0.0 25.9 %copy-start.1 = (bf16[1,256,512]{2,1,0:T(8,128)(2,1)S(1)}, bf16[1,256,512]{2,1,0:T(8,128)(2,1)}, u32[]{:S(2)}) copy-start(bf16[1,256,512]{2,1,0:T(8,128)(2,1)} %param.7) | copy-start | bytes 786436
  0.0 71.1 %copy-start = (bf16[512,8192]{1,0:T(8,128)(2,1)S(1)}, bf16[512,8192]{1,0:T(8,128)(2,1)}, u32[]{:S(2)}) copy-start(bf16[512,8192]{1,0:T(8,128)(2,1)} %w_ref.5) | copy-start | bytes 25165828
  2.4 51.7 %copy-start.2 = (s32[1,4096]{1,0:T(1,128)S(1)}, s32[1,4096]{1,0:T(1,128)}, u32[]{:S(2)}) copy-start(s32[1,4096]{1,0:T(1,128)} %param.11) | copy-start | bytes 49156
  2.4 51.7 %copy-start.3 = (s32[32]{0:T(128)S(1)}, s32[32]{0:T(128)}, u32[]{:S(2)}) copy-start(s32[32]{0:T(128)} %spans.1) | copy-start | bytes 388
  2.4 68.7 %collective-permute-start.4 = (bf16[8,512,512]{2,1,0:T(8,128)(2,1)S(1)}, bf16[8,512,512]{2,1,0:T(8,128)(2,1)S(1)}, u32[]{:S(2)}, u32[]{:S(2)}) collective-permute-start(bf16[8,512,512]{2,1,0:T(8,128)(2,1)S(1)} %pack.1), channel_id=1, source_target_pairs={{0,1},{1,0},{2,3},{3,2},{4,5},{5,4},{6,7},{7,6},{8,9},{9,8},{10,11... | collective-permute-start | bytes 12582920 | tf_op jit(solution)/shard_map/ppermute | solution.py:319
  15.9 8.1 %collective-permute-start.1 = (bf16[136,256]{1,0:T(8,128)(2,1)S(1)}, bf16[136,256]{1,0:T(8,128)(2,1)S(1)}, u32[]{:S(2)}, u32[]{:S(2)}) collective-permute-start(bf16[136,256]{1,0:T(8,128)(2,1)S(1)} %prepare.1), channel_id=1, source_target_pairs={{0,16},{1,49},{2,18},{3,51},{4,20},{5,53},{6,22},{7,55},{8,24},{9,... | collective-permute-start | bytes 208904 | tf_op jit(solution)/shard_map/ppermute | solution.py:314
  24.0 19.2 %collective-permute-start.2 = (bf16[272,256]{1,0:T(8,128)(2,1)S(1)}, bf16[272,256]{1,0:T(8,128)(2,1)S(1)}, u32[]{:S(2)}, u32[]{:S(2)}) collective-permute-start(bf16[272,256]{1,0:T(8,128)(2,1)S(1)} %pad_maximum_fusion.1), channel_id=1, source_target_pairs={{0,48},{1,17},{2,50},{3,19},{4,52},{5,21},{6,54},{7,23},{8,56},{9,... | collective-permute-start | bytes 417800 | tf_op jit(solution)/shard_map/ppermute | solution.py:316
  25.9 28.2 %collective-permute-start = (bf16[256,512]{1,0:T(8,128)(2,1)S(1)}, bf16[256,512]{1,0:T(8,128)(2,1)S(1)}, u32[]{:S(2)}, u32[]{:S(2)}) collective-permute-start(bf16[256,512]{1,0:T(8,128)(2,1)S(1)} %bitcast.16), channel_id=1, source_target_pairs={{0,1},{1,0},{2,3},{3,2},{4,5},{5,4},{6,7},{7,6},{8,9},{9,8},{10,11... | collective-permute-start | bytes 786440 | tf_op jit(solution)/shard_map/ppermute | solution.py:317
  59.7 11.4 %collective-permute-start.3 = (bf16[136,2048]{1,0:T(8,128)(2,1)S(1)}, bf16[136,2048]{1,0:T(8,128)(2,1)S(1)}, u32[]{:S(2)}, u32[]{:S(2)}) collective-permute-start(bf16[136,2048]{1,0:T(8,128)(2,1)S(1)} %get-tuple-element.9.mine_ref), channel_id=1, source_target_pairs={{0,1},{1,0},{2,3},{3,2},{4,5},{5,4},{6,7},{7,6},{8,9},{9,8},{10,11... | collective-permute-start | bytes 1671176 | tf_op jit(solution)/shard_map/ppermute | solution.py:322
  72.1 10.2 %collective-permute-start.5 = (bf16[2,256,512]{2,1,0:T(8,128)(2,1)S(1)}, bf16[2,256,512]{2,1,0:T(8,128)(2,1)S(1)}, u32[]{:S(2)}, u32[]{:S(2)}) collective-permute-start(bf16[2,256,512]{2,1,0:T(8,128)(2,1)S(1)} %get-tuple-element.11), channel_id=1, source_target_pairs={{0,14},{1,3},{2,4},{3,1},{4,2},{5,7},{6,8},{7,5},{8,6},{9,11},{10,... | collective-permute-start | bytes 1572872 | tf_op jit(solution)/shard_map/ppermute | solution.py:326
  82.4 29.9 %copy-start.4 = (s32[1,256]{1,0:T(1,128)S(1)}, s32[1,256]{1,0:T(1,128)}, u32[]{:S(2)}) copy-start(s32[1,256]{1,0:T(1,128)} %mask_hbm.1) | copy-start | bytes 3076
  82.5 11.6 %collective-permute-start.6 = (bf16[2,256,512]{2,1,0:T(8,128)(2,1)S(1)}, bf16[2,256,512]{2,1,0:T(8,128)(2,1)S(1)}, u32[]{:S(2)}, u32[]{:S(2)}) collective-permute-start(bf16[2,256,512]{2,1,0:T(8,128)(2,1)S(1)} %add_convert_fusion.1), channel_id=1, source_target_pairs={{0,2},{1,15},{2,0},{3,5},{4,6},{5,3},{6,4},{7,9},{8,10},{9,7},{10,... | collective-permute-start | bytes 1572872 | tf_op jit(solution)/shard_map/ppermute | solution.py:331
  94.2 15.5 %collective-permute-start.7 = (bf16[2,256,512]{2,1,0:T(8,128)(2,1)S(1)}, bf16[2,256,512]{2,1,0:T(8,128)(2,1)S(1)}, u32[]{:S(2)}, u32[]{:S(2)}) collective-permute-start(bf16[2,256,512]{2,1,0:T(8,128)(2,1)S(1)} %add_convert_fusion), channel_id=1, source_target_pairs={{0,14},{1,3},{2,4},{3,1},{4,2},{5,7},{6,8},{7,5},{8,6},{9,11},{10,... | collective-permute-start | bytes 1572872 | tf_op jit(solution)/shard_map/ppermute | solution.py:332
  96.1 4.4 %collective-permute-start.9 = (f32[8,128]{1,0:T(8,128)S(1)}, f32[8,128]{1,0:T(8,128)S(1)}, u32[]{:S(2)}, u32[]{:S(2)}) collective-permute-start(f32[8,128]{1,0:T(8,128)S(1)} %get-tuple-element.12), channel_id=1, source_target_pairs={{0,256},{1,513},{2,258},{3,515},{4,260},{5,517},{6,262},{7,519},{8... | collective-permute-start | bytes 12296 | tf_op jit(solution)/shard_map/ppermute | solution.py:329
  100.5 11.3 %collective-permute-start.10 = (f32[8,128]{1,0:T(8,128)S(1)}, f32[8,128]{1,0:T(8,128)S(1)}, u32[]{:S(2)}, u32[]{:S(2)}) collective-permute-start(f32[8,128]{1,0:T(8,128)S(1)} %collective-permute-done.9), channel_id=1, source_target_pairs={{0,1},{1,0},{2,3},{3,2},{4,5},{5,4},{6,7},{7,6},{8,9},{9,8},{10,11... | collective-permute-start | bytes 12296 | tf_op jit(solution)/shard_map/ppermute | solution.py:330
  109.8 8.3 %collective-permute-start.8 = (bf16[256,512]{1,0:T(8,128)(2,1)S(1)}, bf16[256,512]{1,0:T(8,128)(2,1)S(1)}, u32[]{:S(2)}, u32[]{:S(2)}) collective-permute-start(bf16[256,512]{1,0:T(8,128)(2,1)S(1)} %fusion.2), channel_id=1, source_target_pairs={{0,2},{1,15},{2,0},{3,5},{4,6},{5,3},{6,4},{7,9},{8,10},{9,7},{10,... | collective-permute-start | bytes 786440 | tf_op jit(solution)/shard_map/ppermute | solution.py:333

commit v3 on v2

--- a/solution.py
+++ b/solution.py
@@ -50,13 +50,13 @@
 
 
 def gathered_slot(context, core, i):
-    z = context & (NZ - 1)
-    far = outer(z, core, NZ)
-    if i < NX:
-        return 2 * (i * NZ + z) + core
-    x, which = divmod(i - NX, NZ - 1)
-    zs = (inner(z, core, NZ), far, inner(far, core, NZ))
-    return 2 * (x * NZ + zs[which]) + core
+    def known(at, n):
+        far = outer(at, core, n)
+        return (at, inner(at, core, n), far, inner(far, core, n))
+
+    x = known(context >> 2, NX)[i // NZ]
+    z = known(context & (NZ - 1), NZ)[i % NZ]
+    return 2 * (x * NZ + z) + core
 
 
 def column_blocks(tensor):
@@ -130,56 +130,31 @@
     )(w)
 
 
-def attention_kernel(
-    spans, seg_ref, q_ref, q_other_ref, a_ref, b_ref, out_ref, tally_ref, kv, q8, places, items, lo_ref, m_ref, l_ref, acc
-):
+def attend(first_block, spans, blocks_ref, q8, lo_ref, m_ref, l_ref, acc, kv, places, items):
     f32 = jnp.float32
     context = lax.axis_index("context")
     core = lax.rem(lax.axis_index("tensor"), NC)
-    heads = 2 * q_ref.shape[1] // HD
-    half = heads // 2
-    width = heads * SPAN
-    tally = jnp.zeros((TALLY, HD), f32)
-    at = 0
-    for ref in (a_ref, b_ref):
-        for i in range(ref.shape[0] // BLOCK):
-            kv[at] = ref[i * BLOCK : i * BLOCK + SPAN, :]
-            tally += ref[i * BLOCK + SPAN : (i + 1) * BLOCK, :HD].astype(f32)
-            at += 1
-    tally_ref[...] = tally
-    seg = seg_ref[...]
-    starts = [jnp.sum((seg < d).astype(f32), keepdims=True) for d in range(1, 8)]
+    width = q8.shape[1]
     count = jnp.int32(0)
-    for b in range(16):
-        places[b] = spans[gathered_slot(context, core, b)]
+    for b in range(8):
+        kv[b] = blocks_ref[b * BLOCK : b * BLOCK + SPAN, :]
+        places[b] = spans[gathered_slot(context, core, first_block + b)]
     for i in range(2):
-        for h in range(heads):
-            ref = q_ref if h < half else q_other_ref
-            q8[i, h * SPAN : (h + 1) * SPAN, :] = ref[i * SPAN : (i + 1) * SPAN, h % half * HD : (h % half + 1) * HD]
-        q_seg = seg_ref[pl.ds(2 * context + i, 1), :]
-        lo = jnp.zeros((1, SPAN), f32)
-        for d in range(1, 8):
-            lo = jnp.where(q_seg == d, starts[d - 1], lo)
-        lo_ref[i] = lo
-        first = jnp.min(lo).astype(jnp.int32)
+        first = jnp.min(lo_ref[i]).astype(jnp.int32)
         q_pos = spans[2 * context + i]
-        m_ref[i] = jnp.full((1, width), LOW, f32)
-        l_ref[i] = jnp.zeros((1, width), f32)
-        acc[i] = jnp.zeros((HD, width), f32)
-        for b in range(16):
-            pos = places[b]
-            items[count] = i * 16 + b
-            seen = (pos <= q_pos) & ((pos + 1) * SPAN > first)
+        for b in range(8):
+            items[count] = i * 8 + b
+            seen = (places[b] <= q_pos) & ((places[b] + 1) * SPAN > first)
             count = count + seen.astype(jnp.int32)
 
     def step(j, carry):
         item = items[j]
-        i, b = lax.shift_right_logical(item, 4), item & 15
+        i, b = lax.shift_right_logical(item, 3), item & 7
         pos = lax.broadcasted_iota(jnp.int32, (SPAN, SPAN), 0) + places[b] * SPAN
         hi = lax.broadcasted_iota(jnp.int32, (SPAN, SPAN), 1) + spans[2 * context + i] * SPAN
         bias = jnp.where((pos.astype(f32) >= lo_ref[i]) & (pos <= hi), 0.0, LOW)
         s = lax.dot_general(kv[b, :, :HD], q8[i], (((1,), (1,)), ((), ())), preferred_element_type=f32)
-        s = s * (HD ** (-0.5) * LOG2E) + jnp.concatenate([bias] * heads, axis=1)
+        s = s * (HD ** (-0.5) * LOG2E) + jnp.concatenate([bias] * (width // SPAN), axis=1)
         old = m_ref[i]
         new = jnp.maximum(old, jnp.max(s, axis=0, keepdims=True))
         alpha = jnp.exp2(old - new)
@@ -193,6 +168,46 @@
         return carry
 
     lax.fori_loop(0, count, step, 0)
+    tally = jnp.zeros((TALLY, HD), f32)
+    for b in range(8):
+        tally += blocks_ref[b * BLOCK + SPAN : (b + 1) * BLOCK, :HD].astype(f32)
+    return tally
+
+
+def first_kernel(
+    spans, seg_ref, q_ref, q_other_ref, blocks_ref, q8, lo_ref, m_ref, l_ref, acc, tally_ref, kv, places, items
+):
+    f32 = jnp.float32
+    context = lax.axis_index("context")
+    heads = q8.shape[1] // SPAN
+    half = heads // 2
+    seg = seg_ref[...]
+    starts = [jnp.sum((seg < d).astype(f32), keepdims=True) for d in range(1, 8)]
+    for i in range(2):
+        for h in range(heads):
+            ref = q_ref if h < half else q_other_ref
+            q8[i, h * SPAN : (h + 1) * SPAN, :] = ref[i * SPAN : (i + 1) * SPAN, h % half * HD : (h % half + 1) * HD]
+        q_seg = seg_ref[pl.ds(2 * context + i, 1), :]
+        lo = jnp.zeros((1, SPAN), f32)
+        for d in range(1, 8):
+            lo = jnp.where(q_seg == d, starts[d - 1], lo)
+        lo_ref[i] = lo
+    m_ref[...] = jnp.full(m_ref.shape, LOW, f32)
+    l_ref[...] = jnp.zeros(l_ref.shape, f32)
+    acc[...] = jnp.zeros(acc.shape, f32)
+    tally_ref[...] = attend(0, spans, blocks_ref, q8, lo_ref, m_ref, l_ref, acc, kv, places, items)
+
+
+def second_kernel(
+    spans, blocks_ref, q8, lo_ref, m_in, l_in, acc_in, tally_in, out_ref, tally_ref, m_ref, l_ref, acc, kv, places, items
+):
+    f32 = jnp.float32
+    width = q8.shape[1]
+    m_ref[...] = m_in[...]
+    l_ref[...] = l_in[...]
+    acc[...] = acc_in[...]
+    tally = attend(8, spans, blocks_ref, q8, lo_ref, m_ref, l_ref, acc, kv, places, items)
+    tally_ref[...] = tally_in[...] + tally
     row = lax.broadcasted_iota(jnp.int32, (TALLY, width), 0)
     for i in range(2):
         cols = slice(i * width, (i + 1) * width)
@@ -207,30 +222,38 @@
         out_ref[SPAN:, cols] = parts.astype(jnp.bfloat16)
 
 
-def attention(spans, seg, q, q_other, a, b):
+def attention(spans, seg, q, q_other, blocks, more_blocks):
     heads = 2 * q.shape[1] // HD
     width = heads * SPAN
-    return pl.pallas_call(
-        attention_kernel,
+    f32 = jnp.float32
+    state = [((2, 1, width), f32), ((2, 1, width), f32), ((2, HD, width), f32)]
+    made = [((2, width, HD), jnp.bfloat16), ((2, 1, SPAN), f32), *state, ((TALLY, HD), f32)]
+    scratch = [
+        pltpu.VMEM((8, SPAN, 2 * HD), jnp.bfloat16),
+        pltpu.SMEM((8,), jnp.int32),
+        pltpu.SMEM((17,), jnp.int32),
+    ]
+    made = pl.pallas_call(
+        first_kernel,
+        out_shape=tuple(jax.ShapeDtypeStruct(*m) for m in made),
+        in_specs=[SMEM] + [VMEM] * 4,
+        out_specs=(VMEM,) * 6,
+        scratch_shapes=scratch,
+        compiler_params=grant(12),
+        name="attend_first",
+    )(spans, seg, q, q_other, blocks)
+    return pl.pallas_call(
+        second_kernel,
         out_shape=(
             jax.ShapeDtypeStruct((BLOCK, 2 * width), jnp.bfloat16),
-            jax.ShapeDtypeStruct((TALLY, HD), jnp.float32),
+            jax.ShapeDtypeStruct((TALLY, HD), f32),
         ),
-        in_specs=[SMEM] + [VMEM] * 5,
+        in_specs=[SMEM] + [VMEM] * 7,
         out_specs=(VMEM, VMEM),
-        scratch_shapes=[
-            pltpu.VMEM((16, SPAN, 2 * HD), jnp.bfloat16),
-            pltpu.VMEM((2, width, HD), jnp.bfloat16),
-            pltpu.SMEM((16,), jnp.int32),
-            pltpu.SMEM((33,), jnp.int32),
-            pltpu.VMEM((2, 1, SPAN), jnp.float32),
-            pltpu.VMEM((2, 1, width), jnp.float32),
-            pltpu.VMEM((2, 1, width), jnp.float32),
-            pltpu.VMEM((2, HD, width), jnp.float32),
-        ],
+        scratch_shapes=[pltpu.VMEM(*m) for m in state] + scratch,
         compiler_params=grant(12),
-        name="attend",
-    )(spans, seg, q, q_other, a, b)
+        name="attend_second",
+    )(spans, more_blocks, *made)
 
 
 def multiply(first, heads_ref, w_ref, other_ref, out_ref):
@@ -305,20 +328,18 @@
     both = ("context", "tensor")
     f32 = jnp.float32
     cat = lambda *a: jnp.concatenate(a, axis=0)
-    along_x = [[x * NZ + z for x in range(NX)] for z in range(NZ)]
-    gather = lambda a: lax.all_gather(a, "context", axis=0, tiled=True, axis_index_groups=along_x)
-
     in_hbm = lambda a: pltpu.with_memory_space_constraint(a, pltpu.HBM)
 
     kv1 = prepare(in_hbm(keys), in_hbm(values), in_hbm(loss_mask))
     r1 = lax.ppermute(kv1, both, perm_context("z", inner))
-    near = gather(kv1)
-    r2 = lax.ppermute(cat(kv1, r1), both, perm_context("z", outer))
     q_other = lax.ppermute(queries[0], "tensor", SWAP)
     packed = pack(in_hbm(out_weight))
+    kv2 = cat(kv1, r1)
+    kv4 = cat(kv2, lax.ppermute(kv2, both, perm_context("z", outer)))
     weight_other = lax.ppermute(packed, "tensor", SWAP)
-    far = gather(cat(r1, r2))
-    mine, tally = attention(span_order, segment_ids.reshape(32, SPAN), queries[0], q_other, near, far)
+    kv8 = cat(kv4, lax.ppermute(kv4, both, perm_context("x", inner)))
+    r8 = lax.ppermute(kv8, both, perm_context("x", outer))
+    mine, tally = attention(span_order, segment_ids.reshape(32, SPAN), queries[0], q_other, kv8, r8)
     theirs = lax.ppermute(mine, "tensor", SWAP)
 
     inward, outward = perm_tensor(inner), perm_tensor(outer)

time: 119 us -> 115 us (0.966)
  blocking collectives: 20.4 us -> 0 us
  waiting for transfers between devices: 23.8 us -> 36.2 us
  starting transfers between devices: 60.7 us -> 63.1 us
    all_gather x2 -> x0, blocking collectives: 20.4 us -> none  [per_device(): lax.all_gather(a, 'context', axis=0, tiled=True, axis_index_groups=along_x)]
    ppermute x1 -> x3, waiting for transfers between devices: 0.01 us -> 11.5 us  [the longest x1 6.1 us: per_device(): kv4 = cat(kv2, lax.ppermute(kv2, both, perm_context('z', outer)))]
    ppermute x1, starting transfers between devices: 9.86 us -> 3.8 us  [per_device(): theirs = lax.ppermute(mine, 'tensor', SWAP)]
    ppermute x1 -> x3, starting transfers between devices: 1.92 us -> 6.9 us  [the longest x1 3.05 us: per_device(): kv8 = cat(kv4, lax.ppermute(kv4, both, perm_context('x', inner)))]
    ppermute x1, starting transfers between devices: 7.75 us -> 10.6 us  [per_device(): q_other = lax.ppermute(queries[0], 'tensor', SWAP)]
    pallas_call x1 -> x2, Pallas kernels: 5.57 us -> 6.22 us  [the longest x1 3.36 us: attention(): pl.pallas_call(second_kernel, out_shape=(jax.ShapeDtypeStruct((BLOCK, 2 *...]
  transfers between devices with their start and end apart: 11 -> 13, of which waited for: 6 -> 9; matrix products, arithmetic and copies ran while one was open for 1% -> 1% of each run, Pallas kernels for 7% -> 8%
where the time goes in v3:
time: 115 us; the launch traced here: 114 us
  starting transfers between devices  63.1 us (55%)
  waiting for transfers between devices  36.2 us (31%)
  Pallas kernels  12.2 us (11%)
  other arithmetic  1.88 us (2%)
    ppermute x1, starting transfers between devices, per_device(): weight_other = lax.ppermute(packed, 'tensor', SWAP)  12.6 us
    ppermute x1, starting transfers between devices, per_device(): q_other = lax.ppermute(queries[0], 'tensor', SWAP)  10.6 us
    ppermute x1, starting transfers between devices, per_device(): two = lax.ppermute(one, 'tensor', SWAP)  9.25 us
    ppermute x1, waiting for transfers between devices, per_device(): mid = lax.ppermute(add(rest[0:2], far), 'tensor', inward)  6.56 us
    ppermute x1, waiting for transfers between devices, per_device(): kv4 = cat(kv2, lax.ppermute(kv2, both, perm_context('z', outer)))  6.1 us
    ppermute x1, waiting for transfers between devices, per_device(): kv8 = cat(kv4, lax.ppermute(kv4, both, perm_context('x', inner)))  5.44 us
    ppermute x1, starting transfers between devices, per_device(): r1 = lax.ppermute(kv1, both, perm_context('z', inner))  5.3 us
    ppermute x1, starting transfers between devices, per_device(): mid = lax.ppermute(add(rest[0:2], far), 'tensor', inward)  5.27 us
  transfers between devices with their start and end apart: 13, of which 9 were waited for; matrix products, arithmetic and copies ran while one was open for 1% of the time, Pallas kernels for 8%

profile of v3, /device:TPU:1, one launch (start us, length us, event | category | flops | bytes accessed | tf_op | source)
XLA Modules:
  0.0 114.2 jit_solution(8043074487893404785)
XLA Ops:
  0.0 2.4 %pack.1 = bf16[8,512,512]{2,1,0:T(8,128)(2,1)S(1)} custom-call(bf16[512,8192]{1,0:T(8,128)(2,1)} %w_ref.5), custom_call_target="tpu_custom_call" | custom-call | tf_op jit(solution)/shard_map/pack/pallas_call | solution.py:122
  2.4 12.6 %collective-permute-start.6 = (bf16[8,512,512]{2,1,0:T(8,128)(2,1)S(1)}, bf16[8,512,512]{2,1,0:T(8,128)(2,1)S(1)}, u32[]{:S(2)}, u32[]{:S(2)}) collective-permute-start(bf16[8,512,512]{2,1,0:T(8,128)(2,1)S(1)} %pack.1), channel_id=1, source_target_pairs={{0,1},{1,0},{2,3},{3,2},{4,5},{5,4},{6,7},{7,6},{8,9},{9,8},{10,11... | collective-permute-start | bytes 12582920 | tf_op jit(solution)/shard_map/ppermute | solution.py:339
  15.9 5.3 %collective-permute-start = (bf16[136,256]{1,0:T(8,128)(2,1)S(1)}, bf16[136,256]{1,0:T(8,128)(2,1)S(1)}, u32[]{:S(2)}, u32[]{:S(2)}) collective-permute-start(bf16[136,256]{1,0:T(8,128)(2,1)S(1)} %prepare.1), channel_id=1, source_target_pairs={{0,16},{1,49},{2,18},{3,51},{4,20},{5,53},{6,22},{7,55},{8,24},{9,... | collective-permute-start | bytes 208904 | tf_op jit(solution)/shard_map/ppermute | solution.py:334
  21.2 2.8 %collective-permute-done = bf16[136,256]{1,0:T(8,128)(2,1)S(1)} collective-permute-done((bf16[136,256]{1,0:T(8,128)(2,1)S(1)}, bf16[136,256]{1,0:T(8,128)(2,1)S(1)}, u32[]{:S(2)}, u32[]{:S(2)}) %collective-permute-start) | collective-permute-done | bytes 69664 | tf_op jit(solution)/shard_map/ppermute | solution.py:334
  24.0 1.9 %collective-permute-start.1 = (bf16[272,256]{1,0:T(8,128)(2,1)S(1)}, bf16[272,256]{1,0:T(8,128)(2,1)S(1)}, u32[]{:S(2)}, u32[]{:S(2)}) collective-permute-start(bf16[272,256]{1,0:T(8,128)(2,1)S(1)} %pad_maximum_fusion.2), channel_id=1, source_target_pairs={{0,48},{1,17},{2,50},{3,19},{4,52},{5,21},{6,54},{7,23},{8,56},{9,... | collective-permute-start | bytes 417800 | tf_op jit(solution)/shard_map/ppermute | solution.py:338
  25.9 6.1 %collective-permute-done.1 = bf16[272,256]{1,0:T(8,128)(2,1)S(1)} collective-permute-done((bf16[272,256]{1,0:T(8,128)(2,1)S(1)}, bf16[272,256]{1,0:T(8,128)(2,1)S(1)}, u32[]{:S(2)}, u32[]{:S(2)}) %collective-permute-start.1) | collective-permute-done | bytes 139296 | tf_op jit(solution)/shard_map/ppermute | solution.py:338
  32.0 3.1 %collective-permute-start.2 = (bf16[544,256]{1,0:T(8,128)(2,1)S(1)}, bf16[544,256]{1,0:T(8,128)(2,1)S(1)}, u32[]{:S(2)}, u32[]{:S(2)}) collective-permute-start(bf16[544,256]{1,0:T(8,128)(2,1)S(1)} %pad_maximum_fusion.1), channel_id=1, source_target_pairs={{0,64},{1,193},{2,66},{3,195},{4,68},{5,197},{6,70},{7,199},{8,72}... | collective-permute-start | bytes 835592 | tf_op jit(solution)/shard_map/ppermute | solution.py:340
  35.1 5.4 %collective-permute-done.2 = bf16[544,256]{1,0:T(8,128)(2,1)S(1)} collective-permute-done((bf16[544,256]{1,0:T(8,128)(2,1)S(1)}, bf16[544,256]{1,0:T(8,128)(2,1)S(1)}, u32[]{:S(2)}, u32[]{:S(2)}) %collective-permute-start.2) | collective-permute-done | bytes 278560 | tf_op jit(solution)/shard_map/ppermute | solution.py:340
  40.6 1.9 %collective-permute-start.3 = (bf16[1088,256]{1,0:T(8,128)(2,1)S(1)}, bf16[1088,256]{1,0:T(8,128)(2,1)S(1)}, u32[]{:S(2)}, u32[]{:S(2)}) collective-permute-start(bf16[1088,256]{1,0:T(8,128)(2,1)S(1)} %pad_maximum_fusion.blocks_ref), channel_id=1, source_target_pairs={{0,192},{1,65},{2,194},{3,67},{4,196},{5,69},{6,198},{7,71},{8,200... | collective-permute-start | bytes 1671176 | tf_op jit(solution)/shard_map/ppermute | solution.py:341
  42.5 10.6 %collective-permute-start.4 = (bf16[256,512]{1,0:T(8,128)(2,1)S(1)}, bf16[256,512]{1,0:T(8,128)(2,1)S(1)}, u32[]{:S(2)}, u32[]{:S(2)}) collective-permute-start(bf16[256,512]{1,0:T(8,128)(2,1)S(1)} %bitcast.16), channel_id=1, source_target_pairs={{0,1},{1,0},{2,3},{3,2},{4,5},{5,4},{6,7},{7,6},{8,9},{9,8},{10,11... | collective-permute-start | bytes 786440 | tf_op jit(solution)/shard_map/ppermute | solution.py:335
  54.3 2.9 %attend_first.1 = (bf16[2,1024,128]{2,1,0:T(8,128)(2,1)S(1)}, f32[2,1,128]{2,1,0:T(1,128)S(1)}, f32[2,1,1024]{2,1,0:T(1,128)S(1)}, f32[2,1,1024]{2,1,0:T(1,128)S...) custom-call(s32[32]{0:T(128)S(1)} %copy-done.3, s32[32,128]{1,0:T(8,128)S(1)} %bitcast.18, ...), custom_call_target="tpu_custom_call" | custom-call | tf_op jit(solution)/shard_map/attend_first/pallas_call | solution.py:236
  57.2 3.4 %attend_second.1 = (bf16[136,2048]{1,0:T(8,128)(2,1)S(1)}, f32[8,128]{1,0:T(8,128)S(1)}) custom-call(s32[32]{0:T(128)S(1)} %copy-done.3, bf16[1088,256]{1,0:T(8,128)(2,1)S(1)} %collective-permute-done.3.blocks_ref, bf16[2,1024,128]{2,1,0:T(8,128)(2,1)S(1)} %get-tuple-element.15.q8, f32[2,1,128]{2,1,0:T(1,128)S(1)} %get-tuple-element.16.lo_ref, ...), custom_call_target="tpu_custom_call" | custom-call | tf_op jit(solution)/shard_map/attend_second/pallas_call | solution.py:245
  60.6 3.8 %collective-permute-start.5 = (bf16[136,2048]{1,0:T(8,128)(2,1)S(1)}, bf16[136,2048]{1,0:T(8,128)(2,1)S(1)}, u32[]{:S(2)}, u32[]{:S(2)}) collective-permute-start(bf16[136,2048]{1,0:T(8,128)(2,1)S(1)} %get-tuple-element.21.mine_ref), channel_id=1, source_target_pairs={{0,1},{1,0},{2,3},{3,2},{4,5},{5,4},{6,7},{7,6},{8,9},{9,8},{10,11... | collective-permute-start | bytes 1671176 | tf_op jit(solution)/shard_map/ppermute | solution.py:343
  66.9 3.5 %collective-permute-start.7 = (bf16[2,256,512]{2,1,0:T(8,128)(2,1)S(1)}, bf16[2,256,512]{2,1,0:T(8,128)(2,1)S(1)}, u32[]{:S(2)}, u32[]{:S(2)}) collective-permute-start(bf16[2,256,512]{2,1,0:T(8,128)(2,1)S(1)} %get-tuple-element.23), channel_id=1, source_target_pairs={{0,14},{1,3},{2,4},{3,1},{4,2},{5,7},{6,8},{7,5},{8,6},{9,11},{10,... | collective-permute-start | bytes 1572872 | tf_op jit(solution)/shard_map/ppermute | solution.py:347
  70.4 1.8 %project.1 = bf16[6,256,512]{2,1,0:T(8,128)(2,1)S(1)} custom-call(bf16[256,1024]{1,0:T(8,128)(2,1)S(1)} %get-tuple-element.22.heads_ref, bf16[512,8192]{1,0:T(8,128)(2,1)S(1)} %copy-done, bf16[8,512,512]{2,1,0:T(8,128)(2,1)S(1)} %collective-permute-done.6.other_ref), custom_call_target="tpu_custom_call" | custom-call | tf_op jit(solution)/shard_map/project/pallas_call | solution.py:313
  72.3 5.0 %collective-permute-done.7 = bf16[2,256,512]{2,1,0:T(8,128)(2,1)S(1)} collective-permute-done((bf16[2,256,512]{2,1,0:T(8,128)(2,1)S(1)}, bf16[2,256,512]{2,1,0:T(8,128)(2,1)S(1)}, u32[]{:S(2)}, u32[]{:S(2)}) %collective-permute-start.7) | collective-permute-done | bytes 524320 | tf_op jit(solution)/shard_map/ppermute | solution.py:347
  77.4 5.3 %collective-permute-start.8 = (bf16[2,256,512]{2,1,0:T(8,128)(2,1)S(1)}, bf16[2,256,512]{2,1,0:T(8,128)(2,1)S(1)}, u32[]{:S(2)}, u32[]{:S(2)}) collective-permute-start(bf16[2,256,512]{2,1,0:T(8,128)(2,1)S(1)} %add_convert_fusion.1), channel_id=1, source_target_pairs={{0,2},{1,15},{2,0},{3,5},{4,6},{5,3},{6,4},{7,9},{8,10},{9,7},{10,... | collective-permute-start | bytes 1572872 | tf_op jit(solution)/shard_map/ppermute | solution.py:352
  82.7 6.6 %collective-permute-done.8 = bf16[2,256,512]{2,1,0:T(8,128)(2,1)S(1)} collective-permute-done((bf16[2,256,512]{2,1,0:T(8,128)(2,1)S(1)}, bf16[2,256,512]{2,1,0:T(8,128)(2,1)S(1)}, u32[]{:S(2)}, u32[]{:S(2)}) %collective-permute-start.8) | collective-permute-done | bytes 524320 | tf_op jit(solution)/shard_map/ppermute | solution.py:352
  89.4 1.9 %collective-permute-start.9 = (bf16[2,256,512]{2,1,0:T(8,128)(2,1)S(1)}, bf16[2,256,512]{2,1,0:T(8,128)(2,1)S(1)}, u32[]{:S(2)}, u32[]{:S(2)}) collective-permute-start(bf16[2,256,512]{2,1,0:T(8,128)(2,1)S(1)} %add_convert_fusion), channel_id=1, source_target_pairs={{0,14},{1,3},{2,4},{3,1},{4,2},{5,7},{6,8},{7,5},{8,6},{9,11},{10,... | collective-permute-start | bytes 1572872 | tf_op jit(solution)/shard_map/ppermute | solution.py:353
  91.3 1.9 %collective-permute-start.11 = (f32[8,128]{1,0:T(8,128)S(1)}, f32[8,128]{1,0:T(8,128)S(1)}, u32[]{:S(2)}, u32[]{:S(2)}) collective-permute-start(f32[8,128]{1,0:T(8,128)S(1)} %get-tuple-element.24), channel_id=1, source_target_pairs={{0,256},{1,513},{2,258},{3,515},{4,260},{5,517},{6,262},{7,519},{8... | collective-permute-start | bytes 12296 | tf_op jit(solution)/shard_map/ppermute | solution.py:350
  93.3 2.4 %collective-permute-done.11 = f32[8,128]{1,0:T(8,128)S(1)} collective-permute-done((f32[8,128]{1,0:T(8,128)S(1)}, f32[8,128]{1,0:T(8,128)S(1)}, u32[]{:S(2)}, u32[]{:S(2)}) %collective-permute-start.11) | collective-permute-done | bytes 4128 | tf_op jit(solution)/shard_map/ppermute | solution.py:350
  95.7 9.3 %collective-permute-start.12 = (f32[8,128]{1,0:T(8,128)S(1)}, f32[8,128]{1,0:T(8,128)S(1)}, u32[]{:S(2)}, u32[]{:S(2)}) collective-permute-start(f32[8,128]{1,0:T(8,128)S(1)} %collective-permute-done.11), channel_id=1, source_target_pairs={{0,1},{1,0},{2,3},{3,2},{4,5},{5,4},{6,7},{7,6},{8,9},{9,8},{10,11... | collective-permute-start | bytes 12296 | tf_op jit(solution)/shard_map/ppermute | solution.py:351
  105.0 1.9 %collective-permute-start.10 = (bf16[256,512]{1,0:T(8,128)(2,1)S(1)}, bf16[256,512]{1,0:T(8,128)(2,1)S(1)}, u32[]{:S(2)}, u32[]{:S(2)}) collective-permute-start(bf16[256,512]{1,0:T(8,128)(2,1)S(1)} %fusion.2), channel_id=1, source_target_pairs={{0,2},{1,15},{2,0},{3,5},{4,6},{5,3},{6,4},{7,9},{8,10},{9,7},{10,... | collective-permute-start | bytes 786440 | tf_op jit(solution)/shard_map/ppermute | solution.py:354
  108.2 5.2 %collective-permute-done.10 = bf16[256,512]{1,0:T(8,128)(2,1)S(1)} collective-permute-done((bf16[256,512]{1,0:T(8,128)(2,1)S(1)}, bf16[256,512]{1,0:T(8,128)(2,1)S(1)}, u32[]{:S(2)}, u32[]{:S(2)}) %collective-permute-start.10) | collective-permute-done | bytes 262176 | tf_op jit(solution)/shard_map/ppermute | solution.py:354
  (28 shorter events, 6.9 us)
Async XLA Ops:
  0.0 65.9 %copy-start = (bf16[512,8192]{1,0:T(8,128)(2,1)S(1)}, bf16[512,8192]{1,0:T(8,128)(2,1)}, u32[]{:S(2)}) copy-start(bf16[512,8192]{1,0:T(8,128)(2,1)} %w_ref.5) | copy-start | bytes 25165828
  2.4 40.1 %copy-start.1 = (bf16[1,256,512]{2,1,0:T(8,128)(2,1)S(1)}, bf16[1,256,512]{2,1,0:T(8,128)(2,1)}, u32[]{:S(2)}) copy-start(bf16[1,256,512]{2,1,0:T(8,128)(2,1)} %param.7) | copy-start | bytes 786436
  2.4 51.9 %copy-start.2 = (s32[1,4096]{1,0:T(1,128)S(1)}, s32[1,4096]{1,0:T(1,128)}, u32[]{:S(2)}) copy-start(s32[1,4096]{1,0:T(1,128)} %param.11) | copy-start | bytes 49156
  2.4 51.9 %copy-start.3 = (s32[32]{0:T(128)S(1)}, s32[32]{0:T(128)}, u32[]{:S(2)}) copy-start(s32[32]{0:T(128)} %spans.3) | copy-start | bytes 388
  2.4 63.5 %collective-permute-start.6 = (bf16[8,512,512]{2,1,0:T(8,128)(2,1)S(1)}, bf16[8,512,512]{2,1,0:T(8,128)(2,1)S(1)}, u32[]{:S(2)}, u32[]{:S(2)}) collective-permute-start(bf16[8,512,512]{2,1,0:T(8,128)(2,1)S(1)} %pack.1), channel_id=1, source_target_pairs={{0,1},{1,0},{2,3},{3,2},{4,5},{5,4},{6,7},{7,6},{8,9},{9,8},{10,11... | collective-permute-start | bytes 12582920 | tf_op jit(solution)/shard_map/ppermute | solution.py:339
  15.9 8.1 %collective-permute-start = (bf16[136,256]{1,0:T(8,128)(2,1)S(1)}, bf16[136,256]{1,0:T(8,128)(2,1)S(1)}, u32[]{:S(2)}, u32[]{:S(2)}) collective-permute-start(bf16[136,256]{1,0:T(8,128)(2,1)S(1)} %prepare.1), channel_id=1, source_target_pairs={{0,16},{1,49},{2,18},{3,51},{4,20},{5,53},{6,22},{7,55},{8,24},{9,... | collective-permute-start | bytes 208904 | tf_op jit(solution)/shard_map/ppermute | solution.py:334
  24.0 8.0 %collective-permute-start.1 = (bf16[272,256]{1,0:T(8,128)(2,1)S(1)}, bf16[272,256]{1,0:T(8,128)(2,1)S(1)}, u32[]{:S(2)}, u32[]{:S(2)}) collective-permute-start(bf16[272,256]{1,0:T(8,128)(2,1)S(1)} %pad_maximum_fusion.2), channel_id=1, source_target_pairs={{0,48},{1,17},{2,50},{3,19},{4,52},{5,21},{6,54},{7,23},{8,56},{9,... | collective-permute-start | bytes 417800 | tf_op jit(solution)/shard_map/ppermute | solution.py:338
  32.0 8.5 %collective-permute-start.2 = (bf16[544,256]{1,0:T(8,128)(2,1)S(1)}, bf16[544,256]{1,0:T(8,128)(2,1)S(1)}, u32[]{:S(2)}, u32[]{:S(2)}) collective-permute-start(bf16[544,256]{1,0:T(8,128)(2,1)S(1)} %pad_maximum_fusion.1), channel_id=1, source_target_pairs={{0,64},{1,193},{2,66},{3,195},{4,68},{5,197},{6,70},{7,199},{8,72}... | collective-permute-start | bytes 835592 | tf_op jit(solution)/shard_map/ppermute | solution.py:340
  40.6 16.6 %collective-permute-start.3 = (bf16[1088,256]{1,0:T(8,128)(2,1)S(1)}, bf16[1088,256]{1,0:T(8,128)(2,1)S(1)}, u32[]{:S(2)}, u32[]{:S(2)}) collective-permute-start(bf16[1088,256]{1,0:T(8,128)(2,1)S(1)} %pad_maximum_fusion.blocks_ref), channel_id=1, source_target_pairs={{0,192},{1,65},{2,194},{3,67},{4,196},{5,69},{6,198},{7,71},{8,200... | collective-permute-start | bytes 1671176 | tf_op jit(solution)/shard_map/ppermute | solution.py:341
  42.5 11.8 %collective-permute-start.4 = (bf16[256,512]{1,0:T(8,128)(2,1)S(1)}, bf16[256,512]{1,0:T(8,128)(2,1)S(1)}, u32[]{:S(2)}, u32[]{:S(2)}) collective-permute-start(bf16[256,512]{1,0:T(8,128)(2,1)S(1)} %bitcast.16), channel_id=1, source_target_pairs={{0,1},{1,0},{2,3},{3,2},{4,5},{5,4},{6,7},{7,6},{8,9},{9,8},{10,11... | collective-permute-start | bytes 786440 | tf_op jit(solution)/shard_map/ppermute | solution.py:335
  60.6 5.4 %collective-permute-start.5 = (bf16[136,2048]{1,0:T(8,128)(2,1)S(1)}, bf16[136,2048]{1,0:T(8,128)(2,1)S(1)}, u32[]{:S(2)}, u32[]{:S(2)}) collective-permute-start(bf16[136,2048]{1,0:T(8,128)(2,1)S(1)} %get-tuple-element.21.mine_ref), channel_id=1, source_target_pairs={{0,1},{1,0},{2,3},{3,2},{4,5},{5,4},{6,7},{7,6},{8,9},{9,8},{10,11... | collective-permute-start | bytes 1671176 | tf_op jit(solution)/shard_map/ppermute | solution.py:343
  66.9 10.4 %collective-permute-start.7 = (bf16[2,256,512]{2,1,0:T(8,128)(2,1)S(1)}, bf16[2,256,512]{2,1,0:T(8,128)(2,1)S(1)}, u32[]{:S(2)}, u32[]{:S(2)}) collective-permute-start(bf16[2,256,512]{2,1,0:T(8,128)(2,1)S(1)} %get-tuple-element.23), channel_id=1, source_target_pairs={{0,14},{1,3},{2,4},{3,1},{4,2},{5,7},{6,8},{7,5},{8,6},{9,11},{10,... | collective-permute-start | bytes 1572872 | tf_op jit(solution)/shard_map/ppermute | solution.py:347
  77.4 30.1 %copy-start.4 = (s32[1,256]{1,0:T(1,128)S(1)}, s32[1,256]{1,0:T(1,128)}, u32[]{:S(2)}) copy-start(s32[1,256]{1,0:T(1,128)} %mask_hbm.1) | copy-start | bytes 3076
  77.4 11.8 %collective-permute-start.8 = (bf16[2,256,512]{2,1,0:T(8,128)(2,1)S(1)}, bf16[2,256,512]{2,1,0:T(8,128)(2,1)S(1)}, u32[]{:S(2)}, u32[]{:S(2)}) collective-permute-start(bf16[2,256,512]{2,1,0:T(8,128)(2,1)S(1)} %add_convert_fusion.1), channel_id=1, source_target_pairs={{0,2},{1,15},{2,0},{3,5},{4,6},{5,3},{6,4},{7,9},{8,10},{9,7},{10,... | collective-permute-start | bytes 1572872 | tf_op jit(solution)/shard_map/ppermute | solution.py:352
  89.4 15.5 %collective-permute-start.9 = (bf16[2,256,512]{2,1,0:T(8,128)(2,1)S(1)}, bf16[2,256,512]{2,1,0:T(8,128)(2,1)S(1)}, u32[]{:S(2)}, u32[]{:S(2)}) collective-permute-start(bf16[2,256,512]{2,1,0:T(8,128)(2,1)S(1)} %add_convert_fusion), channel_id=1, source_target_pairs={{0,14},{1,3},{2,4},{3,1},{4,2},{5,7},{6,8},{7,5},{8,6},{9,11},{10,... | collective-permute-start | bytes 1572872 | tf_op jit(solution)/shard_map/ppermute | solution.py:353
  91.3 4.4 %collective-permute-start.11 = (f32[8,128]{1,0:T(8,128)S(1)}, f32[8,128]{1,0:T(8,128)S(1)}, u32[]{:S(2)}, u32[]{:S(2)}) collective-permute-start(f32[8,128]{1,0:T(8,128)S(1)} %get-tuple-element.24), channel_id=1, source_target_pairs={{0,256},{1,513},{2,258},{3,515},{4,260},{5,517},{6,262},{7,519},{8... | collective-permute-start | bytes 12296 | tf_op jit(solution)/shard_map/ppermute | solution.py:350
  95.7 11.3 %collective-permute-start.12 = (f32[8,128]{1,0:T(8,128)S(1)}, f32[8,128]{1,0:T(8,128)S(1)}, u32[]{:S(2)}, u32[]{:S(2)}) collective-permute-start(f32[8,128]{1,0:T(8,128)S(1)} %collective-permute-done.11), channel_id=1, source_target_pairs={{0,1},{1,0},{2,3},{3,2},{4,5},{5,4},{6,7},{7,6},{8,9},{9,8},{10,11... | collective-permute-start | bytes 12296 | tf_op jit(solution)/shard_map/ppermute | solution.py:351
  105.0 8.3 %collective-permute-start.10 = (bf16[256,512]{1,0:T(8,128)(2,1)S(1)}, bf16[256,512]{1,0:T(8,128)(2,1)S(1)}, u32[]{:S(2)}, u32[]{:S(2)}) collective-permute-start(bf16[256,512]{1,0:T(8,128)(2,1)S(1)} %fusion.2), channel_id=1, source_target_pairs={{0,2},{1,15},{2,0},{3,5},{4,6},{5,3},{6,4},{7,9},{8,10},{9,7},{10,... | collective-permute-start | bytes 786440 | tf_op jit(solution)/shard_map/ppermute | solution.py:354

commit v4 on v3

--- a/solution.py
+++ b/solution.py
@@ -130,44 +130,55 @@
     )(w)
 
 
-def attend(first_block, spans, blocks_ref, q8, lo_ref, m_ref, l_ref, acc, kv, places, items):
+def attend(first_block, spans, blocks_ref, q8, lo_ref, m_ref, l_ref, acc, k_pair, v_pair, places, items):
     f32 = jnp.float32
     context = lax.axis_index("context")
     core = lax.rem(lax.axis_index("tensor"), NC)
     width = q8.shape[1]
-    count = jnp.int32(0)
     for b in range(8):
-        kv[b] = blocks_ref[b * BLOCK : b * BLOCK + SPAN, :]
+        k_pair[b] = blocks_ref[b * BLOCK : b * BLOCK + SPAN, :HD]
+        v_pair[b] = blocks_ref[b * BLOCK : b * BLOCK + SPAN, HD:]
         places[b] = spans[gathered_slot(context, core, first_block + b)]
+    places[8] = 1 << 20
+    k_pair[8] = jnp.zeros((SPAN, HD), jnp.bfloat16)
+    v_pair[8] = jnp.zeros((SPAN, HD), jnp.bfloat16)
+
     for i in range(2):
         first = jnp.min(lo_ref[i]).astype(jnp.int32)
         q_pos = spans[2 * context + i]
+        count = jnp.int32(0)
         for b in range(8):
-            items[count] = i * 8 + b
+            items[count] = b
             seen = (places[b] <= q_pos) & ((places[b] + 1) * SPAN > first)
             count = count + seen.astype(jnp.int32)
-
-    def step(j, carry):
-        item = items[j]
-        i, b = lax.shift_right_logical(item, 3), item & 7
-        pos = lax.broadcasted_iota(jnp.int32, (SPAN, SPAN), 0) + places[b] * SPAN
-        hi = lax.broadcasted_iota(jnp.int32, (SPAN, SPAN), 1) + spans[2 * context + i] * SPAN
-        bias = jnp.where((pos.astype(f32) >= lo_ref[i]) & (pos <= hi), 0.0, LOW)
-        s = lax.dot_general(kv[b, :, :HD], q8[i], (((1,), (1,)), ((), ())), preferred_element_type=f32)
-        s = s * (HD ** (-0.5) * LOG2E) + jnp.concatenate([bias] * (width // SPAN), axis=1)
-        old = m_ref[i]
-        new = jnp.maximum(old, jnp.max(s, axis=0, keepdims=True))
-        alpha = jnp.exp2(old - new)
-        p = jnp.exp2(s - new)
-        m_ref[i] = new
-        l_ref[i] = l_ref[i] * alpha + jnp.sum(p, axis=0, keepdims=True)
-        add = lax.dot_general(
-            kv[b, :, HD:], p.astype(jnp.bfloat16), (((0,), (0,)), ((), ())), preferred_element_type=f32
-        )
-        acc[i] = acc[i] * alpha + add
-        return carry
-
-    lax.fori_loop(0, count, step, 0)
+        items[count] = 8
+        hi = lax.broadcasted_iota(jnp.int32, (SPAN, SPAN), 1) + q_pos * SPAN
+        row = lax.broadcasted_iota(jnp.int32, (SPAN, SPAN), 0)
+
+        def bias(place):
+            pos = row + place * SPAN
+            return jnp.where((pos.astype(f32) >= lo_ref[i]) & (pos <= hi), 0.0, LOW)
+
+        def step(j, carry):
+            b, c = items[2 * j], items[2 * j + 1]
+            both = jnp.concatenate([bias(places[b]), bias(places[c])], axis=0)
+            k = jnp.concatenate([k_pair[b], k_pair[c]], axis=0)
+            v = jnp.concatenate([v_pair[b], v_pair[c]], axis=0)
+            s = lax.dot_general(k, q8[i], (((1,), (1,)), ((), ())), preferred_element_type=f32)
+            s = s * (HD ** (-0.5) * LOG2E) + jnp.concatenate([both] * (width // SPAN), axis=1)
+            old = m_ref[i]
+            new = jnp.maximum(old, jnp.max(s, axis=0, keepdims=True))
+            alpha = jnp.exp2(old - new)
+            p = jnp.exp2(s - new)
+            m_ref[i] = new
+            l_ref[i] = l_ref[i] * alpha + jnp.sum(p, axis=0, keepdims=True)
+            add = lax.dot_general(
+                v, p.astype(jnp.bfloat16), (((0,), (0,)), ((), ())), preferred_element_type=f32
+            )
+            acc[i] = acc[i] * alpha + add
+            return carry
+
+        lax.fori_loop(0, lax.shift_right_logical(count + 1, 1), step, 0)
     tally = jnp.zeros((TALLY, HD), f32)
     for b in range(8):
         tally += blocks_ref[b * BLOCK + SPAN : (b + 1) * BLOCK, :HD].astype(f32)
@@ -175,7 +186,7 @@
 
 
 def first_kernel(
-    spans, seg_ref, q_ref, q_other_ref, blocks_ref, q8, lo_ref, m_ref, l_ref, acc, tally_ref, kv, places, items
+    spans, seg_ref, q_ref, q_other_ref, blocks_ref, q8, lo_ref, m_ref, l_ref, acc, tally_ref, k_pair, v_pair, places, items
 ):
     f32 = jnp.float32
     context = lax.axis_index("context")
@@ -195,18 +206,18 @@
     m_ref[...] = jnp.full(m_ref.shape, LOW, f32)
     l_ref[...] = jnp.zeros(l_ref.shape, f32)
     acc[...] = jnp.zeros(acc.shape, f32)
-    tally_ref[...] = attend(0, spans, blocks_ref, q8, lo_ref, m_ref, l_ref, acc, kv, places, items)
+    tally_ref[...] = attend(0, spans, blocks_ref, q8, lo_ref, m_ref, l_ref, acc, k_pair, v_pair, places, items)
 
 
 def second_kernel(
-    spans, blocks_ref, q8, lo_ref, m_in, l_in, acc_in, tally_in, out_ref, tally_ref, m_ref, l_ref, acc, kv, places, items
+    spans, blocks_ref, q8, lo_ref, m_in, l_in, acc_in, tally_in, out_ref, tally_ref, m_ref, l_ref, acc, k_pair, v_pair, places, items
 ):
     f32 = jnp.float32
     width = q8.shape[1]
     m_ref[...] = m_in[...]
     l_ref[...] = l_in[...]
     acc[...] = acc_in[...]
-    tally = attend(8, spans, blocks_ref, q8, lo_ref, m_ref, l_ref, acc, kv, places, items)
+    tally = attend(8, spans, blocks_ref, q8, lo_ref, m_ref, l_ref, acc, k_pair, v_pair, places, items)
     tally_ref[...] = tally_in[...] + tally
     row = lax.broadcasted_iota(jnp.int32, (TALLY, width), 0)
     for i in range(2):
@@ -229,9 +240,10 @@
     state = [((2, 1, width), f32), ((2, 1, width), f32), ((2, HD, width), f32)]
     made = [((2, width, HD), jnp.bfloat16), ((2, 1, SPAN), f32), *state, ((TALLY, HD), f32)]
     scratch = [
-        pltpu.VMEM((8, SPAN, 2 * HD), jnp.bfloat16),
-        pltpu.SMEM((8,), jnp.int32),
-        pltpu.SMEM((17,), jnp.int32),
+        pltpu.VMEM((9, SPAN, HD), jnp.bfloat16),
+        pltpu.VMEM((9, SPAN, HD), jnp.bfloat16),
+        pltpu.SMEM((9,), jnp.int32),
+        pltpu.SMEM((10,), jnp.int32),
     ]
     made = pl.pallas_call(
         first_kernel,

time: 115 us -> 114 us (level)
  no operation moved by 1% of the time
where the time goes in v4:
time: 114 us
  starting transfers between devices  62.8 us (55%)
  waiting for transfers between devices  36.2 us (32%)
  Pallas kernels  12.3 us (11%)
  other arithmetic  1.88 us (2%)
    ppermute x1, starting transfers between devices, per_device(): weight_other = lax.ppermute(packed, 'tensor', SWAP)  12.6 us
    ppermute x1, starting transfers between devices, per_device(): q_other = lax.ppermute(queries[0], 'tensor', SWAP)  10.6 us
    ppermute x1, starting transfers between devices, per_device(): two = lax.ppermute(one, 'tensor', SWAP)  9.25 us
    ppermute x1, waiting for transfers between devices, per_device(): mid = lax.ppermute(add(rest[0:2], far), 'tensor', inward)  6.56 us
    ppermute x1, waiting for transfers between devices, per_device(): kv4 = cat(kv2, lax.ppermute(kv2, both, perm_context('z', outer)))  6.1 us
    ppermute x1, waiting for transfers between devices, per_device(): kv8 = cat(kv4, lax.ppermute(kv4, both, perm_context('x', inner)))  5.44 us
    ppermute x1, starting transfers between devices, per_device(): r1 = lax.ppermute(kv1, both, perm_context('z', inner))  5.3 us
    ppermute x1, starting transfers between devices, per_device(): mid = lax.ppermute(add(rest[0:2], far), 'tensor', inward)  5.26 us
  transfers between devices with their start and end apart: 13, of which 9 were waited for; matrix products, arithmetic and copies ran while one was open for 1% of the time, Pallas kernels for 8%

profile of v4, /device:TPU:1, one launch (start us, length us, event | category | flops | bytes accessed | tf_op | source)
XLA Modules:
  0.0 114.0 jit_solution(9031281793052340890)
XLA Ops:
  0.0 2.4 %pack.1 = bf16[8,512,512]{2,1,0:T(8,128)(2,1)S(1)} custom-call(bf16[512,8192]{1,0:T(8,128)(2,1)} %w_ref.5), custom_call_target="tpu_custom_call" | custom-call | tf_op jit(solution)/shard_map/pack/pallas_call | solution.py:122
  2.4 12.6 %collective-permute-start.6 = (bf16[8,512,512]{2,1,0:T(8,128)(2,1)S(1)}, bf16[8,512,512]{2,1,0:T(8,128)(2,1)S(1)}, u32[]{:S(2)}, u32[]{:S(2)}) collective-permute-start(bf16[8,512,512]{2,1,0:T(8,128)(2,1)S(1)} %pack.1), channel_id=1, source_target_pairs={{0,1},{1,0},{2,3},{3,2},{4,5},{5,4},{6,7},{7,6},{8,9},{9,8},{10,11... | collective-permute-start | bytes 12582920 | tf_op jit(solution)/shard_map/ppermute | solution.py:351
  15.9 5.3 %collective-permute-start = (bf16[136,256]{1,0:T(8,128)(2,1)S(1)}, bf16[136,256]{1,0:T(8,128)(2,1)S(1)}, u32[]{:S(2)}, u32[]{:S(2)}) collective-permute-start(bf16[136,256]{1,0:T(8,128)(2,1)S(1)} %prepare.1), channel_id=1, source_target_pairs={{0,16},{1,49},{2,18},{3,51},{4,20},{5,53},{6,22},{7,55},{8,24},{9,... | collective-permute-start | bytes 208904 | tf_op jit(solution)/shard_map/ppermute | solution.py:346
  21.2 2.8 %collective-permute-done = bf16[136,256]{1,0:T(8,128)(2,1)S(1)} collective-permute-done((bf16[136,256]{1,0:T(8,128)(2,1)S(1)}, bf16[136,256]{1,0:T(8,128)(2,1)S(1)}, u32[]{:S(2)}, u32[]{:S(2)}) %collective-permute-start) | collective-permute-done | bytes 69664 | tf_op jit(solution)/shard_map/ppermute | solution.py:346
  24.0 1.9 %collective-permute-start.1 = (bf16[272,256]{1,0:T(8,128)(2,1)S(1)}, bf16[272,256]{1,0:T(8,128)(2,1)S(1)}, u32[]{:S(2)}, u32[]{:S(2)}) collective-permute-start(bf16[272,256]{1,0:T(8,128)(2,1)S(1)} %pad_maximum_fusion.2), channel_id=1, source_target_pairs={{0,48},{1,17},{2,50},{3,19},{4,52},{5,21},{6,54},{7,23},{8,56},{9,... | collective-permute-start | bytes 417800 | tf_op jit(solution)/shard_map/ppermute | solution.py:350
  25.9 6.1 %collective-permute-done.1 = bf16[272,256]{1,0:T(8,128)(2,1)S(1)} collective-permute-done((bf16[272,256]{1,0:T(8,128)(2,1)S(1)}, bf16[272,256]{1,0:T(8,128)(2,1)S(1)}, u32[]{:S(2)}, u32[]{:S(2)}) %collective-permute-start.1) | collective-permute-done | bytes 139296 | tf_op jit(solution)/shard_map/ppermute | solution.py:350
  32.0 3.1 %collective-permute-start.2 = (bf16[544,256]{1,0:T(8,128)(2,1)S(1)}, bf16[544,256]{1,0:T(8,128)(2,1)S(1)}, u32[]{:S(2)}, u32[]{:S(2)}) collective-permute-start(bf16[544,256]{1,0:T(8,128)(2,1)S(1)} %pad_maximum_fusion.1), channel_id=1, source_target_pairs={{0,64},{1,193},{2,66},{3,195},{4,68},{5,197},{6,70},{7,199},{8,72}... | collective-permute-start | bytes 835592 | tf_op jit(solution)/shard_map/ppermute | solution.py:352
  35.1 5.4 %collective-permute-done.2 = bf16[544,256]{1,0:T(8,128)(2,1)S(1)} collective-permute-done((bf16[544,256]{1,0:T(8,128)(2,1)S(1)}, bf16[544,256]{1,0:T(8,128)(2,1)S(1)}, u32[]{:S(2)}, u32[]{:S(2)}) %collective-permute-start.2) | collective-permute-done | bytes 278560 | tf_op jit(solution)/shard_map/ppermute | solution.py:352
  40.6 1.9 %collective-permute-start.3 = (bf16[1088,256]{1,0:T(8,128)(2,1)S(1)}, bf16[1088,256]{1,0:T(8,128)(2,1)S(1)}, u32[]{:S(2)}, u32[]{:S(2)}) collective-permute-start(bf16[1088,256]{1,0:T(8,128)(2,1)S(1)} %pad_maximum_fusion.blocks_ref), channel_id=1, source_target_pairs={{0,192},{1,65},{2,194},{3,67},{4,196},{5,69},{6,198},{7,71},{8,200... | collective-permute-start | bytes 1671176 | tf_op jit(solution)/shard_map/ppermute | solution.py:353
  42.5 10.6 %collective-permute-start.4 = (bf16[256,512]{1,0:T(8,128)(2,1)S(1)}, bf16[256,512]{1,0:T(8,128)(2,1)S(1)}, u32[]{:S(2)}, u32[]{:S(2)}) collective-permute-start(bf16[256,512]{1,0:T(8,128)(2,1)S(1)} %bitcast.16), channel_id=1, source_target_pairs={{0,1},{1,0},{2,3},{3,2},{4,5},{5,4},{6,7},{7,6},{8,9},{9,8},{10,11... | collective-permute-start | bytes 786440 | tf_op jit(solution)/shard_map/ppermute | solution.py:347
  54.3 3.1 %attend_first.1 = (bf16[2,1024,128]{2,1,0:T(8,128)(2,1)S(1)}, f32[2,1,128]{2,1,0:T(1,128)S(1)}, f32[2,1,1024]{2,1,0:T(1,128)S(1)}, f32[2,1,1024]{2,1,0:T(1,128)S...) custom-call(s32[32]{0:T(128)S(1)} %copy-done.3, s32[32,128]{1,0:T(8,128)S(1)} %bitcast.18, ...), custom_call_target="tpu_custom_call" | custom-call | tf_op jit(solution)/shard_map/attend_first/pallas_call | solution.py:248
  57.4 3.2 %attend_second.1 = (bf16[136,2048]{1,0:T(8,128)(2,1)S(1)}, f32[8,128]{1,0:T(8,128)S(1)}) custom-call(s32[32]{0:T(128)S(1)} %copy-done.3, bf16[1088,256]{1,0:T(8,128)(2,1)S(1)} %collective-permute-done.3.blocks_ref, bf16[2,1024,128]{2,1,0:T(8,128)(2,1)S(1)} %get-tuple-element.15.q8, f32[2,1,128]{2,1,0:T(1,128)S(1)} %get-tuple-element.16.lo_ref, ...), custom_call_target="tpu_custom_call" | custom-call | tf_op jit(solution)/shard_map/attend_second/pallas_call | solution.py:257
  60.6 3.2 %collective-permute-start.5 = (bf16[136,2048]{1,0:T(8,128)(2,1)S(1)}, bf16[136,2048]{1,0:T(8,128)(2,1)S(1)}, u32[]{:S(2)}, u32[]{:S(2)}) collective-permute-start(bf16[136,2048]{1,0:T(8,128)(2,1)S(1)} %get-tuple-element.21.mine_ref), channel_id=1, source_target_pairs={{0,1},{1,0},{2,3},{3,2},{4,5},{5,4},{6,7},{7,6},{8,9},{9,8},{10,11... | collective-permute-start | bytes 1671176 | tf_op jit(solution)/shard_map/ppermute | solution.py:355
  66.4 3.9 %collective-permute-start.7 = (bf16[2,256,512]{2,1,0:T(8,128)(2,1)S(1)}, bf16[2,256,512]{2,1,0:T(8,128)(2,1)S(1)}, u32[]{:S(2)}, u32[]{:S(2)}) collective-permute-start(bf16[2,256,512]{2,1,0:T(8,128)(2,1)S(1)} %get-tuple-element.23), channel_id=1, source_target_pairs={{0,14},{1,3},{2,4},{3,1},{4,2},{5,7},{6,8},{7,5},{8,6},{9,11},{10,... | collective-permute-start | bytes 1572872 | tf_op jit(solution)/shard_map/ppermute | solution.py:359
  70.2 1.8 %project.1 = bf16[6,256,512]{2,1,0:T(8,128)(2,1)S(1)} custom-call(bf16[256,1024]{1,0:T(8,128)(2,1)S(1)} %get-tuple-element.22.heads_ref, bf16[512,8192]{1,0:T(8,128)(2,1)S(1)} %copy-done, bf16[8,512,512]{2,1,0:T(8,128)(2,1)S(1)} %collective-permute-done.6.other_ref), custom_call_target="tpu_custom_call" | custom-call | tf_op jit(solution)/shard_map/project/pallas_call | solution.py:325
  72.0 5.0 %collective-permute-done.7 = bf16[2,256,512]{2,1,0:T(8,128)(2,1)S(1)} collective-permute-done((bf16[2,256,512]{2,1,0:T(8,128)(2,1)S(1)}, bf16[2,256,512]{2,1,0:T(8,128)(2,1)S(1)}, u32[]{:S(2)}, u32[]{:S(2)}) %collective-permute-start.7) | collective-permute-done | bytes 524320 | tf_op jit(solution)/shard_map/ppermute | solution.py:359
  77.2 5.3 %collective-permute-start.8 = (bf16[2,256,512]{2,1,0:T(8,128)(2,1)S(1)}, bf16[2,256,512]{2,1,0:T(8,128)(2,1)S(1)}, u32[]{:S(2)}, u32[]{:S(2)}) collective-permute-start(bf16[2,256,512]{2,1,0:T(8,128)(2,1)S(1)} %add_convert_fusion.1), channel_id=1, source_target_pairs={{0,2},{1,15},{2,0},{3,5},{4,6},{5,3},{6,4},{7,9},{8,10},{9,7},{10,... | collective-permute-start | bytes 1572872 | tf_op jit(solution)/shard_map/ppermute | solution.py:364
  82.5 6.6 %collective-permute-done.8 = bf16[2,256,512]{2,1,0:T(8,128)(2,1)S(1)} collective-permute-done((bf16[2,256,512]{2,1,0:T(8,128)(2,1)S(1)}, bf16[2,256,512]{2,1,0:T(8,128)(2,1)S(1)}, u32[]{:S(2)}, u32[]{:S(2)}) %collective-permute-start.8) | collective-permute-done | bytes 524320 | tf_op jit(solution)/shard_map/ppermute | solution.py:364
  89.2 1.9 %collective-permute-start.9 = (bf16[2,256,512]{2,1,0:T(8,128)(2,1)S(1)}, bf16[2,256,512]{2,1,0:T(8,128)(2,1)S(1)}, u32[]{:S(2)}, u32[]{:S(2)}) collective-permute-start(bf16[2,256,512]{2,1,0:T(8,128)(2,1)S(1)} %add_convert_fusion), channel_id=1, source_target_pairs={{0,14},{1,3},{2,4},{3,1},{4,2},{5,7},{6,8},{7,5},{8,6},{9,11},{10,... | collective-permute-start | bytes 1572872 | tf_op jit(solution)/shard_map/ppermute | solution.py:365
  91.1 1.9 %collective-permute-start.11 = (f32[8,128]{1,0:T(8,128)S(1)}, f32[8,128]{1,0:T(8,128)S(1)}, u32[]{:S(2)}, u32[]{:S(2)}) collective-permute-start(f32[8,128]{1,0:T(8,128)S(1)} %get-tuple-element.24), channel_id=1, source_target_pairs={{0,256},{1,513},{2,258},{3,515},{4,260},{5,517},{6,262},{7,519},{8... | collective-permute-start | bytes 12296 | tf_op jit(solution)/shard_map/ppermute | solution.py:362
  93.1 2.4 %collective-permute-done.11 = f32[8,128]{1,0:T(8,128)S(1)} collective-permute-done((f32[8,128]{1,0:T(8,128)S(1)}, f32[8,128]{1,0:T(8,128)S(1)}, u32[]{:S(2)}, u32[]{:S(2)}) %collective-permute-start.11) | collective-permute-done | bytes 4128 | tf_op jit(solution)/shard_map/ppermute | solution.py:362
  95.5 9.3 %collective-permute-start.12 = (f32[8,128]{1,0:T(8,128)S(1)}, f32[8,128]{1,0:T(8,128)S(1)}, u32[]{:S(2)}, u32[]{:S(2)}) collective-permute-start(f32[8,128]{1,0:T(8,128)S(1)} %collective-permute-done.11), channel_id=1, source_target_pairs={{0,1},{1,0},{2,3},{3,2},{4,5},{5,4},{6,7},{7,6},{8,9},{9,8},{10,11... | collective-permute-start | bytes 12296 | tf_op jit(solution)/shard_map/ppermute | solution.py:363
  104.8 1.9 %collective-permute-start.10 = (bf16[256,512]{1,0:T(8,128)(2,1)S(1)}, bf16[256,512]{1,0:T(8,128)(2,1)S(1)}, u32[]{:S(2)}, u32[]{:S(2)}) collective-permute-start(bf16[256,512]{1,0:T(8,128)(2,1)S(1)} %fusion.2), channel_id=1, source_target_pairs={{0,2},{1,15},{2,0},{3,5},{4,6},{5,3},{6,4},{7,9},{8,10},{9,7},{10,... | collective-permute-start | bytes 786440 | tf_op jit(solution)/shard_map/ppermute | solution.py:366
  107.9 5.2 %collective-permute-done.10 = bf16[256,512]{1,0:T(8,128)(2,1)S(1)} collective-permute-done((bf16[256,512]{1,0:T(8,128)(2,1)S(1)}, bf16[256,512]{1,0:T(8,128)(2,1)S(1)}, u32[]{:S(2)}, u32[]{:S(2)}) %collective-permute-start.10) | collective-permute-done | bytes 262176 | tf_op jit(solution)/shard_map/ppermute | solution.py:366
  (28 shorter events, 6.9 us)
Async XLA Ops:
  0.0 65.4 %copy-start = (bf16[512,8192]{1,0:T(8,128)(2,1)S(1)}, bf16[512,8192]{1,0:T(8,128)(2,1)}, u32[]{:S(2)}) copy-start(bf16[512,8192]{1,0:T(8,128)(2,1)} %w_ref.5) | copy-start | bytes 25165828
  2.4 40.1 %copy-start.1 = (bf16[1,256,512]{2,1,0:T(8,128)(2,1)S(1)}, bf16[1,256,512]{2,1,0:T(8,128)(2,1)}, u32[]{:S(2)}) copy-start(bf16[1,256,512]{2,1,0:T(8,128)(2,1)} %param.7) | copy-start | bytes 786436
  2.4 51.9 %copy-start.2 = (s32[1,4096]{1,0:T(1,128)S(1)}, s32[1,4096]{1,0:T(1,128)}, u32[]{:S(2)}) copy-start(s32[1,4096]{1,0:T(1,128)} %param.11) | copy-start | bytes 49156
  2.4 51.9 %copy-start.3 = (s32[32]{0:T(128)S(1)}, s32[32]{0:T(128)}, u32[]{:S(2)}) copy-start(s32[32]{0:T(128)} %spans.3) | copy-start | bytes 388
  2.4 62.9 %collective-permute-start.6 = (bf16[8,512,512]{2,1,0:T(8,128)(2,1)S(1)}, bf16[8,512,512]{2,1,0:T(8,128)(2,1)S(1)}, u32[]{:S(2)}, u32[]{:S(2)}) collective-permute-start(bf16[8,512,512]{2,1,0:T(8,128)(2,1)S(1)} %pack.1), channel_id=1, source_target_pairs={{0,1},{1,0},{2,3},{3,2},{4,5},{5,4},{6,7},{7,6},{8,9},{9,8},{10,11... | collective-permute-start | bytes 12582920 | tf_op jit(solution)/shard_map/ppermute | solution.py:351
  15.9 8.1 %collective-permute-start = (bf16[136,256]{1,0:T(8,128)(2,1)S(1)}, bf16[136,256]{1,0:T(8,128)(2,1)S(1)}, u32[]{:S(2)}, u32[]{:S(2)}) collective-permute-start(bf16[136,256]{1,0:T(8,128)(2,1)S(1)} %prepare.1), channel_id=1, source_target_pairs={{0,16},{1,49},{2,18},{3,51},{4,20},{5,53},{6,22},{7,55},{8,24},{9,... | collective-permute-start | bytes 208904 | tf_op jit(solution)/shard_map/ppermute | solution.py:346
  24.0 8.0 %collective-permute-start.1 = (bf16[272,256]{1,0:T(8,128)(2,1)S(1)}, bf16[272,256]{1,0:T(8,128)(2,1)S(1)}, u32[]{:S(2)}, u32[]{:S(2)}) collective-permute-start(bf16[272,256]{1,0:T(8,128)(2,1)S(1)} %pad_maximum_fusion.2), channel_id=1, source_target_pairs={{0,48},{1,17},{2,50},{3,19},{4,52},{5,21},{6,54},{7,23},{8,56},{9,... | collective-permute-start | bytes 417800 | tf_op jit(solution)/shard_map/ppermute | solution.py:350
  32.0 8.5 %collective-permute-start.2 = (bf16[544,256]{1,0:T(8,128)(2,1)S(1)}, bf16[544,256]{1,0:T(8,128)(2,1)S(1)}, u32[]{:S(2)}, u32[]{:S(2)}) collective-permute-start(bf16[544,256]{1,0:T(8,128)(2,1)S(1)} %pad_maximum_fusion.1), channel_id=1, source_target_pairs={{0,64},{1,193},{2,66},{3,195},{4,68},{5,197},{6,70},{7,199},{8,72}... | collective-permute-start | bytes 835592 | tf_op jit(solution)/shard_map/ppermute | solution.py:352
  40.6 16.8 %collective-permute-start.3 = (bf16[1088,256]{1,0:T(8,128)(2,1)S(1)}, bf16[1088,256]{1,0:T(8,128)(2,1)S(1)}, u32[]{:S(2)}, u32[]{:S(2)}) collective-permute-start(bf16[1088,256]{1,0:T(8,128)(2,1)S(1)} %pad_maximum_fusion.blocks_ref), channel_id=1, source_target_pairs={{0,192},{1,65},{2,194},{3,67},{4,196},{5,69},{6,198},{7,71},{8,200... | collective-permute-start | bytes 1671176 | tf_op jit(solution)/shard_map/ppermute | solution.py:353
  42.5 11.8 %collective-permute-start.4 = (bf16[256,512]{1,0:T(8,128)(2,1)S(1)}, bf16[256,512]{1,0:T(8,128)(2,1)S(1)}, u32[]{:S(2)}, u32[]{:S(2)}) collective-permute-start(bf16[256,512]{1,0:T(8,128)(2,1)S(1)} %bitcast.16), channel_id=1, source_target_pairs={{0,1},{1,0},{2,3},{3,2},{4,5},{5,4},{6,7},{7,6},{8,9},{9,8},{10,11... | collective-permute-start | bytes 786440 | tf_op jit(solution)/shard_map/ppermute | solution.py:347
  60.6 4.8 %collective-permute-start.5 = (bf16[136,2048]{1,0:T(8,128)(2,1)S(1)}, bf16[136,2048]{1,0:T(8,128)(2,1)S(1)}, u32[]{:S(2)}, u32[]{:S(2)}) collective-permute-start(bf16[136,2048]{1,0:T(8,128)(2,1)S(1)} %get-tuple-element.21.mine_ref), channel_id=1, source_target_pairs={{0,1},{1,0},{2,3},{3,2},{4,5},{5,4},{6,7},{7,6},{8,9},{9,8},{10,11... | collective-permute-start | bytes 1671176 | tf_op jit(solution)/shard_map/ppermute | solution.py:355
  66.4 10.7 %collective-permute-start.7 = (bf16[2,256,512]{2,1,0:T(8,128)(2,1)S(1)}, bf16[2,256,512]{2,1,0:T(8,128)(2,1)S(1)}, u32[]{:S(2)}, u32[]{:S(2)}) collective-permute-start(bf16[2,256,512]{2,1,0:T(8,128)(2,1)S(1)} %get-tuple-element.23), channel_id=1, source_target_pairs={{0,14},{1,3},{2,4},{3,1},{4,2},{5,7},{6,8},{7,5},{8,6},{9,11},{10,... | collective-permute-start | bytes 1572872 | tf_op jit(solution)/shard_map/ppermute | solution.py:359
  77.2 30.1 %copy-start.4 = (s32[1,256]{1,0:T(1,128)S(1)}, s32[1,256]{1,0:T(1,128)}, u32[]{:S(2)}) copy-start(s32[1,256]{1,0:T(1,128)} %mask_hbm.1) | copy-start | bytes 3076
  77.2 11.8 %collective-permute-start.8 = (bf16[2,256,512]{2,1,0:T(8,128)(2,1)S(1)}, bf16[2,256,512]{2,1,0:T(8,128)(2,1)S(1)}, u32[]{:S(2)}, u32[]{:S(2)}) collective-permute-start(bf16[2,256,512]{2,1,0:T(8,128)(2,1)S(1)} %add_convert_fusion.1), channel_id=1, source_target_pairs={{0,2},{1,15},{2,0},{3,5},{4,6},{5,3},{6,4},{7,9},{8,10},{9,7},{10,... | collective-permute-start | bytes 1572872 | tf_op jit(solution)/shard_map/ppermute | solution.py:364
  89.2 15.5 %collective-permute-start.9 = (bf16[2,256,512]{2,1,0:T(8,128)(2,1)S(1)}, bf16[2,256,512]{2,1,0:T(8,128)(2,1)S(1)}, u32[]{:S(2)}, u32[]{:S(2)}) collective-permute-start(bf16[2,256,512]{2,1,0:T(8,128)(2,1)S(1)} %add_convert_fusion), channel_id=1, source_target_pairs={{0,14},{1,3},{2,4},{3,1},{4,2},{5,7},{6,8},{7,5},{8,6},{9,11},{10,... | collective-permute-start | bytes 1572872 | tf_op jit(solution)/shard_map/ppermute | solution.py:365
  91.1 4.4 %collective-permute-start.11 = (f32[8,128]{1,0:T(8,128)S(1)}, f32[8,128]{1,0:T(8,128)S(1)}, u32[]{:S(2)}, u32[]{:S(2)}) collective-permute-start(f32[8,128]{1,0:T(8,128)S(1)} %get-tuple-element.24), channel_id=1, source_target_pairs={{0,256},{1,513},{2,258},{3,515},{4,260},{5,517},{6,262},{7,519},{8... | collective-permute-start | bytes 12296 | tf_op jit(solution)/shard_map/ppermute | solution.py:362
  95.5 11.3 %collective-permute-start.12 = (f32[8,128]{1,0:T(8,128)S(1)}, f32[8,128]{1,0:T(8,128)S(1)}, u32[]{:S(2)}, u32[]{:S(2)}) collective-permute-start(f32[8,128]{1,0:T(8,128)S(1)} %collective-permute-done.11), channel_id=1, source_target_pairs={{0,1},{1,0},{2,3},{3,2},{4,5},{5,4},{6,7},{7,6},{8,9},{9,8},{10,11... | collective-permute-start | bytes 12296 | tf_op jit(solution)/shard_map/ppermute | solution.py:363
  104.8 8.3 %collective-permute-start.10 = (bf16[256,512]{1,0:T(8,128)(2,1)S(1)}, bf16[256,512]{1,0:T(8,128)(2,1)S(1)}, u32[]{:S(2)}, u32[]{:S(2)}) collective-permute-start(bf16[256,512]{1,0:T(8,128)(2,1)S(1)} %fusion.2), channel_id=1, source_target_pairs={{0,2},{1,15},{2,0},{3,5},{4,6},{5,3},{6,4},{7,9},{8,10},{9,7},{10,... | collective-permute-start | bytes 786440 | tf_op jit(solution)/shard_map/ppermute | solution.py:366

commit v5 on v4

--- a/solution.py
+++ b/solution.py
@@ -130,28 +130,30 @@
     )(w)
 
 
-def attend(first_block, spans, blocks_ref, q8, lo_ref, m_ref, l_ref, acc, k_pair, v_pair, places, items):
+def attend(first_block, spans, blocks_refs, q8, lo_ref, m_ref, l_ref, acc, k_pair, v_pair, places, items):
     f32 = jnp.float32
     context = lax.axis_index("context")
     core = lax.rem(lax.axis_index("tensor"), NC)
     width = q8.shape[1]
-    for b in range(8):
-        k_pair[b] = blocks_ref[b * BLOCK : b * BLOCK + SPAN, :HD]
-        v_pair[b] = blocks_ref[b * BLOCK : b * BLOCK + SPAN, HD:]
+    blocks = len(blocks_refs) * NZ
+    for b in range(blocks):
+        ref, at = blocks_refs[b // NZ], b % NZ * BLOCK
+        k_pair[b] = ref[at : at + SPAN, :HD]
+        v_pair[b] = ref[at : at + SPAN, HD:]
         places[b] = spans[gathered_slot(context, core, first_block + b)]
-    places[8] = 1 << 20
-    k_pair[8] = jnp.zeros((SPAN, HD), jnp.bfloat16)
-    v_pair[8] = jnp.zeros((SPAN, HD), jnp.bfloat16)
+    places[blocks] = 1 << 20
+    k_pair[blocks] = jnp.zeros((SPAN, HD), jnp.bfloat16)
+    v_pair[blocks] = jnp.zeros((SPAN, HD), jnp.bfloat16)
 
     for i in range(2):
         first = jnp.min(lo_ref[i]).astype(jnp.int32)
         q_pos = spans[2 * context + i]
         count = jnp.int32(0)
-        for b in range(8):
+        for b in range(blocks):
             items[count] = b
             seen = (places[b] <= q_pos) & ((places[b] + 1) * SPAN > first)
             count = count + seen.astype(jnp.int32)
-        items[count] = 8
+        items[count] = blocks
         hi = lax.broadcasted_iota(jnp.int32, (SPAN, SPAN), 1) + q_pos * SPAN
         row = lax.broadcasted_iota(jnp.int32, (SPAN, SPAN), 0)
 
@@ -180,8 +182,9 @@
 
         lax.fori_loop(0, lax.shift_right_logical(count + 1, 1), step, 0)
     tally = jnp.zeros((TALLY, HD), f32)
-    for b in range(8):
-        tally += blocks_ref[b * BLOCK + SPAN : (b + 1) * BLOCK, :HD].astype(f32)
+    for ref in blocks_refs:
+        for b in range(NZ):
+            tally += ref[b * BLOCK + SPAN : (b + 1) * BLOCK, :HD].astype(f32)
     return tally
 
 
@@ -206,10 +209,20 @@
     m_ref[...] = jnp.full(m_ref.shape, LOW, f32)
     l_ref[...] = jnp.zeros(l_ref.shape, f32)
     acc[...] = jnp.zeros(acc.shape, f32)
-    tally_ref[...] = attend(0, spans, blocks_ref, q8, lo_ref, m_ref, l_ref, acc, k_pair, v_pair, places, items)
+    tally_ref[...] = attend(0, spans, (blocks_ref,), q8, lo_ref, m_ref, l_ref, acc, k_pair, v_pair, places, items)
 
 
 def second_kernel(
+    spans, a_ref, b_ref, q8, lo_ref, m_in, l_in, acc_in, tally_in, m_ref, l_ref, acc, tally_ref, k_pair, v_pair, places, items
+):
+    m_ref[...] = m_in[...]
+    l_ref[...] = l_in[...]
+    acc[...] = acc_in[...]
+    tally = attend(NZ, spans, (a_ref, b_ref), q8, lo_ref, m_ref, l_ref, acc, k_pair, v_pair, places, items)
+    tally_ref[...] = tally_in[...] + tally
+
+
+def third_kernel(
     spans, blocks_ref, q8, lo_ref, m_in, l_in, acc_in, tally_in, out_ref, tally_ref, m_ref, l_ref, acc, k_pair, v_pair, places, items
 ):
     f32 = jnp.float32
@@ -217,7 +230,7 @@
     m_ref[...] = m_in[...]
     l_ref[...] = l_in[...]
     acc[...] = acc_in[...]
-    tally = attend(8, spans, blocks_ref, q8, lo_ref, m_ref, l_ref, acc, k_pair, v_pair, places, items)
+    tally = attend(3 * NZ, spans, (blocks_ref,), q8, lo_ref, m_ref, l_ref, acc, k_pair, v_pair, places, items)
     tally_ref[...] = tally_in[...] + tally
     row = lax.broadcasted_iota(jnp.int32, (TALLY, width), 0)
     for i in range(2):
@@ -233,39 +246,34 @@
         out_ref[SPAN:, cols] = parts.astype(jnp.bfloat16)
 
 
-def attention(spans, seg, q, q_other, blocks, more_blocks):
+def attention(spans, seg, q, q_other, own, inner_blocks, outer_blocks, far_blocks):
     heads = 2 * q.shape[1] // HD
     width = heads * SPAN
     f32 = jnp.float32
     state = [((2, 1, width), f32), ((2, 1, width), f32), ((2, HD, width), f32)]
-    made = [((2, width, HD), jnp.bfloat16), ((2, 1, SPAN), f32), *state, ((TALLY, HD), f32)]
-    scratch = [
-        pltpu.VMEM((9, SPAN, HD), jnp.bfloat16),
-        pltpu.VMEM((9, SPAN, HD), jnp.bfloat16),
-        pltpu.SMEM((9,), jnp.int32),
-        pltpu.SMEM((10,), jnp.int32),
-    ]
-    made = pl.pallas_call(
-        first_kernel,
-        out_shape=tuple(jax.ShapeDtypeStruct(*m) for m in made),
-        in_specs=[SMEM] + [VMEM] * 4,
-        out_specs=(VMEM,) * 6,
-        scratch_shapes=scratch,
-        compiler_params=grant(12),
-        name="attend_first",
-    )(spans, seg, q, q_other, blocks)
-    return pl.pallas_call(
-        second_kernel,
-        out_shape=(
-            jax.ShapeDtypeStruct((BLOCK, 2 * width), jnp.bfloat16),
-            jax.ShapeDtypeStruct((TALLY, HD), f32),
-        ),
-        in_specs=[SMEM] + [VMEM] * 7,
-        out_specs=(VMEM, VMEM),
-        scratch_shapes=[pltpu.VMEM(*m) for m in state] + scratch,
-        compiler_params=grant(12),
-        name="attend_second",
-    )(spans, more_blocks, *made)
+    tally = ((TALLY, HD), f32)
+
+    def call(kernel, blocks, made, kept, *operands):
+        return pl.pallas_call(
+            kernel,
+            out_shape=tuple(jax.ShapeDtypeStruct(*m) for m in made),
+            in_specs=[SMEM] + [VMEM] * (len(operands) - 1),
+            out_specs=(VMEM,) * len(made),
+            scratch_shapes=[pltpu.VMEM(*m) for m in kept]
+            + [
+                pltpu.VMEM((blocks + 1, SPAN, HD), jnp.bfloat16),
+                pltpu.VMEM((blocks + 1, SPAN, HD), jnp.bfloat16),
+                pltpu.SMEM((blocks + 1,), jnp.int32),
+                pltpu.SMEM((blocks + 2,), jnp.int32),
+            ],
+            compiler_params=grant(12),
+        )(*operands)
+
+    made = [((2, width, HD), jnp.bfloat16), ((2, 1, SPAN), f32), *state, tally]
+    q8, lo, *running = call(first_kernel, NZ, made, [], spans, seg, q, q_other, own)
+    running = call(second_kernel, 2 * NZ, [*state, tally], [], spans, inner_blocks, outer_blocks, q8, lo, *running)
+    made = [((BLOCK, 2 * width), jnp.bfloat16), tally]
+    return call(third_kernel, NZ, made, state, spans, far_blocks, q8, lo, *running)
 
 
 def multiply(first, heads_ref, w_ref, other_ref, out_ref):
@@ -349,9 +357,13 @@
     kv2 = cat(kv1, r1)
     kv4 = cat(kv2, lax.ppermute(kv2, both, perm_context("z", outer)))
     weight_other = lax.ppermute(packed, "tensor", SWAP)
-    kv8 = cat(kv4, lax.ppermute(kv4, both, perm_context("x", inner)))
-    r8 = lax.ppermute(kv8, both, perm_context("x", outer))
-    mine, tally = attention(span_order, segment_ids.reshape(32, SPAN), queries[0], q_other, kv8, r8)
+    beyond = lambda i, c, n: inner(outer(i, c, n), c, n)
+    gathered = [
+        lax.ppermute(kv4, both, perm_context("x", inner)),
+        lax.ppermute(kv4, both, perm_context("x", outer)),
+        lax.ppermute(kv4, both, perm_context("x", beyond)),
+    ]
+    mine, tally = attention(span_order, segment_ids.reshape(32, SPAN), queries[0], q_other, kv4, *gathered)
     theirs = lax.ppermute(mine, "tensor", SWAP)
 
     inward, outward = perm_tensor(inner), perm_tensor(outer)
@@ -359,15 +371,17 @@
     far = lax.ppermute(far, "tensor", outward)
     rest = project(heads, out_weight, weight_other)
     around = [(d * 16 + t, (d + 1 + t % 2) % 3 * 16 + t) for d in range(3) for t in range(16)]
+    early = lax.ppermute(rest[4], "tensor", inward)
     one = lax.ppermute(tally, ("dp", "tensor"), around)
     two = lax.ppermute(one, "tensor", SWAP)
     mid = lax.ppermute(add(rest[0:2], far), "tensor", inward)
-    near = lax.ppermute(add(rest[2:4], mid), "tensor", outward)
-    last = lax.ppermute(add(rest[4], near[0]), "tensor", inward)
+    near = add(rest[2:4], mid)
+    passing = lax.ppermute(near[0], "tensor", perm_tensor(beyond))
+    near = lax.ppermute(near[1], "tensor", outward)
     count = (tally + one + two)[0, 0]
     scale_all = lax.axis_size("dp") * lax.axis_size("context") * queries.shape[1]
     weight = loss_mask[0].astype(f32) * scale_all / count
-    summed = rest[5].astype(f32) + near[1].astype(f32) + last.astype(f32)
+    summed = rest[5].astype(f32) + early.astype(f32) + near.astype(f32) + passing.astype(f32)
     return (summed * weight[:, None]).astype(jnp.bfloat16)[None]
 
 

time: 114 us -> 108 us (0.947)
  waiting for transfers between devices: 36.2 us -> 25.4 us
  starting transfers between devices: 62.8 us -> 65.7 us
    ppermute x4 -> x6, starting transfers between devices: 8.82 us -> 20.5 us  [the longest x1 4.89 us: per_device(): early = lax.ppermute(rest[4], 'tensor', inward)]
    ppermute x1, waiting for transfers between devices: 6.56 us -> 0.01 us  [per_device(): mid = lax.ppermute(add(rest[0:2], far), 'tensor', inward)]
    ppermute x1, starting transfers between devices: 9.25 us -> 3.26 us  [per_device(): two = lax.ppermute(one, 'tensor', SWAP)]
    ppermute x4 -> x6, waiting for transfers between devices: 10.6 us -> 5.9 us  [the longest x1 5.89 us: per_device(): passing = lax.ppermute(near[0], 'tensor', perm_tensor(beyond))]
    ppermute x1, starting transfers between devices: 10.6 us -> 8.26 us  [per_device(): q_other = lax.ppermute(queries[0], 'tensor', SWAP)]
    pallas_call x2 -> x3, Pallas kernels: 6.27 us -> 7.12 us  [call(): pl.pallas_call(kernel, out_shape=tuple((jax.ShapeDtypeStruct(*m) for m in...]
  transfers between devices with their start and end apart: 13 -> 15, of which waited for: 9 -> 7; matrix products, arithmetic and copies ran while one was open for 1% -> 1% of each run, Pallas kernels for 8% -> 9%
where the time goes in v5:
time: 108 us; the launch traced here: 107 us
  starting transfers between devices  65.7 us (61%)
  waiting for transfers between devices  25.4 us (24%)
  Pallas kernels  13.1 us (12%)
  other arithmetic  1.82 us (2%)
    ppermute x1, starting transfers between devices, per_device(): weight_other = lax.ppermute(packed, 'tensor', SWAP)  12.6 us
    ppermute x1, starting transfers between devices, per_device(): q_other = lax.ppermute(queries[0], 'tensor', SWAP)  8.26 us
    pallas_call x3, Pallas kernels, call(): pl.pallas_call(kernel, out_shape=tuple((jax.ShapeDtypeStruct(*m) for m in...  7.12 us
    ppermute x1, waiting for transfers between devices, per_device(): kv4 = cat(kv2, lax.ppermute(kv2, both, perm_context('z', outer)))  6.1 us
    ppermute x1, waiting for transfers between devices, per_device(): passing = lax.ppermute(near[0], 'tensor', perm_tensor(beyond))  5.89 us
    ppermute x1, starting transfers between devices, per_device(): r1 = lax.ppermute(kv1, both, perm_context('z', inner))  5.3 us
    ppermute x1, waiting for transfers between devices, per_device(): far = lax.ppermute(far, 'tensor', outward)  5.2 us
    ppermute x1, starting transfers between devices, per_device(): mid = lax.ppermute(add(rest[0:2], far), 'tensor', inward)  5.09 us
  transfers between devices with their start and end apart: 15, of which 7 were waited for; matrix products, arithmetic and copies ran while one was open for 1% of the time, Pallas kernels for 9%

profile of v5, /device:TPU:1, one launch (start us, length us, event | category | flops | bytes accessed | tf_op | source)
XLA Modules:
  0.0 107.0 jit_solution(6993280468135688849)
XLA Ops:
  0.0 2.4 %pack.1 = bf16[8,512,512]{2,1,0:T(8,128)(2,1)S(1)} custom-call(bf16[512,8192]{1,0:T(8,128)(2,1)} %w_ref.5), custom_call_target="tpu_custom_call" | custom-call | tf_op jit(solution)/shard_map/pack/pallas_call | solution.py:122
  2.4 12.6 %collective-permute-start.7 = (bf16[8,512,512]{2,1,0:T(8,128)(2,1)S(1)}, bf16[8,512,512]{2,1,0:T(8,128)(2,1)S(1)}, u32[]{:S(2)}, u32[]{:S(2)}) collective-permute-start(bf16[8,512,512]{2,1,0:T(8,128)(2,1)S(1)} %pack.1), channel_id=1, source_target_pairs={{0,1},{1,0},{2,3},{3,2},{4,5},{5,4},{6,7},{7,6},{8,9},{9,8},{10,11... | collective-permute-start | bytes 12582920 | tf_op jit(solution)/shard_map/ppermute | solution.py:359
  15.9 5.3 %collective-permute-start = (bf16[136,256]{1,0:T(8,128)(2,1)S(1)}, bf16[136,256]{1,0:T(8,128)(2,1)S(1)}, u32[]{:S(2)}, u32[]{:S(2)}) collective-permute-start(bf16[136,256]{1,0:T(8,128)(2,1)S(1)} %prepare.1), channel_id=1, source_target_pairs={{0,16},{1,49},{2,18},{3,51},{4,20},{5,53},{6,22},{7,55},{8,24},{9,... | collective-permute-start | bytes 208904 | tf_op jit(solution)/shard_map/ppermute | solution.py:354
  21.2 2.8 %collective-permute-done = bf16[136,256]{1,0:T(8,128)(2,1)S(1)} collective-permute-done((bf16[136,256]{1,0:T(8,128)(2,1)S(1)}, bf16[136,256]{1,0:T(8,128)(2,1)S(1)}, u32[]{:S(2)}, u32[]{:S(2)}) %collective-permute-start) | collective-permute-done | bytes 69664 | tf_op jit(solution)/shard_map/ppermute | solution.py:354
  24.0 1.9 %collective-permute-start.1 = (bf16[272,256]{1,0:T(8,128)(2,1)S(1)}, bf16[272,256]{1,0:T(8,128)(2,1)S(1)}, u32[]{:S(2)}, u32[]{:S(2)}) collective-permute-start(bf16[272,256]{1,0:T(8,128)(2,1)S(1)} %pad_maximum_fusion.1), channel_id=1, source_target_pairs={{0,48},{1,17},{2,50},{3,19},{4,52},{5,21},{6,54},{7,23},{8,56},{9,... | collective-permute-start | bytes 417800 | tf_op jit(solution)/shard_map/ppermute | solution.py:358
  25.9 6.1 %collective-permute-done.1 = bf16[272,256]{1,0:T(8,128)(2,1)S(1)} collective-permute-done((bf16[272,256]{1,0:T(8,128)(2,1)S(1)}, bf16[272,256]{1,0:T(8,128)(2,1)S(1)}, u32[]{:S(2)}, u32[]{:S(2)}) %collective-permute-start.1) | collective-permute-done | bytes 139296 | tf_op jit(solution)/shard_map/ppermute | solution.py:358
  32.0 1.9 %collective-permute-start.5 = (bf16[544,256]{1,0:T(8,128)(2,1)S(1)}, bf16[544,256]{1,0:T(8,128)(2,1)S(1)}, u32[]{:S(2)}, u32[]{:S(2)}) collective-permute-start(bf16[544,256]{1,0:T(8,128)(2,1)S(1)} %pad_maximum_fusion.blocks_ref), channel_id=1, source_target_pairs={{0,192},{1,65},{2,194},{3,67},{4,196},{5,69},{6,198},{7,71},{8,200... | collective-permute-start | bytes 835592 | tf_op jit(solution)/shard_map/ppermute | solution.py:363
  34.0 3.6 %collective-permute-start.4 = (bf16[544,256]{1,0:T(8,128)(2,1)S(1)}, bf16[544,256]{1,0:T(8,128)(2,1)S(1)}, u32[]{:S(2)}, u32[]{:S(2)}) collective-permute-start(bf16[544,256]{1,0:T(8,128)(2,1)S(1)} %pad_maximum_fusion.blocks_ref), channel_id=1, source_target_pairs={{0,64},{1,193},{2,66},{3,195},{4,68},{5,197},{6,70},{7,199},{8,72}... | collective-permute-start | bytes 835592 | tf_op jit(solution)/shard_map/ppermute | solution.py:362
  37.6 3.5 %collective-permute-start.2 = (bf16[544,256]{1,0:T(8,128)(2,1)S(1)}, bf16[544,256]{1,0:T(8,128)(2,1)S(1)}, u32[]{:S(2)}, u32[]{:S(2)}) collective-permute-start(bf16[544,256]{1,0:T(8,128)(2,1)S(1)} %pad_maximum_fusion.blocks_ref), channel_id=1, source_target_pairs={{0,128},{1,129},{2,130},{3,131},{4,132},{5,133},{6,134},{7,135},{8... | collective-permute-start | bytes 835592 | tf_op jit(solution)/shard_map/ppermute | solution.py:364
  41.1 8.3 %collective-permute-start.3 = (bf16[256,512]{1,0:T(8,128)(2,1)S(1)}, bf16[256,512]{1,0:T(8,128)(2,1)S(1)}, u32[]{:S(2)}, u32[]{:S(2)}) collective-permute-start(bf16[256,512]{1,0:T(8,128)(2,1)S(1)} %bitcast.17), channel_id=1, source_target_pairs={{0,1},{1,0},{2,3},{3,2},{4,5},{5,4},{6,7},{7,6},{8,9},{9,8},{10,11... | collective-permute-start | bytes 786440 | tf_op jit(solution)/shard_map/ppermute | solution.py:355
  50.5 2.3 %shard_map.73 = (bf16[2,1024,128]{2,1,0:T(8,128)(2,1)S(1)}, f32[2,1,128]{2,1,0:T(1,128)S(1)}, f32[2,1,1024]{2,1,0:T(1,128)S(1)}, f32[2,1,1024]{2,1,0:T(1,128)S(1...) custom-call(s32[32]{0:T(128)S(1)} %copy-done.3, s32[32,128]{1,0:T(8,128)S(1)} %bitcast.19, ...), custom_call_target="tpu_custom_call" | custom-call | tf_op jit(solution)/shard_map/pallas_call | solution.py:257
  52.8 3.1 %shard_map.74 = (f32[2,1,1024]{2,1,0:T(1,128)S(1)}, f32[2,1,1024]{2,1,0:T(1,128)S(1)}, f32[2,128,1024]{2,1,0:T(8,128)S(1)}, f32[8,128]{1,0:T(8,128)S(1)}) custom-call(s32[32]{0:T(128)S(1)} %copy-done.3, bf16[544,256]{1,0:T(8,128)(2,1)S(1)} %collective-permute-done.4.a_ref, bf16[544,256]{1,0:T(8,128)(2,1)S(1)} %collective-permute-done.5.b_ref, ...), custom_call_target="tpu_custom_call" | custom-call | tf_op jit(solution)/shard_map/pallas_call | solution.py:257
  57.6 3.7 %collective-permute-start.6 = (bf16[136,2048]{1,0:T(8,128)(2,1)S(1)}, bf16[136,2048]{1,0:T(8,128)(2,1)S(1)}, u32[]{:S(2)}, u32[]{:S(2)}) collective-permute-start(bf16[136,2048]{1,0:T(8,128)(2,1)S(1)} %get-tuple-element.29.mine_ref), channel_id=1, source_target_pairs={{0,1},{1,0},{2,3},{3,2},{4,5},{5,4},{6,7},{7,6},{8,9},{9,8},{10,11... | collective-permute-start | bytes 1671176 | tf_op jit(solution)/shard_map/ppermute | solution.py:367
  63.8 3.2 %collective-permute-start.9 = (bf16[2,256,512]{2,1,0:T(8,128)(2,1)S(1)}, bf16[2,256,512]{2,1,0:T(8,128)(2,1)S(1)}, u32[]{:S(2)}, u32[]{:S(2)}) collective-permute-start(bf16[2,256,512]{2,1,0:T(8,128)(2,1)S(1)} %get-tuple-element.31), channel_id=1, source_target_pairs={{0,14},{1,3},{2,4},{3,1},{4,2},{5,7},{6,8},{7,5},{8,6},{9,11},{10,... | collective-permute-start | bytes 1572872 | tf_op jit(solution)/shard_map/ppermute | solution.py:371
  67.1 1.8 %project.1 = bf16[6,256,512]{2,1,0:T(8,128)(2,1)S(1)} custom-call(bf16[256,1024]{1,0:T(8,128)(2,1)S(1)} %get-tuple-element.30.heads_ref, bf16[512,8192]{1,0:T(8,128)(2,1)S(1)} %copy-done, bf16[8,512,512]{2,1,0:T(8,128)(2,1)S(1)} %collective-permute-done.7.other_ref), custom_call_target="tpu_custom_call" | custom-call | tf_op jit(solution)/shard_map/project/pallas_call | solution.py:333
  68.9 5.2 %collective-permute-done.9 = bf16[2,256,512]{2,1,0:T(8,128)(2,1)S(1)} collective-permute-done((bf16[2,256,512]{2,1,0:T(8,128)(2,1)S(1)}, bf16[2,256,512]{2,1,0:T(8,128)(2,1)S(1)}, u32[]{:S(2)}, u32[]{:S(2)}) %collective-permute-start.9) | collective-permute-done | bytes 524320 | tf_op jit(solution)/shard_map/ppermute | solution.py:371
  74.2 5.1 %collective-permute-start.10 = (bf16[2,256,512]{2,1,0:T(8,128)(2,1)S(1)}, bf16[2,256,512]{2,1,0:T(8,128)(2,1)S(1)}, u32[]{:S(2)}, u32[]{:S(2)}) collective-permute-start(bf16[2,256,512]{2,1,0:T(8,128)(2,1)S(1)} %add_convert_fusion.1), channel_id=1, source_target_pairs={{0,2},{1,15},{2,0},{3,5},{4,6},{5,3},{6,4},{7,9},{8,10},{9,7},{10,... | collective-permute-start | bytes 1572872 | tf_op jit(solution)/shard_map/ppermute | solution.py:377
  79.3 1.9 %collective-permute-start.13 = (f32[8,128]{1,0:T(8,128)S(1)}, f32[8,128]{1,0:T(8,128)S(1)}, u32[]{:S(2)}, u32[]{:S(2)}) collective-permute-start(f32[8,128]{1,0:T(8,128)S(1)} %get-tuple-element.32), channel_id=1, source_target_pairs={{0,256},{1,513},{2,258},{3,515},{4,260},{5,517},{6,262},{7,519},{8... | collective-permute-start | bytes 12296 | tf_op jit(solution)/shard_map/ppermute | solution.py:375
  81.2 2.7 %collective-permute-done.13 = f32[8,128]{1,0:T(8,128)S(1)} collective-permute-done((f32[8,128]{1,0:T(8,128)S(1)}, f32[8,128]{1,0:T(8,128)S(1)}, u32[]{:S(2)}, u32[]{:S(2)}) %collective-permute-start.13) | collective-permute-done | bytes 4128 | tf_op jit(solution)/shard_map/ppermute | solution.py:375
  84.0 3.3 %collective-permute-start.14 = (f32[8,128]{1,0:T(8,128)S(1)}, f32[8,128]{1,0:T(8,128)S(1)}, u32[]{:S(2)}, u32[]{:S(2)}) collective-permute-start(f32[8,128]{1,0:T(8,128)S(1)} %collective-permute-done.13), channel_id=1, source_target_pairs={{0,1},{1,0},{2,3},{3,2},{4,5},{5,4},{6,7},{7,6},{8,9},{9,8},{10,11... | collective-permute-start | bytes 12296 | tf_op jit(solution)/shard_map/ppermute | solution.py:376
  87.3 4.9 %collective-permute-start.8 = (bf16[256,512]{1,0:T(8,128)(2,1)S(1)}, bf16[256,512]{1,0:T(8,128)(2,1)S(1)}, u32[]{:S(2)}, u32[]{:S(2)}) collective-permute-start(bf16[256,512]{1,0:T(8,128)(2,1)S(1)} %slice_bitcast_fusion.2), channel_id=1, source_target_pairs={{0,2},{1,15},{2,0},{3,5},{4,6},{5,3},{6,4},{7,9},{8,10},{9,7},{10,... | collective-permute-start | bytes 786440 | tf_op jit(solution)/shard_map/ppermute | solution.py:374
  92.4 2.8 %collective-permute-start.11 = (bf16[256,512]{1,0:T(8,128)(2,1)S(1)}, bf16[256,512]{1,0:T(8,128)(2,1)S(1)}, u32[]{:S(2)}, u32[]{:S(2)}) collective-permute-start(bf16[256,512]{1,0:T(8,128)(2,1)S(1)} %get-tuple-element.33), channel_id=1, source_target_pairs={{0,14},{1,3},{2,4},{3,1},{4,2},{5,7},{6,8},{7,5},{8,6},{9,11},{10,... | collective-permute-start | bytes 786440 | tf_op jit(solution)/shard_map/ppermute | solution.py:380
  95.1 3.8 %collective-permute-start.12 = (bf16[256,512]{1,0:T(8,128)(2,1)S(1)}, bf16[256,512]{1,0:T(8,128)(2,1)S(1)}, u32[]{:S(2)}, u32[]{:S(2)}) collective-permute-start(bf16[256,512]{1,0:T(8,128)(2,1)S(1)} %get-tuple-element.34), channel_id=1, source_target_pairs={{0,12},{1,5},{2,6},{3,15},{4,0},{5,9},{6,10},{7,3},{8,4},{9,13},{1... | collective-permute-start | bytes 786440 | tf_op jit(solution)/shard_map/ppermute | solution.py:379
  100.2 5.9 %collective-permute-done.12 = bf16[256,512]{1,0:T(8,128)(2,1)S(1)} collective-permute-done((bf16[256,512]{1,0:T(8,128)(2,1)S(1)}, bf16[256,512]{1,0:T(8,128)(2,1)S(1)}, u32[]{:S(2)}, u32[]{:S(2)}) %collective-permute-start.12) | collective-permute-done | bytes 262176 | tf_op jit(solution)/shard_map/ppermute | solution.py:379
  (33 shorter events, 8.6 us)
Async XLA Ops:
  0.0 62.9 %copy-start = (bf16[512,8192]{1,0:T(8,128)(2,1)S(1)}, bf16[512,8192]{1,0:T(8,128)(2,1)}, u32[]{:S(2)}) copy-start(bf16[512,8192]{1,0:T(8,128)(2,1)} %w_ref.5) | copy-start | bytes 25165828
  2.4 38.6 %copy-start.1 = (bf16[1,256,512]{2,1,0:T(8,128)(2,1)S(1)}, bf16[1,256,512]{2,1,0:T(8,128)(2,1)}, u32[]{:S(2)}) copy-start(bf16[1,256,512]{2,1,0:T(8,128)(2,1)} %param.7) | copy-start | bytes 786436
  2.4 48.1 %copy-start.2 = (s32[1,4096]{1,0:T(1,128)S(1)}, s32[1,4096]{1,0:T(1,128)}, u32[]{:S(2)}) copy-start(s32[1,4096]{1,0:T(1,128)} %param.11) | copy-start | bytes 49156
  2.4 48.0 %copy-start.3 = (s32[32]{0:T(128)S(1)}, s32[32]{0:T(128)}, u32[]{:S(2)}) copy-start(s32[32]{0:T(128)} %spans.5) | copy-start | bytes 388
  2.4 60.4 %collective-permute-start.7 = (bf16[8,512,512]{2,1,0:T(8,128)(2,1)S(1)}, bf16[8,512,512]{2,1,0:T(8,128)(2,1)S(1)}, u32[]{:S(2)}, u32[]{:S(2)}) collective-permute-start(bf16[8,512,512]{2,1,0:T(8,128)(2,1)S(1)} %pack.1), channel_id=1, source_target_pairs={{0,1},{1,0},{2,3},{3,2},{4,5},{5,4},{6,7},{7,6},{8,9},{9,8},{10,11... | collective-permute-start | bytes 12582920 | tf_op jit(solution)/shard_map/ppermute | solution.py:359
  15.9 8.1 %collective-permute-start = (bf16[136,256]{1,0:T(8,128)(2,1)S(1)}, bf16[136,256]{1,0:T(8,128)(2,1)S(1)}, u32[]{:S(2)}, u32[]{:S(2)}) collective-permute-start(bf16[136,256]{1,0:T(8,128)(2,1)S(1)} %prepare.1), channel_id=1, source_target_pairs={{0,16},{1,49},{2,18},{3,51},{4,20},{5,53},{6,22},{7,55},{8,24},{9,... | collective-permute-start | bytes 208904 | tf_op jit(solution)/shard_map/ppermute | solution.py:354
  24.0 8.0 %collective-permute-start.1 = (bf16[272,256]{1,0:T(8,128)(2,1)S(1)}, bf16[272,256]{1,0:T(8,128)(2,1)S(1)}, u32[]{:S(2)}, u32[]{:S(2)}) collective-permute-start(bf16[272,256]{1,0:T(8,128)(2,1)S(1)} %pad_maximum_fusion.1), channel_id=1, source_target_pairs={{0,48},{1,17},{2,50},{3,19},{4,52},{5,21},{6,54},{7,23},{8,56},{9,... | collective-permute-start | bytes 417800 | tf_op jit(solution)/shard_map/ppermute | solution.py:358
  32.0 20.8 %collective-permute-start.5 = (bf16[544,256]{1,0:T(8,128)(2,1)S(1)}, bf16[544,256]{1,0:T(8,128)(2,1)S(1)}, u32[]{:S(2)}, u32[]{:S(2)}) collective-permute-start(bf16[544,256]{1,0:T(8,128)(2,1)S(1)} %pad_maximum_fusion.blocks_ref), channel_id=1, source_target_pairs={{0,192},{1,65},{2,194},{3,67},{4,196},{5,69},{6,198},{7,71},{8,200... | collective-permute-start | bytes 835592 | tf_op jit(solution)/shard_map/ppermute | solution.py:363
  34.0 18.8 %collective-permute-start.4 = (bf16[544,256]{1,0:T(8,128)(2,1)S(1)}, bf16[544,256]{1,0:T(8,128)(2,1)S(1)}, u32[]{:S(2)}, u32[]{:S(2)}) collective-permute-start(bf16[544,256]{1,0:T(8,128)(2,1)S(1)} %pad_maximum_fusion.blocks_ref), channel_id=1, source_target_pairs={{0,64},{1,193},{2,66},{3,195},{4,68},{5,197},{6,70},{7,199},{8,72}... | collective-permute-start | bytes 835592 | tf_op jit(solution)/shard_map/ppermute | solution.py:362
  37.6 18.3 %collective-permute-start.2 = (bf16[544,256]{1,0:T(8,128)(2,1)S(1)}, bf16[544,256]{1,0:T(8,128)(2,1)S(1)}, u32[]{:S(2)}, u32[]{:S(2)}) collective-permute-start(bf16[544,256]{1,0:T(8,128)(2,1)S(1)} %pad_maximum_fusion.blocks_ref), channel_id=1, source_target_pairs={{0,128},{1,129},{2,130},{3,131},{4,132},{5,133},{6,134},{7,135},{8... | collective-permute-start | bytes 835592 | tf_op jit(solution)/shard_map/ppermute | solution.py:364
  41.1 9.4 %collective-permute-start.3 = (bf16[256,512]{1,0:T(8,128)(2,1)S(1)}, bf16[256,512]{1,0:T(8,128)(2,1)S(1)}, u32[]{:S(2)}, u32[]{:S(2)}) collective-permute-start(bf16[256,512]{1,0:T(8,128)(2,1)S(1)} %bitcast.17), channel_id=1, source_target_pairs={{0,1},{1,0},{2,3},{3,2},{4,5},{5,4},{6,7},{7,6},{8,9},{9,8},{10,11... | collective-permute-start | bytes 786440 | tf_op jit(solution)/shard_map/ppermute | solution.py:355
  57.6 5.2 %collective-permute-start.6 = (bf16[136,2048]{1,0:T(8,128)(2,1)S(1)}, bf16[136,2048]{1,0:T(8,128)(2,1)S(1)}, u32[]{:S(2)}, u32[]{:S(2)}) collective-permute-start(bf16[136,2048]{1,0:T(8,128)(2,1)S(1)} %get-tuple-element.29.mine_ref), channel_id=1, source_target_pairs={{0,1},{1,0},{2,3},{3,2},{4,5},{5,4},{6,7},{7,6},{8,9},{9,8},{10,11... | collective-permute-start | bytes 1671176 | tf_op jit(solution)/shard_map/ppermute | solution.py:367
  63.8 10.2 %collective-permute-start.9 = (bf16[2,256,512]{2,1,0:T(8,128)(2,1)S(1)}, bf16[2,256,512]{2,1,0:T(8,128)(2,1)S(1)}, u32[]{:S(2)}, u32[]{:S(2)}) collective-permute-start(bf16[2,256,512]{2,1,0:T(8,128)(2,1)S(1)} %get-tuple-element.31), channel_id=1, source_target_pairs={{0,14},{1,3},{2,4},{3,1},{4,2},{5,7},{6,8},{7,5},{8,6},{9,11},{10,... | collective-permute-start | bytes 1572872 | tf_op jit(solution)/shard_map/ppermute | solution.py:371
  74.2 18.0 %collective-permute-start.10 = (bf16[2,256,512]{2,1,0:T(8,128)(2,1)S(1)}, bf16[2,256,512]{2,1,0:T(8,128)(2,1)S(1)}, u32[]{:S(2)}, u32[]{:S(2)}) collective-permute-start(bf16[2,256,512]{2,1,0:T(8,128)(2,1)S(1)} %add_convert_fusion.1), channel_id=1, source_target_pairs={{0,2},{1,15},{2,0},{3,5},{4,6},{5,3},{6,4},{7,9},{8,10},{9,7},{10,... | collective-permute-start | bytes 1572872 | tf_op jit(solution)/shard_map/ppermute | solution.py:377
  79.3 20.2 %copy-start.4 = (s32[1,256]{1,0:T(1,128)S(1)}, s32[1,256]{1,0:T(1,128)}, u32[]{:S(2)}) copy-start(s32[1,256]{1,0:T(1,128)} %mask_hbm.1) | copy-start | bytes 3076
  79.3 4.6 %collective-permute-start.13 = (f32[8,128]{1,0:T(8,128)S(1)}, f32[8,128]{1,0:T(8,128)S(1)}, u32[]{:S(2)}, u32[]{:S(2)}) collective-permute-start(f32[8,128]{1,0:T(8,128)S(1)} %get-tuple-element.32), channel_id=1, source_target_pairs={{0,256},{1,513},{2,258},{3,515},{4,260},{5,517},{6,262},{7,519},{8... | collective-permute-start | bytes 12296 | tf_op jit(solution)/shard_map/ppermute | solution.py:375
  84.0 15.0 %collective-permute-start.14 = (f32[8,128]{1,0:T(8,128)S(1)}, f32[8,128]{1,0:T(8,128)S(1)}, u32[]{:S(2)}, u32[]{:S(2)}) collective-permute-start(f32[8,128]{1,0:T(8,128)S(1)} %collective-permute-done.13), channel_id=1, source_target_pairs={{0,1},{1,0},{2,3},{3,2},{4,5},{5,4},{6,7},{7,6},{8,9},{9,8},{10,11... | collective-permute-start | bytes 12296 | tf_op jit(solution)/shard_map/ppermute | solution.py:376
  87.3 12.9 %collective-permute-start.8 = (bf16[256,512]{1,0:T(8,128)(2,1)S(1)}, bf16[256,512]{1,0:T(8,128)(2,1)S(1)}, u32[]{:S(2)}, u32[]{:S(2)}) collective-permute-start(bf16[256,512]{1,0:T(8,128)(2,1)S(1)} %slice_bitcast_fusion.2), channel_id=1, source_target_pairs={{0,2},{1,15},{2,0},{3,5},{4,6},{5,3},{6,4},{7,9},{8,10},{9,7},{10,... | collective-permute-start | bytes 786440 | tf_op jit(solution)/shard_map/ppermute | solution.py:374
  92.4 7.8 %collective-permute-start.11 = (bf16[256,512]{1,0:T(8,128)(2,1)S(1)}, bf16[256,512]{1,0:T(8,128)(2,1)S(1)}, u32[]{:S(2)}, u32[]{:S(2)}) collective-permute-start(bf16[256,512]{1,0:T(8,128)(2,1)S(1)} %get-tuple-element.33), channel_id=1, source_target_pairs={{0,14},{1,3},{2,4},{3,1},{4,2},{5,7},{6,8},{7,5},{8,6},{9,11},{10,... | collective-permute-start | bytes 786440 | tf_op jit(solution)/shard_map/ppermute | solution.py:380
  95.1 11.0 %collective-permute-start.12 = (bf16[256,512]{1,0:T(8,128)(2,1)S(1)}, bf16[256,512]{1,0:T(8,128)(2,1)S(1)}, u32[]{:S(2)}, u32[]{:S(2)}) collective-permute-start(bf16[256,512]{1,0:T(8,128)(2,1)S(1)} %get-tuple-element.34), channel_id=1, source_target_pairs={{0,12},{1,5},{2,6},{3,15},{4,0},{5,9},{6,10},{7,3},{8,4},{9,13},{1... | collective-permute-start | bytes 786440 | tf_op jit(solution)/shard_map/ppermute | solution.py:379

commit v6 on v5

--- a/solution.py
+++ b/solution.py
@@ -276,17 +276,17 @@
     return call(third_kernel, NZ, made, state, spans, far_blocks, q8, lo, *running)
 
 
-def multiply(first, heads_ref, w_ref, other_ref, out_ref):
+def multiply(first, heads_ref, w_ref, other_ref, out_refs):
     depth = w_ref.shape[0]
     blocks = column_blocks(lax.axis_index("tensor"))
-    for g in range(out_ref.shape[0]):
+    for g, out_ref in enumerate(out_refs):
         at = pl.multiple_of(blocks[first + g] * COLS, COLS)
         total = jnp.dot(heads_ref[:, :depth], w_ref[:, pl.ds(at, COLS)], preferred_element_type=jnp.float32)
         total += jnp.dot(heads_ref[:, depth:], other_ref[first + g], preferred_element_type=jnp.float32)
-        out_ref[g] = total.astype(jnp.bfloat16)
-
-
-def join_kernel(mine_ref, theirs_ref, w_ref, other_ref, heads_ref, out_ref):
+        out_ref[...] = total.astype(jnp.bfloat16)
+
+
+def join_kernel(mine_ref, theirs_ref, w_ref, other_ref, heads_ref, *out_refs):
     f32 = jnp.float32
     width = mine_ref.shape[1] // 2
     heads = width // SPAN
@@ -306,7 +306,7 @@
             joined = mine_ref[:SPAN, a : a + SPAN].astype(f32) * (part_a / total)
             joined += theirs_ref[:SPAN, b : b + SPAN].astype(f32) * (part_b / total)
             heads_ref[i * SPAN : (i + 1) * SPAN, h * HD : (h + 1) * HD] = joined.T.astype(jnp.bfloat16)
-    multiply(0, heads_ref, w_ref, other_ref, out_ref)
+    multiply(0, heads_ref, w_ref, other_ref, out_refs)
 
 
 def join(mine, theirs, w, other):
@@ -315,33 +315,45 @@
         join_kernel,
         out_shape=(
             jax.ShapeDtypeStruct((rows, depth), jnp.bfloat16),
-            jax.ShapeDtypeStruct((2, rows, COLS), jnp.bfloat16),
+            jax.ShapeDtypeStruct((rows, COLS), jnp.bfloat16),
+            jax.ShapeDtypeStruct((rows, COLS), jnp.bfloat16),
         ),
         in_specs=[VMEM] * 4,
-        out_specs=(VMEM, VMEM),
+        out_specs=(VMEM,) * 3,
         compiler_params=grant(20),
         name="join",
     )(mine, theirs, w, other)
 
 
-def project_kernel(heads_ref, w_ref, other_ref, out_ref):
-    multiply(2, heads_ref, w_ref, other_ref, out_ref)
+def project_kernel(heads_ref, w_ref, other_ref, *out_refs):
+    multiply(2, heads_ref, w_ref, other_ref, out_refs)
 
 
 def project(heads, w, other):
     rows = heads.shape[0]
     return pl.pallas_call(
         project_kernel,
-        out_shape=jax.ShapeDtypeStruct((6, rows, COLS), jnp.bfloat16),
+        out_shape=(jax.ShapeDtypeStruct((rows, COLS), jnp.bfloat16),) * 6,
         in_specs=[VMEM] * 3,
-        out_specs=VMEM,
+        out_specs=(VMEM,) * 6,
         compiler_params=grant(20),
         name="project",
     )(heads, w, other)
 
 
+def add_kernel(a_ref, b_ref, out_ref):
+    out_ref[...] = (a_ref[...].astype(jnp.float32) + b_ref[...].astype(jnp.float32)).astype(jnp.bfloat16)
+
+
 def add(a, b):
-    return (a.astype(jnp.float32) + b.astype(jnp.float32)).astype(jnp.bfloat16)
+    return pl.pallas_call(
+        add_kernel,
+        out_shape=jax.ShapeDtypeStruct(a.shape, a.dtype),
+        in_specs=[VMEM, VMEM],
+        out_specs=VMEM,
+        compiler_params=grant(4),
+        name="add",
+    )(a, b)
 
 
 def per_device(queries, keys, values, out_weight, segment_ids, loss_mask, span_order):
@@ -367,21 +379,22 @@
     theirs = lax.ppermute(mine, "tensor", SWAP)
 
     inward, outward = perm_tensor(inner), perm_tensor(outer)
-    heads, far = join(mine, theirs, out_weight, weight_other)
-    far = lax.ppermute(far, "tensor", outward)
-    rest = project(heads, out_weight, weight_other)
+    heads, far_a, far_b = join(mine, theirs, out_weight, weight_other)
+    far_a = lax.ppermute(far_a, "tensor", outward)
+    far_b = lax.ppermute(far_b, "tensor", outward)
+    mid_a, mid_b, near_a, near_b, early, own = project(heads, out_weight, weight_other)
     around = [(d * 16 + t, (d + 1 + t % 2) % 3 * 16 + t) for d in range(3) for t in range(16)]
-    early = lax.ppermute(rest[4], "tensor", inward)
+    early = lax.ppermute(early, "tensor", inward)
     one = lax.ppermute(tally, ("dp", "tensor"), around)
     two = lax.ppermute(one, "tensor", SWAP)
-    mid = lax.ppermute(add(rest[0:2], far), "tensor", inward)
-    near = add(rest[2:4], mid)
-    passing = lax.ppermute(near[0], "tensor", perm_tensor(beyond))
-    near = lax.ppermute(near[1], "tensor", outward)
+    mid_a = lax.ppermute(add(mid_a, far_a), "tensor", inward)
+    mid_b = lax.ppermute(add(mid_b, far_b), "tensor", inward)
+    near_a = lax.ppermute(add(near_a, mid_a), "tensor", perm_tensor(beyond))
+    near_b = lax.ppermute(add(near_b, mid_b), "tensor", outward)
     count = (tally + one + two)[0, 0]
     scale_all = lax.axis_size("dp") * lax.axis_size("context") * queries.shape[1]
     weight = loss_mask[0].astype(f32) * scale_all / count
-    summed = rest[5].astype(f32) + early.astype(f32) + near.astype(f32) + passing.astype(f32)
+    summed = own.astype(f32) + early.astype(f32) + near_a.astype(f32) + near_b.astype(f32)
     return (summed * weight[:, None]).astype(jnp.bfloat16)[None]
 
 

time: 108 us -> 109 us (level)
  starting transfers between devices: 65.7 us -> 72.2 us
  waiting for transfers between devices: 25.4 us -> 20.7 us
    ppermute x5 -> x7, waiting for transfers between devices: 11.1 us -> 6.76 us  [the longest x1 3.9 us: per_device(): near_b = lax.ppermute(add(near_b, mid_b), 'tensor', outward)]
    ppermute x1, starting transfers between devices: 3.26 us -> 6.63 us  [per_device(): two = lax.ppermute(one, 'tensor', SWAP)]
    ppermute x5 -> x7, starting transfers between devices: 19.8 us -> 22.9 us  [the longest x1 5.09 us: per_device(): mid_a = lax.ppermute(add(mid_a, far_a), 'tensor', inward)]
  transfers between devices with their start and end apart: 15 -> 17, of which waited for: 7 -> 8; matrix products, arithmetic and copies ran while one was open for 1% -> 1% of each run, Pallas kernels for 9% -> 9%
where the time goes in v6:
time: 109 us
  starting transfers between devices  72.2 us (66%)
  waiting for transfers between devices  20.7 us (19%)
  Pallas kernels  13.4 us (12%)
  other arithmetic  1.55 us (1%)
    ppermute x1, starting transfers between devices, per_device(): weight_other = lax.ppermute(packed, 'tensor', SWAP)  12.6 us
    ppermute x1, starting transfers between devices, per_device(): q_other = lax.ppermute(queries[0], 'tensor', SWAP)  8.27 us
    pallas_call x3, Pallas kernels, call(): pl.pallas_call(kernel, out_shape=tuple((jax.ShapeDtypeStruct(*m) for m in...  7.11 us
    ppermute x1, starting transfers between devices, per_device(): two = lax.ppermute(one, 'tensor', SWAP)  6.63 us
    ppermute x1, waiting for transfers between devices, per_device(): kv4 = cat(kv2, lax.ppermute(kv2, both, perm_context('z', outer)))  6.1 us
    ppermute x1, starting transfers between devices, per_device(): r1 = lax.ppermute(kv1, both, perm_context('z', inner))  5.32 us
    ppermute x1, starting transfers between devices, per_device(): mid_a = lax.ppermute(add(mid_a, far_a), 'tensor', inward)  5.09 us
    ppermute x1, starting transfers between devices, per_device(): near_a = lax.ppermute(add(near_a, mid_a), 'tensor', perm_tensor(beyond))  4.16 us
  transfers between devices with their start and end apart: 17, of which 8 were waited for; matrix products, arithmetic and copies ran while one was open for 1% of the time, Pallas kernels for 9%

profile of v6, /device:TPU:1, one launch (start us, length us, event | category | flops | bytes accessed | tf_op | source)
XLA Modules:
  0.0 108.7 jit_solution(535010090312541944)
XLA Ops:
  0.0 2.4 %pack.1 = bf16[8,512,512]{2,1,0:T(8,128)(2,1)S(1)} custom-call(bf16[512,8192]{1,0:T(8,128)(2,1)} %w_ref.5), custom_call_target="tpu_custom_call" | custom-call | tf_op jit(solution)/shard_map/pack/pallas_call | solution.py:122
  2.4 12.6 %collective-permute-start.7 = (bf16[8,512,512]{2,1,0:T(8,128)(2,1)S(1)}, bf16[8,512,512]{2,1,0:T(8,128)(2,1)S(1)}, u32[]{:S(2)}, u32[]{:S(2)}) collective-permute-start(bf16[8,512,512]{2,1,0:T(8,128)(2,1)S(1)} %pack.1), channel_id=1, source_target_pairs={{0,1},{1,0},{2,3},{3,2},{4,5},{5,4},{6,7},{7,6},{8,9},{9,8},{10,11... | collective-permute-start | bytes 12582920 | tf_op jit(solution)/shard_map/ppermute | solution.py:371
  15.9 5.3 %collective-permute-start = (bf16[136,256]{1,0:T(8,128)(2,1)S(1)}, bf16[136,256]{1,0:T(8,128)(2,1)S(1)}, u32[]{:S(2)}, u32[]{:S(2)}) collective-permute-start(bf16[136,256]{1,0:T(8,128)(2,1)S(1)} %prepare.1), channel_id=1, source_target_pairs={{0,16},{1,49},{2,18},{3,51},{4,20},{5,53},{6,22},{7,55},{8,24},{9,... | collective-permute-start | bytes 208904 | tf_op jit(solution)/shard_map/ppermute | solution.py:366
  21.2 2.7 %collective-permute-done = bf16[136,256]{1,0:T(8,128)(2,1)S(1)} collective-permute-done((bf16[136,256]{1,0:T(8,128)(2,1)S(1)}, bf16[136,256]{1,0:T(8,128)(2,1)S(1)}, u32[]{:S(2)}, u32[]{:S(2)}) %collective-permute-start) | collective-permute-done | bytes 69664 | tf_op jit(solution)/shard_map/ppermute | solution.py:366
  24.0 1.9 %collective-permute-start.1 = (bf16[272,256]{1,0:T(8,128)(2,1)S(1)}, bf16[272,256]{1,0:T(8,128)(2,1)S(1)}, u32[]{:S(2)}, u32[]{:S(2)}) collective-permute-start(bf16[272,256]{1,0:T(8,128)(2,1)S(1)} %pad_maximum_fusion.1), channel_id=1, source_target_pairs={{0,48},{1,17},{2,50},{3,19},{4,52},{5,21},{6,54},{7,23},{8,56},{9,... | collective-permute-start | bytes 417800 | tf_op jit(solution)/shard_map/ppermute | solution.py:370
  25.9 6.1 %collective-permute-done.1 = bf16[272,256]{1,0:T(8,128)(2,1)S(1)} collective-permute-done((bf16[272,256]{1,0:T(8,128)(2,1)S(1)}, bf16[272,256]{1,0:T(8,128)(2,1)S(1)}, u32[]{:S(2)}, u32[]{:S(2)}) %collective-permute-start.1) | collective-permute-done | bytes 139296 | tf_op jit(solution)/shard_map/ppermute | solution.py:370
  34.0 3.6 %collective-permute-start.4 = (bf16[544,256]{1,0:T(8,128)(2,1)S(1)}, bf16[544,256]{1,0:T(8,128)(2,1)S(1)}, u32[]{:S(2)}, u32[]{:S(2)}) collective-permute-start(bf16[544,256]{1,0:T(8,128)(2,1)S(1)} %pad_maximum_fusion.blocks_ref), channel_id=1, source_target_pairs={{0,64},{1,193},{2,66},{3,195},{4,68},{5,197},{6,70},{7,199},{8,72}... | collective-permute-start | bytes 835592 | tf_op jit(solution)/shard_map/ppermute | solution.py:374
  37.6 3.5 %collective-permute-start.2 = (bf16[544,256]{1,0:T(8,128)(2,1)S(1)}, bf16[544,256]{1,0:T(8,128)(2,1)S(1)}, u32[]{:S(2)}, u32[]{:S(2)}) collective-permute-start(bf16[544,256]{1,0:T(8,128)(2,1)S(1)} %pad_maximum_fusion.blocks_ref), channel_id=1, source_target_pairs={{0,128},{1,129},{2,130},{3,131},{4,132},{5,133},{6,134},{7,135},{8... | collective-permute-start | bytes 835592 | tf_op jit(solution)/shard_map/ppermute | solution.py:376
  41.0 8.3 %collective-permute-start.3 = (bf16[256,512]{1,0:T(8,128)(2,1)S(1)}, bf16[256,512]{1,0:T(8,128)(2,1)S(1)}, u32[]{:S(2)}, u32[]{:S(2)}) collective-permute-start(bf16[256,512]{1,0:T(8,128)(2,1)S(1)} %bitcast.6), channel_id=1, source_target_pairs={{0,1},{1,0},{2,3},{3,2},{4,5},{5,4},{6,7},{7,6},{8,9},{9,8},{10,11... | collective-permute-start | bytes 786440 | tf_op jit(solution)/shard_map/ppermute | solution.py:367
  50.5 2.3 %shard_map.73 = (bf16[2,1024,128]{2,1,0:T(8,128)(2,1)S(1)}, f32[2,1,128]{2,1,0:T(1,128)S(1)}, f32[2,1,1024]{2,1,0:T(1,128)S(1)}, f32[2,1,1024]{2,1,0:T(1,128)S(1...) custom-call(s32[32]{0:T(128)S(1)} %copy-done.3, s32[32,128]{1,0:T(8,128)S(1)} %bitcast.8, ...), custom_call_target="tpu_custom_call" | custom-call | tf_op jit(solution)/shard_map/pallas_call | solution.py:257
  52.8 3.1 %shard_map.74 = (f32[2,1,1024]{2,1,0:T(1,128)S(1)}, f32[2,1,1024]{2,1,0:T(1,128)S(1)}, f32[2,128,1024]{2,1,0:T(8,128)S(1)}, f32[8,128]{1,0:T(8,128)S(1)}) custom-call(s32[32]{0:T(128)S(1)} %copy-done.3, bf16[544,256]{1,0:T(8,128)(2,1)S(1)} %collective-permute-done.4.a_ref, bf16[544,256]{1,0:T(8,128)(2,1)S(1)} %collective-permute-done.5.b_ref, ...), custom_call_target="tpu_custom_call" | custom-call | tf_op jit(solution)/shard_map/pallas_call | solution.py:257
  57.6 3.7 %collective-permute-start.6 = (bf16[136,2048]{1,0:T(8,128)(2,1)S(1)}, bf16[136,2048]{1,0:T(8,128)(2,1)S(1)}, u32[]{:S(2)}, u32[]{:S(2)}) collective-permute-start(bf16[136,2048]{1,0:T(8,128)(2,1)S(1)} %get-tuple-element.36.mine_ref), channel_id=1, source_target_pairs={{0,1},{1,0},{2,3},{3,2},{4,5},{5,4},{6,7},{7,6},{8,9},{9,8},{10,11... | collective-permute-start | bytes 1671176 | tf_op jit(solution)/shard_map/ppermute | solution.py:379
  63.8 3.2 %collective-permute-start.9 = (bf16[256,512]{1,0:T(8,128)(2,1)S(1)}, bf16[256,512]{1,0:T(8,128)(2,1)S(1)}, u32[]{:S(2)}, u32[]{:S(2)}) collective-permute-start(bf16[256,512]{1,0:T(8,128)(2,1)S(1)} %get-tuple-element.42), channel_id=1, source_target_pairs={{0,14},{1,3},{2,4},{3,1},{4,2},{5,7},{6,8},{7,5},{8,6},{9,11},{10,... | collective-permute-start | bytes 786440 | tf_op jit(solution)/shard_map/ppermute | solution.py:383
  67.1 2.1 %collective-permute-start.12 = (bf16[256,512]{1,0:T(8,128)(2,1)S(1)}, bf16[256,512]{1,0:T(8,128)(2,1)S(1)}, u32[]{:S(2)}, u32[]{:S(2)}) collective-permute-start(bf16[256,512]{1,0:T(8,128)(2,1)S(1)} %get-tuple-element.45), channel_id=1, source_target_pairs={{0,14},{1,3},{2,4},{3,1},{4,2},{5,7},{6,8},{7,5},{8,6},{9,11},{10,... | collective-permute-start | bytes 786440 | tf_op jit(solution)/shard_map/ppermute | solution.py:384
  71.3 5.1 %collective-permute-start.10 = (bf16[256,512]{1,0:T(8,128)(2,1)S(1)}, bf16[256,512]{1,0:T(8,128)(2,1)S(1)}, u32[]{:S(2)}, u32[]{:S(2)}) collective-permute-start(bf16[256,512]{1,0:T(8,128)(2,1)S(1)} %add.35), channel_id=1, source_target_pairs={{0,2},{1,15},{2,0},{3,5},{4,6},{5,3},{6,4},{7,9},{8,10},{9,7},{10,... | collective-permute-start | bytes 786440 | tf_op jit(solution)/shard_map/ppermute | solution.py:390
  76.5 2.9 %collective-permute-start.13 = (bf16[256,512]{1,0:T(8,128)(2,1)S(1)}, bf16[256,512]{1,0:T(8,128)(2,1)S(1)}, u32[]{:S(2)}, u32[]{:S(2)}) collective-permute-start(bf16[256,512]{1,0:T(8,128)(2,1)S(1)} %add.37), channel_id=1, source_target_pairs={{0,2},{1,15},{2,0},{3,5},{4,6},{5,3},{6,4},{7,9},{8,10},{9,7},{10,... | collective-permute-start | bytes 786440 | tf_op jit(solution)/shard_map/ppermute | solution.py:391
  79.4 1.9 %collective-permute-start.15 = (f32[8,128]{1,0:T(8,128)S(1)}, f32[8,128]{1,0:T(8,128)S(1)}, u32[]{:S(2)}, u32[]{:S(2)}) collective-permute-start(f32[8,128]{1,0:T(8,128)S(1)} %get-tuple-element.46), channel_id=1, source_target_pairs={{0,256},{1,513},{2,258},{3,515},{4,260},{5,517},{6,262},{7,519},{8... | collective-permute-start | bytes 12296 | tf_op jit(solution)/shard_map/ppermute | solution.py:388
  81.3 2.4 %collective-permute-done.15 = f32[8,128]{1,0:T(8,128)S(1)} collective-permute-done((f32[8,128]{1,0:T(8,128)S(1)}, f32[8,128]{1,0:T(8,128)S(1)}, u32[]{:S(2)}, u32[]{:S(2)}) %collective-permute-start.15) | collective-permute-done | bytes 4128 | tf_op jit(solution)/shard_map/ppermute | solution.py:388
  83.8 6.6 %collective-permute-start.16 = (f32[8,128]{1,0:T(8,128)S(1)}, f32[8,128]{1,0:T(8,128)S(1)}, u32[]{:S(2)}, u32[]{:S(2)}) collective-permute-start(f32[8,128]{1,0:T(8,128)S(1)} %collective-permute-done.15), channel_id=1, source_target_pairs={{0,1},{1,0},{2,3},{3,2},{4,5},{5,4},{6,7},{7,6},{8,9},{9,8},{10,11... | collective-permute-start | bytes 12296 | tf_op jit(solution)/shard_map/ppermute | solution.py:389
  90.4 2.7 %collective-permute-start.8 = (bf16[256,512]{1,0:T(8,128)(2,1)S(1)}, bf16[256,512]{1,0:T(8,128)(2,1)S(1)}, u32[]{:S(2)}, u32[]{:S(2)}) collective-permute-start(bf16[256,512]{1,0:T(8,128)(2,1)S(1)} %get-tuple-element.39), channel_id=1, source_target_pairs={{0,2},{1,15},{2,0},{3,5},{4,6},{5,3},{6,4},{7,9},{8,10},{9,7},{10,... | collective-permute-start | bytes 786440 | tf_op jit(solution)/shard_map/ppermute | solution.py:387
  93.2 4.2 %collective-permute-start.11 = (bf16[256,512]{1,0:T(8,128)(2,1)S(1)}, bf16[256,512]{1,0:T(8,128)(2,1)S(1)}, u32[]{:S(2)}, u32[]{:S(2)}) collective-permute-start(bf16[256,512]{1,0:T(8,128)(2,1)S(1)} %add.36), channel_id=1, source_target_pairs={{0,12},{1,5},{2,6},{3,15},{4,0},{5,9},{6,10},{7,3},{8,4},{9,13},{1... | collective-permute-start | bytes 786440 | tf_op jit(solution)/shard_map/ppermute | solution.py:392
  97.4 2.7 %collective-permute-start.14 = (bf16[256,512]{1,0:T(8,128)(2,1)S(1)}, bf16[256,512]{1,0:T(8,128)(2,1)S(1)}, u32[]{:S(2)}, u32[]{:S(2)}) collective-permute-start(bf16[256,512]{1,0:T(8,128)(2,1)S(1)} %add.38), channel_id=1, source_target_pairs={{0,14},{1,3},{2,4},{3,1},{4,2},{5,7},{6,8},{7,5},{8,6},{9,11},{10,... | collective-permute-start | bytes 786440 | tf_op jit(solution)/shard_map/ppermute | solution.py:393
  101.4 2.6 %collective-permute-done.11 = bf16[256,512]{1,0:T(8,128)(2,1)S(1)} collective-permute-done((bf16[256,512]{1,0:T(8,128)(2,1)S(1)}, bf16[256,512]{1,0:T(8,128)(2,1)S(1)}, u32[]{:S(2)}, u32[]{:S(2)}) %collective-permute-start.11) | collective-permute-done | bytes 262176 | tf_op jit(solution)/shard_map/ppermute | solution.py:392
  103.9 3.9 %collective-permute-done.14 = bf16[256,512]{1,0:T(8,128)(2,1)S(1)} collective-permute-done((bf16[256,512]{1,0:T(8,128)(2,1)S(1)}, bf16[256,512]{1,0:T(8,128)(2,1)S(1)}, u32[]{:S(2)}, u32[]{:S(2)}) %collective-permute-start.14) | collective-permute-done | bytes 262176 | tf_op jit(solution)/shard_map/ppermute | solution.py:393
  (37 shorter events, 12.6 us)
Async XLA Ops:
  0.0 41.0 %copy-start.1 = (bf16[1,256,512]{2,1,0:T(8,128)(2,1)S(1)}, bf16[1,256,512]{2,1,0:T(8,128)(2,1)}, u32[]{:S(2)}) copy-start(bf16[1,256,512]{2,1,0:T(8,128)(2,1)} %param.7) | copy-start | bytes 786436
  0.0 50.5 %copy-start.3 = (s32[32]{0:T(128)S(1)}, s32[32]{0:T(128)}, u32[]{:S(2)}) copy-start(s32[32]{0:T(128)} %spans.5) | copy-start | bytes 388
  0.0 50.5 %copy-start.2 = (s32[1,4096]{1,0:T(1,128)S(1)}, s32[1,4096]{1,0:T(1,128)}, u32[]{:S(2)}) copy-start(s32[1,4096]{1,0:T(1,128)} %param.11) | copy-start | bytes 49156
  0.0 62.9 %copy-start = (bf16[512,8192]{1,0:T(8,128)(2,1)S(1)}, bf16[512,8192]{1,0:T(8,128)(2,1)}, u32[]{:S(2)}) copy-start(bf16[512,8192]{1,0:T(8,128)(2,1)} %w_ref.5) | copy-start | bytes 25165828
  2.4 60.4 %collective-permute-start.7 = (bf16[8,512,512]{2,1,0:T(8,128)(2,1)S(1)}, bf16[8,512,512]{2,1,0:T(8,128)(2,1)S(1)}, u32[]{:S(2)}, u32[]{:S(2)}) collective-permute-start(bf16[8,512,512]{2,1,0:T(8,128)(2,1)S(1)} %pack.1), channel_id=1, source_target_pairs={{0,1},{1,0},{2,3},{3,2},{4,5},{5,4},{6,7},{7,6},{8,9},{9,8},{10,11... | collective-permute-start | bytes 12582920 | tf_op jit(solution)/shard_map/ppermute | solution.py:371
  15.9 8.1 %collective-permute-start = (bf16[136,256]{1,0:T(8,128)(2,1)S(1)}, bf16[136,256]{1,0:T(8,128)(2,1)S(1)}, u32[]{:S(2)}, u32[]{:S(2)}) collective-permute-start(bf16[136,256]{1,0:T(8,128)(2,1)S(1)} %prepare.1), channel_id=1, source_target_pairs={{0,16},{1,49},{2,18},{3,51},{4,20},{5,53},{6,22},{7,55},{8,24},{9,... | collective-permute-start | bytes 208904 | tf_op jit(solution)/shard_map/ppermute | solution.py:366
  24.0 8.0 %collective-permute-start.1 = (bf16[272,256]{1,0:T(8,128)(2,1)S(1)}, bf16[272,256]{1,0:T(8,128)(2,1)S(1)}, u32[]{:S(2)}, u32[]{:S(2)}) collective-permute-start(bf16[272,256]{1,0:T(8,128)(2,1)S(1)} %pad_maximum_fusion.1), channel_id=1, source_target_pairs={{0,48},{1,17},{2,50},{3,19},{4,52},{5,21},{6,54},{7,23},{8,56},{9,... | collective-permute-start | bytes 417800 | tf_op jit(solution)/shard_map/ppermute | solution.py:370
  32.0 20.8 %collective-permute-start.5 = (bf16[544,256]{1,0:T(8,128)(2,1)S(1)}, bf16[544,256]{1,0:T(8,128)(2,1)S(1)}, u32[]{:S(2)}, u32[]{:S(2)}) collective-permute-start(bf16[544,256]{1,0:T(8,128)(2,1)S(1)} %pad_maximum_fusion.blocks_ref), channel_id=1, source_target_pairs={{0,192},{1,65},{2,194},{3,67},{4,196},{5,69},{6,198},{7,71},{8,200... | collective-permute-start | bytes 835592 | tf_op jit(solution)/shard_map/ppermute | solution.py:375
  34.0 18.9 %collective-permute-start.4 = (bf16[544,256]{1,0:T(8,128)(2,1)S(1)}, bf16[544,256]{1,0:T(8,128)(2,1)S(1)}, u32[]{:S(2)}, u32[]{:S(2)}) collective-permute-start(bf16[544,256]{1,0:T(8,128)(2,1)S(1)} %pad_maximum_fusion.blocks_ref), channel_id=1, source_target_pairs={{0,64},{1,193},{2,66},{3,195},{4,68},{5,197},{6,70},{7,199},{8,72}... | collective-permute-start | bytes 835592 | tf_op jit(solution)/shard_map/ppermute | solution.py:374
  37.6 18.3 %collective-permute-start.2 = (bf16[544,256]{1,0:T(8,128)(2,1)S(1)}, bf16[544,256]{1,0:T(8,128)(2,1)S(1)}, u32[]{:S(2)}, u32[]{:S(2)}) collective-permute-start(bf16[544,256]{1,0:T(8,128)(2,1)S(1)} %pad_maximum_fusion.blocks_ref), channel_id=1, source_target_pairs={{0,128},{1,129},{2,130},{3,131},{4,132},{5,133},{6,134},{7,135},{8... | collective-permute-start | bytes 835592 | tf_op jit(solution)/shard_map/ppermute | solution.py:376
  41.0 9.4 %collective-permute-start.3 = (bf16[256,512]{1,0:T(8,128)(2,1)S(1)}, bf16[256,512]{1,0:T(8,128)(2,1)S(1)}, u32[]{:S(2)}, u32[]{:S(2)}) collective-permute-start(bf16[256,512]{1,0:T(8,128)(2,1)S(1)} %bitcast.6), channel_id=1, source_target_pairs={{0,1},{1,0},{2,3},{3,2},{4,5},{5,4},{6,7},{7,6},{8,9},{9,8},{10,11... | collective-permute-start | bytes 786440 | tf_op jit(solution)/shard_map/ppermute | solution.py:367
  57.6 5.2 %collective-permute-start.6 = (bf16[136,2048]{1,0:T(8,128)(2,1)S(1)}, bf16[136,2048]{1,0:T(8,128)(2,1)S(1)}, u32[]{:S(2)}, u32[]{:S(2)}) collective-permute-start(bf16[136,2048]{1,0:T(8,128)(2,1)S(1)} %get-tuple-element.36.mine_ref), channel_id=1, source_target_pairs={{0,1},{1,0},{2,3},{3,2},{4,5},{5,4},{6,7},{7,6},{8,9},{9,8},{10,11... | collective-permute-start | bytes 1671176 | tf_op jit(solution)/shard_map/ppermute | solution.py:379
  63.8 7.4 %collective-permute-start.9 = (bf16[256,512]{1,0:T(8,128)(2,1)S(1)}, bf16[256,512]{1,0:T(8,128)(2,1)S(1)}, u32[]{:S(2)}, u32[]{:S(2)}) collective-permute-start(bf16[256,512]{1,0:T(8,128)(2,1)S(1)} %get-tuple-element.42), channel_id=1, source_target_pairs={{0,14},{1,3},{2,4},{3,1},{4,2},{5,7},{6,8},{7,5},{8,6},{9,11},{10,... | collective-permute-start | bytes 786440 | tf_op jit(solution)/shard_map/ppermute | solution.py:383
  67.1 9.4 %collective-permute-start.12 = (bf16[256,512]{1,0:T(8,128)(2,1)S(1)}, bf16[256,512]{1,0:T(8,128)(2,1)S(1)}, u32[]{:S(2)}, u32[]{:S(2)}) collective-permute-start(bf16[256,512]{1,0:T(8,128)(2,1)S(1)} %get-tuple-element.45), channel_id=1, source_target_pairs={{0,14},{1,3},{2,4},{3,1},{4,2},{5,7},{6,8},{7,5},{8,6},{9,11},{10,... | collective-permute-start | bytes 786440 | tf_op jit(solution)/shard_map/ppermute | solution.py:384
  69.1 31.6 %copy-start.4 = (s32[1,256]{1,0:T(1,128)S(1)}, s32[1,256]{1,0:T(1,128)}, u32[]{:S(2)}) copy-start(s32[1,256]{1,0:T(1,128)} %mask_hbm.1) | copy-start | bytes 3076
  71.3 21.8 %collective-permute-start.10 = (bf16[256,512]{1,0:T(8,128)(2,1)S(1)}, bf16[256,512]{1,0:T(8,128)(2,1)S(1)}, u32[]{:S(2)}, u32[]{:S(2)}) collective-permute-start(bf16[256,512]{1,0:T(8,128)(2,1)S(1)} %add.35), channel_id=1, source_target_pairs={{0,2},{1,15},{2,0},{3,5},{4,6},{5,3},{6,4},{7,9},{8,10},{9,7},{10,... | collective-permute-start | bytes 786440 | tf_op jit(solution)/shard_map/ppermute | solution.py:390
  76.5 20.9 %collective-permute-start.13 = (bf16[256,512]{1,0:T(8,128)(2,1)S(1)}, bf16[256,512]{1,0:T(8,128)(2,1)S(1)}, u32[]{:S(2)}, u32[]{:S(2)}) collective-permute-start(bf16[256,512]{1,0:T(8,128)(2,1)S(1)} %add.37), channel_id=1, source_target_pairs={{0,2},{1,15},{2,0},{3,5},{4,6},{5,3},{6,4},{7,9},{8,10},{9,7},{10,... | collective-permute-start | bytes 786440 | tf_op jit(solution)/shard_map/ppermute | solution.py:391
  79.4 4.4 %collective-permute-start.15 = (f32[8,128]{1,0:T(8,128)S(1)}, f32[8,128]{1,0:T(8,128)S(1)}, u32[]{:S(2)}, u32[]{:S(2)}) collective-permute-start(f32[8,128]{1,0:T(8,128)S(1)} %get-tuple-element.46), channel_id=1, source_target_pairs={{0,256},{1,513},{2,258},{3,515},{4,260},{5,517},{6,262},{7,519},{8... | collective-permute-start | bytes 12296 | tf_op jit(solution)/shard_map/ppermute | solution.py:388
  83.8 16.4 %collective-permute-start.16 = (f32[8,128]{1,0:T(8,128)S(1)}, f32[8,128]{1,0:T(8,128)S(1)}, u32[]{:S(2)}, u32[]{:S(2)}) collective-permute-start(f32[8,128]{1,0:T(8,128)S(1)} %collective-permute-done.15), channel_id=1, source_target_pairs={{0,1},{1,0},{2,3},{3,2},{4,5},{5,4},{6,7},{7,6},{8,9},{9,8},{10,11... | collective-permute-start | bytes 12296 | tf_op jit(solution)/shard_map/ppermute | solution.py:389
  90.4 11.0 %collective-permute-start.8 = (bf16[256,512]{1,0:T(8,128)(2,1)S(1)}, bf16[256,512]{1,0:T(8,128)(2,1)S(1)}, u32[]{:S(2)}, u32[]{:S(2)}) collective-permute-start(bf16[256,512]{1,0:T(8,128)(2,1)S(1)} %get-tuple-element.39), channel_id=1, source_target_pairs={{0,2},{1,15},{2,0},{3,5},{4,6},{5,3},{6,4},{7,9},{8,10},{9,7},{10,... | collective-permute-start | bytes 786440 | tf_op jit(solution)/shard_map/ppermute | solution.py:387
  93.2 10.8 %collective-permute-start.11 = (bf16[256,512]{1,0:T(8,128)(2,1)S(1)}, bf16[256,512]{1,0:T(8,128)(2,1)S(1)}, u32[]{:S(2)}, u32[]{:S(2)}) collective-permute-start(bf16[256,512]{1,0:T(8,128)(2,1)S(1)} %add.36), channel_id=1, source_target_pairs={{0,12},{1,5},{2,6},{3,15},{4,0},{5,9},{6,10},{7,3},{8,4},{9,13},{1... | collective-permute-start | bytes 786440 | tf_op jit(solution)/shard_map/ppermute | solution.py:392
  97.4 10.4 %collective-permute-start.14 = (bf16[256,512]{1,0:T(8,128)(2,1)S(1)}, bf16[256,512]{1,0:T(8,128)(2,1)S(1)}, u32[]{:S(2)}, u32[]{:S(2)}) collective-permute-start(bf16[256,512]{1,0:T(8,128)(2,1)S(1)} %add.38), channel_id=1, source_target_pairs={{0,14},{1,3},{2,4},{3,1},{4,2},{5,7},{6,8},{7,5},{8,6},{9,11},{10,... | collective-permute-start | bytes 786440 | tf_op jit(solution)/shard_map/ppermute | solution.py:393

commit v7 on v6

--- a/solution.py
+++ b/solution.py
@@ -370,11 +370,9 @@
     kv4 = cat(kv2, lax.ppermute(kv2, both, perm_context("z", outer)))
     weight_other = lax.ppermute(packed, "tensor", SWAP)
     beyond = lambda i, c, n: inner(outer(i, c, n), c, n)
-    gathered = [
-        lax.ppermute(kv4, both, perm_context("x", inner)),
-        lax.ppermute(kv4, both, perm_context("x", outer)),
-        lax.ppermute(kv4, both, perm_context("x", beyond)),
-    ]
+    x_inner = lax.ppermute(kv4, both, perm_context("x", inner))
+    x_outer = lax.ppermute(kv4, both, perm_context("x", outer))
+    gathered = x_inner, x_outer, lax.ppermute(x_inner, both, perm_context("x", outer))
     mine, tally = attention(span_order, segment_ids.reshape(32, SPAN), queries[0], q_other, kv4, *gathered)
     theirs = lax.ppermute(mine, "tensor", SWAP)
 

time: 109 us -> 113 us (1.037)
  waiting for transfers between devices: 20.7 us -> 24.2 us
    ppermute x3, waiting for transfers between devices: 0.01 us -> 3.51 us  [the longest x1 3.5 us: per_device(): x_inner = lax.ppermute(kv4, both, perm_context('x', inner))]
    ppermute x1, starting transfers between devices: 8.27 us -> 10.7 us  [per_device(): q_other = lax.ppermute(queries[0], 'tensor', SWAP)]
    ppermute x3, starting transfers between devices: 8.98 us -> 6.89 us  [the longest x1 3.07 us: per_device(): x_inner = lax.ppermute(kv4, both, perm_context('x', inner))]
  transfers between devices with their start and end apart: 17 -> 17, of which waited for: 8 -> 9; matrix products, arithmetic and copies ran while one was open for 1% -> 1% of each run, Pallas kernels for 9% -> 9%
where the time goes in v7:
time: 113 us
  starting transfers between devices  72.5 us (64%)
  waiting for transfers between devices  24.2 us (21%)
  Pallas kernels  13.4 us (12%)
  other arithmetic  1.55 us (1%)
    ppermute x1, starting transfers between devices, per_device(): weight_other = lax.ppermute(packed, 'tensor', SWAP)  12.6 us
    ppermute x1, starting transfers between devices, per_device(): q_other = lax.ppermute(queries[0], 'tensor', SWAP)  10.7 us
    pallas_call x3, Pallas kernels, call(): pl.pallas_call(kernel, out_shape=tuple((jax.ShapeDtypeStruct(*m) for m in...  7.12 us
    ppermute x1, starting transfers between devices, per_device(): two = lax.ppermute(one, 'tensor', SWAP)  6.62 us
    ppermute x1, waiting for transfers between devices, per_device(): kv4 = cat(kv2, lax.ppermute(kv2, both, perm_context('z', outer)))  6.1 us
    ppermute x1, starting transfers between devices, per_device(): r1 = lax.ppermute(kv1, both, perm_context('z', inner))  5.32 us
    ppermute x1, starting transfers between devices, per_device(): mid_a = lax.ppermute(add(mid_a, far_a), 'tensor', inward)  5.09 us
    ppermute x1, starting transfers between devices, per_device(): near_a = lax.ppermute(add(near_a, mid_a), 'tensor', perm_tensor(beyond))  4.12 us
  transfers between devices with their start and end apart: 17, of which 9 were waited for; matrix products, arithmetic and copies ran while one was open for 1% of the time, Pallas kernels for 9%

profile of v7, /device:TPU:1, one launch (start us, length us, event | category | flops | bytes accessed | tf_op | source)
XLA Modules:
  0.0 112.5 jit_solution(9224851804702713259)
XLA Ops:
  0.0 2.4 %pack.1 = bf16[8,512,512]{2,1,0:T(8,128)(2,1)S(1)} custom-call(bf16[512,8192]{1,0:T(8,128)(2,1)} %w_ref.5), custom_call_target="tpu_custom_call" | custom-call | tf_op jit(solution)/shard_map/pack/pallas_call | solution.py:122
  2.4 12.6 %collective-permute-start.7 = (bf16[8,512,512]{2,1,0:T(8,128)(2,1)S(1)}, bf16[8,512,512]{2,1,0:T(8,128)(2,1)S(1)}, u32[]{:S(2)}, u32[]{:S(2)}) collective-permute-start(bf16[8,512,512]{2,1,0:T(8,128)(2,1)S(1)} %pack.1), channel_id=1, source_target_pairs={{0,1},{1,0},{2,3},{3,2},{4,5},{5,4},{6,7},{7,6},{8,9},{9,8},{10,11... | collective-permute-start | bytes 12582920 | tf_op jit(solution)/shard_map/ppermute | solution.py:371
  15.9 5.3 %collective-permute-start = (bf16[136,256]{1,0:T(8,128)(2,1)S(1)}, bf16[136,256]{1,0:T(8,128)(2,1)S(1)}, u32[]{:S(2)}, u32[]{:S(2)}) collective-permute-start(bf16[136,256]{1,0:T(8,128)(2,1)S(1)} %prepare.1), channel_id=1, source_target_pairs={{0,16},{1,49},{2,18},{3,51},{4,20},{5,53},{6,22},{7,55},{8,24},{9,... | collective-permute-start | bytes 208904 | tf_op jit(solution)/shard_map/ppermute | solution.py:366
  21.2 2.7 %collective-permute-done = bf16[136,256]{1,0:T(8,128)(2,1)S(1)} collective-permute-done((bf16[136,256]{1,0:T(8,128)(2,1)S(1)}, bf16[136,256]{1,0:T(8,128)(2,1)S(1)}, u32[]{:S(2)}, u32[]{:S(2)}) %collective-permute-start) | collective-permute-done | bytes 69664 | tf_op jit(solution)/shard_map/ppermute | solution.py:366
  24.0 1.9 %collective-permute-start.1 = (bf16[272,256]{1,0:T(8,128)(2,1)S(1)}, bf16[272,256]{1,0:T(8,128)(2,1)S(1)}, u32[]{:S(2)}, u32[]{:S(2)}) collective-permute-start(bf16[272,256]{1,0:T(8,128)(2,1)S(1)} %pad_maximum_fusion.1), channel_id=1, source_target_pairs={{0,48},{1,17},{2,50},{3,19},{4,52},{5,21},{6,54},{7,23},{8,56},{9,... | collective-permute-start | bytes 417800 | tf_op jit(solution)/shard_map/ppermute | solution.py:370
  25.9 6.1 %collective-permute-done.1 = bf16[272,256]{1,0:T(8,128)(2,1)S(1)} collective-permute-done((bf16[272,256]{1,0:T(8,128)(2,1)S(1)}, bf16[272,256]{1,0:T(8,128)(2,1)S(1)}, u32[]{:S(2)}, u32[]{:S(2)}) %collective-permute-start.1) | collective-permute-done | bytes 139296 | tf_op jit(solution)/shard_map/ppermute | solution.py:370
  32.0 3.1 %collective-permute-start.2 = (bf16[544,256]{1,0:T(8,128)(2,1)S(1)}, bf16[544,256]{1,0:T(8,128)(2,1)S(1)}, u32[]{:S(2)}, u32[]{:S(2)}) collective-permute-start(bf16[544,256]{1,0:T(8,128)(2,1)S(1)} %pad_maximum_fusion.blocks_ref), channel_id=1, source_target_pairs={{0,64},{1,193},{2,66},{3,195},{4,68},{5,197},{6,70},{7,199},{8,72}... | collective-permute-start | bytes 835592 | tf_op jit(solution)/shard_map/ppermute | solution.py:373
  37.0 3.5 %collective-permute-done.2.a_ref = bf16[544,256]{1,0:T(8,128)(2,1)S(1)} collective-permute-done((bf16[544,256]{1,0:T(8,128)(2,1)S(1)}, bf16[544,256]{1,0:T(8,128)(2,1)S(1)}, u32[]{:S(2)}, u32[]{:S(2)}) %collective-permute-start.2) | collective-permute-done | bytes 278560 | tf_op jit(solution)/shard_map/ppermute | solution.py:373
  42.5 10.7 %collective-permute-start.4 = (bf16[256,512]{1,0:T(8,128)(2,1)S(1)}, bf16[256,512]{1,0:T(8,128)(2,1)S(1)}, u32[]{:S(2)}, u32[]{:S(2)}) collective-permute-start(bf16[256,512]{1,0:T(8,128)(2,1)S(1)} %bitcast.6), channel_id=1, source_target_pairs={{0,1},{1,0},{2,3},{3,2},{4,5},{5,4},{6,7},{7,6},{8,9},{9,8},{10,11... | collective-permute-start | bytes 786440 | tf_op jit(solution)/shard_map/ppermute | solution.py:367
  54.3 2.3 %shard_map.73 = (bf16[2,1024,128]{2,1,0:T(8,128)(2,1)S(1)}, f32[2,1,128]{2,1,0:T(1,128)S(1)}, f32[2,1,1024]{2,1,0:T(1,128)S(1)}, f32[2,1,1024]{2,1,0:T(1,128)S(1...) custom-call(s32[32]{0:T(128)S(1)} %copy-done.3, s32[32,128]{1,0:T(8,128)S(1)} %bitcast.8, ...), custom_call_target="tpu_custom_call" | custom-call | tf_op jit(solution)/shard_map/pallas_call | solution.py:257
  56.7 3.1 %shard_map.74 = (f32[2,1,1024]{2,1,0:T(1,128)S(1)}, f32[2,1,1024]{2,1,0:T(1,128)S(1)}, f32[2,128,1024]{2,1,0:T(8,128)S(1)}, f32[8,128]{1,0:T(8,128)S(1)}) custom-call(s32[32]{0:T(128)S(1)} %copy-done.3, bf16[544,256]{1,0:T(8,128)(2,1)S(1)} %collective-permute-done.2.a_ref, bf16[544,256]{1,0:T(8,128)(2,1)S(1)} %collective-permute-done.5.b_ref, ...), custom_call_target="tpu_custom_call" | custom-call | tf_op jit(solution)/shard_map/pallas_call | solution.py:257
  61.5 3.7 %collective-permute-start.6 = (bf16[136,2048]{1,0:T(8,128)(2,1)S(1)}, bf16[136,2048]{1,0:T(8,128)(2,1)S(1)}, u32[]{:S(2)}, u32[]{:S(2)}) collective-permute-start(bf16[136,2048]{1,0:T(8,128)(2,1)S(1)} %get-tuple-element.36.mine_ref), channel_id=1, source_target_pairs={{0,1},{1,0},{2,3},{3,2},{4,5},{5,4},{6,7},{7,6},{8,9},{9,8},{10,11... | collective-permute-start | bytes 1671176 | tf_op jit(solution)/shard_map/ppermute | solution.py:377
  67.7 3.2 %collective-permute-start.9 = (bf16[256,512]{1,0:T(8,128)(2,1)S(1)}, bf16[256,512]{1,0:T(8,128)(2,1)S(1)}, u32[]{:S(2)}, u32[]{:S(2)}) collective-permute-start(bf16[256,512]{1,0:T(8,128)(2,1)S(1)} %get-tuple-element.42), channel_id=1, source_target_pairs={{0,14},{1,3},{2,4},{3,1},{4,2},{5,7},{6,8},{7,5},{8,6},{9,11},{10,... | collective-permute-start | bytes 786440 | tf_op jit(solution)/shard_map/ppermute | solution.py:381
  70.9 2.1 %collective-permute-start.12 = (bf16[256,512]{1,0:T(8,128)(2,1)S(1)}, bf16[256,512]{1,0:T(8,128)(2,1)S(1)}, u32[]{:S(2)}, u32[]{:S(2)}) collective-permute-start(bf16[256,512]{1,0:T(8,128)(2,1)S(1)} %get-tuple-element.45), channel_id=1, source_target_pairs={{0,14},{1,3},{2,4},{3,1},{4,2},{5,7},{6,8},{7,5},{8,6},{9,11},{10,... | collective-permute-start | bytes 786440 | tf_op jit(solution)/shard_map/ppermute | solution.py:382
  75.2 5.1 %collective-permute-start.10 = (bf16[256,512]{1,0:T(8,128)(2,1)S(1)}, bf16[256,512]{1,0:T(8,128)(2,1)S(1)}, u32[]{:S(2)}, u32[]{:S(2)}) collective-permute-start(bf16[256,512]{1,0:T(8,128)(2,1)S(1)} %add.35), channel_id=1, source_target_pairs={{0,2},{1,15},{2,0},{3,5},{4,6},{5,3},{6,4},{7,9},{8,10},{9,7},{10,... | collective-permute-start | bytes 786440 | tf_op jit(solution)/shard_map/ppermute | solution.py:388
  80.3 2.9 %collective-permute-start.13 = (bf16[256,512]{1,0:T(8,128)(2,1)S(1)}, bf16[256,512]{1,0:T(8,128)(2,1)S(1)}, u32[]{:S(2)}, u32[]{:S(2)}) collective-permute-start(bf16[256,512]{1,0:T(8,128)(2,1)S(1)} %add.37), channel_id=1, source_target_pairs={{0,2},{1,15},{2,0},{3,5},{4,6},{5,3},{6,4},{7,9},{8,10},{9,7},{10,... | collective-permute-start | bytes 786440 | tf_op jit(solution)/shard_map/ppermute | solution.py:389
  83.2 1.9 %collective-permute-start.15 = (f32[8,128]{1,0:T(8,128)S(1)}, f32[8,128]{1,0:T(8,128)S(1)}, u32[]{:S(2)}, u32[]{:S(2)}) collective-permute-start(f32[8,128]{1,0:T(8,128)S(1)} %get-tuple-element.46), channel_id=1, source_target_pairs={{0,256},{1,513},{2,258},{3,515},{4,260},{5,517},{6,262},{7,519},{8... | collective-permute-start | bytes 12296 | tf_op jit(solution)/shard_map/ppermute | solution.py:386
  85.2 2.4 %collective-permute-done.15 = f32[8,128]{1,0:T(8,128)S(1)} collective-permute-done((f32[8,128]{1,0:T(8,128)S(1)}, f32[8,128]{1,0:T(8,128)S(1)}, u32[]{:S(2)}, u32[]{:S(2)}) %collective-permute-start.15) | collective-permute-done | bytes 4128 | tf_op jit(solution)/shard_map/ppermute | solution.py:386
  87.6 6.6 %collective-permute-start.16 = (f32[8,128]{1,0:T(8,128)S(1)}, f32[8,128]{1,0:T(8,128)S(1)}, u32[]{:S(2)}, u32[]{:S(2)}) collective-permute-start(f32[8,128]{1,0:T(8,128)S(1)} %collective-permute-done.15), channel_id=1, source_target_pairs={{0,1},{1,0},{2,3},{3,2},{4,5},{5,4},{6,7},{7,6},{8,9},{9,8},{10,11... | collective-permute-start | bytes 12296 | tf_op jit(solution)/shard_map/ppermute | solution.py:387
  94.2 2.7 %collective-permute-start.8 = (bf16[256,512]{1,0:T(8,128)(2,1)S(1)}, bf16[256,512]{1,0:T(8,128)(2,1)S(1)}, u32[]{:S(2)}, u32[]{:S(2)}) collective-permute-start(bf16[256,512]{1,0:T(8,128)(2,1)S(1)} %get-tuple-element.39), channel_id=1, source_target_pairs={{0,2},{1,15},{2,0},{3,5},{4,6},{5,3},{6,4},{7,9},{8,10},{9,7},{10,... | collective-permute-start | bytes 786440 | tf_op jit(solution)/shard_map/ppermute | solution.py:385
  97.0 4.1 %collective-permute-start.11 = (bf16[256,512]{1,0:T(8,128)(2,1)S(1)}, bf16[256,512]{1,0:T(8,128)(2,1)S(1)}, u32[]{:S(2)}, u32[]{:S(2)}) collective-permute-start(bf16[256,512]{1,0:T(8,128)(2,1)S(1)} %add.36), channel_id=1, source_target_pairs={{0,12},{1,5},{2,6},{3,15},{4,0},{5,9},{6,10},{7,3},{8,4},{9,13},{1... | collective-permute-start | bytes 786440 | tf_op jit(solution)/shard_map/ppermute | solution.py:390
  101.2 2.8 %collective-permute-start.14 = (bf16[256,512]{1,0:T(8,128)(2,1)S(1)}, bf16[256,512]{1,0:T(8,128)(2,1)S(1)}, u32[]{:S(2)}, u32[]{:S(2)}) collective-permute-start(bf16[256,512]{1,0:T(8,128)(2,1)S(1)} %add.38), channel_id=1, source_target_pairs={{0,14},{1,3},{2,4},{3,1},{4,2},{5,7},{6,8},{7,5},{8,6},{9,11},{10,... | collective-permute-start | bytes 786440 | tf_op jit(solution)/shard_map/ppermute | solution.py:391
  105.2 2.5 %collective-permute-done.11 = bf16[256,512]{1,0:T(8,128)(2,1)S(1)} collective-permute-done((bf16[256,512]{1,0:T(8,128)(2,1)S(1)}, bf16[256,512]{1,0:T(8,128)(2,1)S(1)}, u32[]{:S(2)}, u32[]{:S(2)}) %collective-permute-start.11) | collective-permute-done | bytes 262176 | tf_op jit(solution)/shard_map/ppermute | solution.py:390
  107.7 3.9 %collective-permute-done.14 = bf16[256,512]{1,0:T(8,128)(2,1)S(1)} collective-permute-done((bf16[256,512]{1,0:T(8,128)(2,1)S(1)}, bf16[256,512]{1,0:T(8,128)(2,1)S(1)}, u32[]{:S(2)}, u32[]{:S(2)}) %collective-permute-start.14) | collective-permute-done | bytes 262176 | tf_op jit(solution)/shard_map/ppermute | solution.py:391
  (37 shorter events, 14.5 us)
Async XLA Ops:
  0.0 42.5 %copy-start.1 = (bf16[1,256,512]{2,1,0:T(8,128)(2,1)S(1)}, bf16[1,256,512]{2,1,0:T(8,128)(2,1)}, u32[]{:S(2)}) copy-start(bf16[1,256,512]{2,1,0:T(8,128)(2,1)} %param.7) | copy-start | bytes 786436
  0.0 54.3 %copy-start.3 = (s32[32]{0:T(128)S(1)}, s32[32]{0:T(128)}, u32[]{:S(2)}) copy-start(s32[32]{0:T(128)} %spans.5) | copy-start | bytes 388
  0.0 54.3 %copy-start.2 = (s32[1,4096]{1,0:T(1,128)S(1)}, s32[1,4096]{1,0:T(1,128)}, u32[]{:S(2)}) copy-start(s32[1,4096]{1,0:T(1,128)} %param.11) | copy-start | bytes 49156
  0.0 66.7 %copy-start = (bf16[512,8192]{1,0:T(8,128)(2,1)S(1)}, bf16[512,8192]{1,0:T(8,128)(2,1)}, u32[]{:S(2)}) copy-start(bf16[512,8192]{1,0:T(8,128)(2,1)} %w_ref.5) | copy-start | bytes 25165828
  2.4 64.3 %collective-permute-start.7 = (bf16[8,512,512]{2,1,0:T(8,128)(2,1)S(1)}, bf16[8,512,512]{2,1,0:T(8,128)(2,1)S(1)}, u32[]{:S(2)}, u32[]{:S(2)}) collective-permute-start(bf16[8,512,512]{2,1,0:T(8,128)(2,1)S(1)} %pack.1), channel_id=1, source_target_pairs={{0,1},{1,0},{2,3},{3,2},{4,5},{5,4},{6,7},{7,6},{8,9},{9,8},{10,11... | collective-permute-start | bytes 12582920 | tf_op jit(solution)/shard_map/ppermute | solution.py:371
  15.9 8.1 %collective-permute-start = (bf16[136,256]{1,0:T(8,128)(2,1)S(1)}, bf16[136,256]{1,0:T(8,128)(2,1)S(1)}, u32[]{:S(2)}, u32[]{:S(2)}) collective-permute-start(bf16[136,256]{1,0:T(8,128)(2,1)S(1)} %prepare.1), channel_id=1, source_target_pairs={{0,16},{1,49},{2,18},{3,51},{4,20},{5,53},{6,22},{7,55},{8,24},{9,... | collective-permute-start | bytes 208904 | tf_op jit(solution)/shard_map/ppermute | solution.py:366
  24.0 8.0 %collective-permute-start.1 = (bf16[272,256]{1,0:T(8,128)(2,1)S(1)}, bf16[272,256]{1,0:T(8,128)(2,1)S(1)}, u32[]{:S(2)}, u32[]{:S(2)}) collective-permute-start(bf16[272,256]{1,0:T(8,128)(2,1)S(1)} %pad_maximum_fusion.1), channel_id=1, source_target_pairs={{0,48},{1,17},{2,50},{3,19},{4,52},{5,21},{6,54},{7,23},{8,56},{9,... | collective-permute-start | bytes 417800 | tf_op jit(solution)/shard_map/ppermute | solution.py:370
  32.0 8.5 %collective-permute-start.2 = (bf16[544,256]{1,0:T(8,128)(2,1)S(1)}, bf16[544,256]{1,0:T(8,128)(2,1)S(1)}, u32[]{:S(2)}, u32[]{:S(2)}) collective-permute-start(bf16[544,256]{1,0:T(8,128)(2,1)S(1)} %pad_maximum_fusion.blocks_ref), channel_id=1, source_target_pairs={{0,64},{1,193},{2,66},{3,195},{4,68},{5,197},{6,70},{7,199},{8,72}... | collective-permute-start | bytes 835592 | tf_op jit(solution)/shard_map/ppermute | solution.py:373
  35.1 21.5 %collective-permute-start.5 = (bf16[544,256]{1,0:T(8,128)(2,1)S(1)}, bf16[544,256]{1,0:T(8,128)(2,1)S(1)}, u32[]{:S(2)}, u32[]{:S(2)}) collective-permute-start(bf16[544,256]{1,0:T(8,128)(2,1)S(1)} %pad_maximum_fusion.blocks_ref), channel_id=1, source_target_pairs={{0,192},{1,65},{2,194},{3,67},{4,196},{5,69},{6,198},{7,71},{8,200... | collective-permute-start | bytes 835592 | tf_op jit(solution)/shard_map/ppermute | solution.py:374
  40.5 19.2 %collective-permute-start.3 = (bf16[544,256]{1,0:T(8,128)(2,1)S(1)}, bf16[544,256]{1,0:T(8,128)(2,1)S(1)}, u32[]{:S(2)}, u32[]{:S(2)}) collective-permute-start(bf16[544,256]{1,0:T(8,128)(2,1)S(1)} %collective-permute-done.2.a_ref), channel_id=1, source_target_pairs={{0,192},{1,65},{2,194},{3,67},{4,196},{5,69},{6,198},{7,71},{8,200... | collective-permute-start | bytes 835592 | tf_op jit(solution)/shard_map/ppermute | solution.py:375
  42.5 11.8 %collective-permute-start.4 = (bf16[256,512]{1,0:T(8,128)(2,1)S(1)}, bf16[256,512]{1,0:T(8,128)(2,1)S(1)}, u32[]{:S(2)}, u32[]{:S(2)}) collective-permute-start(bf16[256,512]{1,0:T(8,128)(2,1)S(1)} %bitcast.6), channel_id=1, source_target_pairs={{0,1},{1,0},{2,3},{3,2},{4,5},{5,4},{6,7},{7,6},{8,9},{9,8},{10,11... | collective-permute-start | bytes 786440 | tf_op jit(solution)/shard_map/ppermute | solution.py:367
  61.5 5.2 %collective-permute-start.6 = (bf16[136,2048]{1,0:T(8,128)(2,1)S(1)}, bf16[136,2048]{1,0:T(8,128)(2,1)S(1)}, u32[]{:S(2)}, u32[]{:S(2)}) collective-permute-start(bf16[136,2048]{1,0:T(8,128)(2,1)S(1)} %get-tuple-element.36.mine_ref), channel_id=1, source_target_pairs={{0,1},{1,0},{2,3},{3,2},{4,5},{5,4},{6,7},{7,6},{8,9},{9,8},{10,11... | collective-permute-start | bytes 1671176 | tf_op jit(solution)/shard_map/ppermute | solution.py:377
  67.7 7.4 %collective-permute-start.9 = (bf16[256,512]{1,0:T(8,128)(2,1)S(1)}, bf16[256,512]{1,0:T(8,128)(2,1)S(1)}, u32[]{:S(2)}, u32[]{:S(2)}) collective-permute-start(bf16[256,512]{1,0:T(8,128)(2,1)S(1)} %get-tuple-element.42), channel_id=1, source_target_pairs={{0,14},{1,3},{2,4},{3,1},{4,2},{5,7},{6,8},{7,5},{8,6},{9,11},{10,... | collective-permute-start | bytes 786440 | tf_op jit(solution)/shard_map/ppermute | solution.py:381
  70.9 9.4 %collective-permute-start.12 = (bf16[256,512]{1,0:T(8,128)(2,1)S(1)}, bf16[256,512]{1,0:T(8,128)(2,1)S(1)}, u32[]{:S(2)}, u32[]{:S(2)}) collective-permute-start(bf16[256,512]{1,0:T(8,128)(2,1)S(1)} %get-tuple-element.45), channel_id=1, source_target_pairs={{0,14},{1,3},{2,4},{3,1},{4,2},{5,7},{6,8},{7,5},{8,6},{9,11},{10,... | collective-permute-start | bytes 786440 | tf_op jit(solution)/shard_map/ppermute | solution.py:382
  73.0 31.6 %copy-start.4 = (s32[1,256]{1,0:T(1,128)S(1)}, s32[1,256]{1,0:T(1,128)}, u32[]{:S(2)}) copy-start(s32[1,256]{1,0:T(1,128)} %mask_hbm.1) | copy-start | bytes 3076
  75.2 21.8 %collective-permute-start.10 = (bf16[256,512]{1,0:T(8,128)(2,1)S(1)}, bf16[256,512]{1,0:T(8,128)(2,1)S(1)}, u32[]{:S(2)}, u32[]{:S(2)}) collective-permute-start(bf16[256,512]{1,0:T(8,128)(2,1)S(1)} %add.35), channel_id=1, source_target_pairs={{0,2},{1,15},{2,0},{3,5},{4,6},{5,3},{6,4},{7,9},{8,10},{9,7},{10,... | collective-permute-start | bytes 786440 | tf_op jit(solution)/shard_map/ppermute | solution.py:388
  80.3 20.8 %collective-permute-start.13 = (bf16[256,512]{1,0:T(8,128)(2,1)S(1)}, bf16[256,512]{1,0:T(8,128)(2,1)S(1)}, u32[]{:S(2)}, u32[]{:S(2)}) collective-permute-start(bf16[256,512]{1,0:T(8,128)(2,1)S(1)} %add.37), channel_id=1, source_target_pairs={{0,2},{1,15},{2,0},{3,5},{4,6},{5,3},{6,4},{7,9},{8,10},{9,7},{10,... | collective-permute-start | bytes 786440 | tf_op jit(solution)/shard_map/ppermute | solution.py:389
  83.2 4.4 %collective-permute-start.15 = (f32[8,128]{1,0:T(8,128)S(1)}, f32[8,128]{1,0:T(8,128)S(1)}, u32[]{:S(2)}, u32[]{:S(2)}) collective-permute-start(f32[8,128]{1,0:T(8,128)S(1)} %get-tuple-element.46), channel_id=1, source_target_pairs={{0,256},{1,513},{2,258},{3,515},{4,260},{5,517},{6,262},{7,519},{8... | collective-permute-start | bytes 12296 | tf_op jit(solution)/shard_map/ppermute | solution.py:386
  87.6 16.4 %collective-permute-start.16 = (f32[8,128]{1,0:T(8,128)S(1)}, f32[8,128]{1,0:T(8,128)S(1)}, u32[]{:S(2)}, u32[]{:S(2)}) collective-permute-start(f32[8,128]{1,0:T(8,128)S(1)} %collective-permute-done.15), channel_id=1, source_target_pairs={{0,1},{1,0},{2,3},{3,2},{4,5},{5,4},{6,7},{7,6},{8,9},{9,8},{10,11... | collective-permute-start | bytes 12296 | tf_op jit(solution)/shard_map/ppermute | solution.py:387
  94.2 11.0 %collective-permute-start.8 = (bf16[256,512]{1,0:T(8,128)(2,1)S(1)}, bf16[256,512]{1,0:T(8,128)(2,1)S(1)}, u32[]{:S(2)}, u32[]{:S(2)}) collective-permute-start(bf16[256,512]{1,0:T(8,128)(2,1)S(1)} %get-tuple-element.39), channel_id=1, source_target_pairs={{0,2},{1,15},{2,0},{3,5},{4,6},{5,3},{6,4},{7,9},{8,10},{9,7},{10,... | collective-permute-start | bytes 786440 | tf_op jit(solution)/shard_map/ppermute | solution.py:385
  97.0 10.7 %collective-permute-start.11 = (bf16[256,512]{1,0:T(8,128)(2,1)S(1)}, bf16[256,512]{1,0:T(8,128)(2,1)S(1)}, u32[]{:S(2)}, u32[]{:S(2)}) collective-permute-start(bf16[256,512]{1,0:T(8,128)(2,1)S(1)} %add.36), channel_id=1, source_target_pairs={{0,12},{1,5},{2,6},{3,15},{4,0},{5,9},{6,10},{7,3},{8,4},{9,13},{1... | collective-permute-start | bytes 786440 | tf_op jit(solution)/shard_map/ppermute | solution.py:390
  101.2 10.4 %collective-permute-start.14 = (bf16[256,512]{1,0:T(8,128)(2,1)S(1)}, bf16[256,512]{1,0:T(8,128)(2,1)S(1)}, u32[]{:S(2)}, u32[]{:S(2)}) collective-permute-start(bf16[256,512]{1,0:T(8,128)(2,1)S(1)} %add.38), channel_id=1, source_target_pairs={{0,14},{1,3},{2,4},{3,1},{4,2},{5,7},{6,8},{7,5},{8,6},{9,11},{10,... | collective-permute-start | bytes 786440 | tf_op jit(solution)/shard_map/ppermute | solution.py:391

commit v8 on v7

--- a/solution.py
+++ b/solution.py
@@ -341,19 +341,23 @@
     )(heads, w, other)
 
 
-def add_kernel(a_ref, b_ref, out_ref):
-    out_ref[...] = (a_ref[...].astype(jnp.float32) + b_ref[...].astype(jnp.float32)).astype(jnp.bfloat16)
-
-
-def add(a, b):
+def add_kernel(a_ref, b_ref, *refs):
+    *beside, out_ref = refs
+    total = a_ref[...].astype(jnp.float32) + b_ref[0].astype(jnp.float32)
+    out_ref[0] = total.astype(jnp.bfloat16)
+    for i, ref in enumerate(beside):
+        out_ref[1 + i] = ref[...]
+
+
+def add(a, b, *beside):
     return pl.pallas_call(
         add_kernel,
-        out_shape=jax.ShapeDtypeStruct(a.shape, a.dtype),
-        in_specs=[VMEM, VMEM],
+        out_shape=jax.ShapeDtypeStruct((1 + len(beside), *a.shape), a.dtype),
+        in_specs=[VMEM] * (2 + len(beside)),
         out_specs=VMEM,
         compiler_params=grant(4),
         name="add",
-    )(a, b)
+    )(a, b, *beside)
 
 
 def per_device(queries, keys, values, out_weight, segment_ids, loss_mask, span_order):
@@ -380,19 +384,18 @@
     heads, far_a, far_b = join(mine, theirs, out_weight, weight_other)
     far_a = lax.ppermute(far_a, "tensor", outward)
     far_b = lax.ppermute(far_b, "tensor", outward)
-    mid_a, mid_b, near_a, near_b, early, own = project(heads, out_weight, weight_other)
+    mid_a, mid_b, near_a, near_b, beside, own = project(heads, out_weight, weight_other)
     around = [(d * 16 + t, (d + 1 + t % 2) % 3 * 16 + t) for d in range(3) for t in range(16)]
-    early = lax.ppermute(early, "tensor", inward)
     one = lax.ppermute(tally, ("dp", "tensor"), around)
     two = lax.ppermute(one, "tensor", SWAP)
-    mid_a = lax.ppermute(add(mid_a, far_a), "tensor", inward)
-    mid_b = lax.ppermute(add(mid_b, far_b), "tensor", inward)
+    mid_a = lax.ppermute(add(mid_a, far_a[None]), "tensor", inward)
+    mid_b = lax.ppermute(add(mid_b, far_b[None], beside), "tensor", inward)
     near_a = lax.ppermute(add(near_a, mid_a), "tensor", perm_tensor(beyond))
     near_b = lax.ppermute(add(near_b, mid_b), "tensor", outward)
     count = (tally + one + two)[0, 0]
     scale_all = lax.axis_size("dp") * lax.axis_size("context") * queries.shape[1]
     weight = loss_mask[0].astype(f32) * scale_all / count
-    summed = own.astype(f32) + early.astype(f32) + near_a.astype(f32) + near_b.astype(f32)
+    summed = own.astype(f32) + mid_b[1].astype(f32) + near_a[0].astype(f32) + near_b[0].astype(f32)
     return (summed * weight[:, None]).astype(jnp.bfloat16)[None]
 
 

time: 113 us -> 110 us (0.973)
  starting transfers between devices: 72.5 us -> 69.5 us
    ppermute x3 -> x2, starting transfers between devices: 10.7 us -> 7.98 us  [the longest x1 5.09 us: per_device(): mid_b = lax.ppermute(add(mid_b, far_b[None], beside), 'tensor', inward)]
    ppermute x1, waiting for transfers between devices: 3.93 us -> 2.38 us  [per_device(): near_b = lax.ppermute(add(near_b, mid_b), 'tensor', outward)]
    ppermute x1, waiting for transfers between devices: 2.54 us -> 4 us  [per_device(): near_a = lax.ppermute(add(near_a, mid_a), 'tensor', perm_tensor(beyond))]
  transfers between devices with their start and end apart: 17 -> 16, of which waited for: 9 -> 9; matrix products, arithmetic and copies ran while one was open for 1% -> 1% of each run, Pallas kernels for 9% -> 9%
where the time goes in v8:
time: 110 us
  starting transfers between devices  69.5 us (63%)
  waiting for transfers between devices  24.4 us (22%)
  Pallas kernels  13.4 us (12%)
  other arithmetic  1.55 us (1%)
    ppermute x1, starting transfers between devices, per_device(): weight_other = lax.ppermute(packed, 'tensor', SWAP)  12.6 us
    ppermute x1, starting transfers between devices, per_device(): q_other = lax.ppermute(queries[0], 'tensor', SWAP)  10.7 us
    pallas_call x3, Pallas kernels, call(): pl.pallas_call(kernel, out_shape=tuple((jax.ShapeDtypeStruct(*m) for m in...  7.12 us
    ppermute x1, starting transfers between devices, per_device(): two = lax.ppermute(one, 'tensor', SWAP)  6.32 us
    ppermute x1, waiting for transfers between devices, per_device(): kv4 = cat(kv2, lax.ppermute(kv2, both, perm_context('z', outer)))  6.1 us
    ppermute x1, starting transfers between devices, per_device(): r1 = lax.ppermute(kv1, both, perm_context('z', inner))  5.32 us
    ppermute x1, starting transfers between devices, per_device(): mid_b = lax.ppermute(add(mid_b, far_b[None], beside), 'tensor', inward)  5.09 us
    ppermute x1, starting transfers between devices, per_device(): near_a = lax.ppermute(add(near_a, mid_a), 'tensor', perm_tensor(beyond))  4.91 us
  transfers between devices with their start and end apart: 16, of which 9 were waited for; matrix products, arithmetic and copies ran while one was open for 1% of the time, Pallas kernels for 9%

profile of v8, /device:TPU:1, one launch (start us, length us, event | category | flops | bytes accessed | tf_op | source)
XLA Modules:
  0.0 109.7 jit_solution(17308052285557331389)
XLA Ops:
  0.0 2.4 %pack.1 = bf16[8,512,512]{2,1,0:T(8,128)(2,1)S(1)} custom-call(bf16[512,8192]{1,0:T(8,128)(2,1)} %w_ref.5), custom_call_target="tpu_custom_call" | custom-call | tf_op jit(solution)/shard_map/pack/pallas_call | solution.py:122
  2.4 12.6 %collective-permute-start.7 = (bf16[8,512,512]{2,1,0:T(8,128)(2,1)S(1)}, bf16[8,512,512]{2,1,0:T(8,128)(2,1)S(1)}, u32[]{:S(2)}, u32[]{:S(2)}) collective-permute-start(bf16[8,512,512]{2,1,0:T(8,128)(2,1)S(1)} %pack.1), channel_id=1, source_target_pairs={{0,1},{1,0},{2,3},{3,2},{4,5},{5,4},{6,7},{7,6},{8,9},{9,8},{10,11... | collective-permute-start | bytes 12582920 | tf_op jit(solution)/shard_map/ppermute | solution.py:375
  15.9 5.3 %collective-permute-start = (bf16[136,256]{1,0:T(8,128)(2,1)S(1)}, bf16[136,256]{1,0:T(8,128)(2,1)S(1)}, u32[]{:S(2)}, u32[]{:S(2)}) collective-permute-start(bf16[136,256]{1,0:T(8,128)(2,1)S(1)} %prepare.1), channel_id=1, source_target_pairs={{0,16},{1,49},{2,18},{3,51},{4,20},{5,53},{6,22},{7,55},{8,24},{9,... | collective-permute-start | bytes 208904 | tf_op jit(solution)/shard_map/ppermute | solution.py:370
  21.2 2.7 %collective-permute-done = bf16[136,256]{1,0:T(8,128)(2,1)S(1)} collective-permute-done((bf16[136,256]{1,0:T(8,128)(2,1)S(1)}, bf16[136,256]{1,0:T(8,128)(2,1)S(1)}, u32[]{:S(2)}, u32[]{:S(2)}) %collective-permute-start) | collective-permute-done | bytes 69664 | tf_op jit(solution)/shard_map/ppermute | solution.py:370
  24.0 1.9 %collective-permute-start.1 = (bf16[272,256]{1,0:T(8,128)(2,1)S(1)}, bf16[272,256]{1,0:T(8,128)(2,1)S(1)}, u32[]{:S(2)}, u32[]{:S(2)}) collective-permute-start(bf16[272,256]{1,0:T(8,128)(2,1)S(1)} %pad_maximum_fusion.1), channel_id=1, source_target_pairs={{0,48},{1,17},{2,50},{3,19},{4,52},{5,21},{6,54},{7,23},{8,56},{9,... | collective-permute-start | bytes 417800 | tf_op jit(solution)/shard_map/ppermute | solution.py:374
  25.9 6.1 %collective-permute-done.1 = bf16[272,256]{1,0:T(8,128)(2,1)S(1)} collective-permute-done((bf16[272,256]{1,0:T(8,128)(2,1)S(1)}, bf16[272,256]{1,0:T(8,128)(2,1)S(1)}, u32[]{:S(2)}, u32[]{:S(2)}) %collective-permute-start.1) | collective-permute-done | bytes 139296 | tf_op jit(solution)/shard_map/ppermute | solution.py:374
  32.0 3.1 %collective-permute-start.2 = (bf16[544,256]{1,0:T(8,128)(2,1)S(1)}, bf16[544,256]{1,0:T(8,128)(2,1)S(1)}, u32[]{:S(2)}, u32[]{:S(2)}) collective-permute-start(bf16[544,256]{1,0:T(8,128)(2,1)S(1)} %pad_maximum_fusion.blocks_ref), channel_id=1, source_target_pairs={{0,64},{1,193},{2,66},{3,195},{4,68},{5,197},{6,70},{7,199},{8,72}... | collective-permute-start | bytes 835592 | tf_op jit(solution)/shard_map/ppermute | solution.py:377
  35.1 1.9 %collective-permute-start.5 = (bf16[544,256]{1,0:T(8,128)(2,1)S(1)}, bf16[544,256]{1,0:T(8,128)(2,1)S(1)}, u32[]{:S(2)}, u32[]{:S(2)}) collective-permute-start(bf16[544,256]{1,0:T(8,128)(2,1)S(1)} %pad_maximum_fusion.blocks_ref), channel_id=1, source_target_pairs={{0,192},{1,65},{2,194},{3,67},{4,196},{5,69},{6,198},{7,71},{8,200... | collective-permute-start | bytes 835592 | tf_op jit(solution)/shard_map/ppermute | solution.py:378
  37.0 3.5 %collective-permute-done.2.a_ref = bf16[544,256]{1,0:T(8,128)(2,1)S(1)} collective-permute-done((bf16[544,256]{1,0:T(8,128)(2,1)S(1)}, bf16[544,256]{1,0:T(8,128)(2,1)S(1)}, u32[]{:S(2)}, u32[]{:S(2)}) %collective-permute-start.2) | collective-permute-done | bytes 278560 | tf_op jit(solution)/shard_map/ppermute | solution.py:377
  42.5 10.7 %collective-permute-start.4 = (bf16[256,512]{1,0:T(8,128)(2,1)S(1)}, bf16[256,512]{1,0:T(8,128)(2,1)S(1)}, u32[]{:S(2)}, u32[]{:S(2)}) collective-permute-start(bf16[256,512]{1,0:T(8,128)(2,1)S(1)} %bitcast.21), channel_id=1, source_target_pairs={{0,1},{1,0},{2,3},{3,2},{4,5},{5,4},{6,7},{7,6},{8,9},{9,8},{10,11... | collective-permute-start | bytes 786440 | tf_op jit(solution)/shard_map/ppermute | solution.py:371
  54.3 2.3 %shard_map.73 = (bf16[2,1024,128]{2,1,0:T(8,128)(2,1)S(1)}, f32[2,1,128]{2,1,0:T(1,128)S(1)}, f32[2,1,1024]{2,1,0:T(1,128)S(1)}, f32[2,1,1024]{2,1,0:T(1,128)S(1...) custom-call(s32[32]{0:T(128)S(1)} %copy-done.3, s32[32,128]{1,0:T(8,128)S(1)} %bitcast.23, ...), custom_call_target="tpu_custom_call" | custom-call | tf_op jit(solution)/shard_map/pallas_call | solution.py:257
  56.7 3.1 %shard_map.74 = (f32[2,1,1024]{2,1,0:T(1,128)S(1)}, f32[2,1,1024]{2,1,0:T(1,128)S(1)}, f32[2,128,1024]{2,1,0:T(8,128)S(1)}, f32[8,128]{1,0:T(8,128)S(1)}) custom-call(s32[32]{0:T(128)S(1)} %copy-done.3, bf16[544,256]{1,0:T(8,128)(2,1)S(1)} %collective-permute-done.2.a_ref, bf16[544,256]{1,0:T(8,128)(2,1)S(1)} %collective-permute-done.5.b_ref, ...), custom_call_target="tpu_custom_call" | custom-call | tf_op jit(solution)/shard_map/pallas_call | solution.py:257
  61.5 3.7 %collective-permute-start.6 = (bf16[136,2048]{1,0:T(8,128)(2,1)S(1)}, bf16[136,2048]{1,0:T(8,128)(2,1)S(1)}, u32[]{:S(2)}, u32[]{:S(2)}) collective-permute-start(bf16[136,2048]{1,0:T(8,128)(2,1)S(1)} %get-tuple-element.36.mine_ref), channel_id=1, source_target_pairs={{0,1},{1,0},{2,3},{3,2},{4,5},{5,4},{6,7},{7,6},{8,9},{9,8},{10,11... | collective-permute-start | bytes 1671176 | tf_op jit(solution)/shard_map/ppermute | solution.py:381
  67.7 3.2 %collective-permute-start.8 = (bf16[256,512]{1,0:T(8,128)(2,1)S(1)}, bf16[256,512]{1,0:T(8,128)(2,1)S(1)}, u32[]{:S(2)}, u32[]{:S(2)}) collective-permute-start(bf16[256,512]{1,0:T(8,128)(2,1)S(1)} %get-tuple-element.40), channel_id=1, source_target_pairs={{0,14},{1,3},{2,4},{3,1},{4,2},{5,7},{6,8},{7,5},{8,6},{9,11},{10,... | collective-permute-start | bytes 786440 | tf_op jit(solution)/shard_map/ppermute | solution.py:386
  70.9 2.1 %collective-permute-start.10 = (bf16[256,512]{1,0:T(8,128)(2,1)S(1)}, bf16[256,512]{1,0:T(8,128)(2,1)S(1)}, u32[]{:S(2)}, u32[]{:S(2)}) collective-permute-start(bf16[256,512]{1,0:T(8,128)(2,1)S(1)} %get-tuple-element.44), channel_id=1, source_target_pairs={{0,14},{1,3},{2,4},{3,1},{4,2},{5,7},{6,8},{7,5},{8,6},{9,11},{10,... | collective-permute-start | bytes 786440 | tf_op jit(solution)/shard_map/ppermute | solution.py:385
  75.2 5.1 %collective-permute-start.9 = (bf16[2,256,512]{2,1,0:T(8,128)(2,1)S(1)}, bf16[2,256,512]{2,1,0:T(8,128)(2,1)S(1)}, u32[]{:S(2)}, u32[]{:S(2)}) collective-permute-start(bf16[2,256,512]{2,1,0:T(8,128)(2,1)S(1)} %add.43), channel_id=1, source_target_pairs={{0,2},{1,15},{2,0},{3,5},{4,6},{5,3},{6,4},{7,9},{8,10},{9,7},{10,... | collective-permute-start | bytes 1572872 | tf_op jit(solution)/shard_map/ppermute | solution.py:392
  80.3 2.9 %collective-permute-start.11 = (bf16[1,256,512]{2,1,0:T(8,128)(2,1)S(1)}, bf16[1,256,512]{2,1,0:T(8,128)(2,1)S(1)}, u32[]{:S(2)}, u32[]{:S(2)}) collective-permute-start(bf16[1,256,512]{2,1,0:T(8,128)(2,1)S(1)} %add.44), channel_id=1, source_target_pairs={{0,2},{1,15},{2,0},{3,5},{4,6},{5,3},{6,4},{7,9},{8,10},{9,7},{10,... | collective-permute-start | bytes 786440 | tf_op jit(solution)/shard_map/ppermute | solution.py:391
  83.2 1.9 %collective-permute-start.14 = (f32[8,128]{1,0:T(8,128)S(1)}, f32[8,128]{1,0:T(8,128)S(1)}, u32[]{:S(2)}, u32[]{:S(2)}) collective-permute-start(f32[8,128]{1,0:T(8,128)S(1)} %get-tuple-element.46), channel_id=1, source_target_pairs={{0,256},{1,513},{2,258},{3,515},{4,260},{5,517},{6,262},{7,519},{8... | collective-permute-start | bytes 12296 | tf_op jit(solution)/shard_map/ppermute | solution.py:389
  85.2 2.7 %collective-permute-done.14 = f32[8,128]{1,0:T(8,128)S(1)} collective-permute-done((f32[8,128]{1,0:T(8,128)S(1)}, f32[8,128]{1,0:T(8,128)S(1)}, u32[]{:S(2)}, u32[]{:S(2)}) %collective-permute-start.14) | collective-permute-done | bytes 4128 | tf_op jit(solution)/shard_map/ppermute | solution.py:389
  87.9 6.3 %collective-permute-start.15 = (f32[8,128]{1,0:T(8,128)S(1)}, f32[8,128]{1,0:T(8,128)S(1)}, u32[]{:S(2)}, u32[]{:S(2)}) collective-permute-start(f32[8,128]{1,0:T(8,128)S(1)} %collective-permute-done.14), channel_id=1, source_target_pairs={{0,1},{1,0},{2,3},{3,2},{4,5},{5,4},{6,7},{7,6},{8,9},{9,8},{10,11... | collective-permute-start | bytes 12296 | tf_op jit(solution)/shard_map/ppermute | solution.py:390
  94.3 4.9 %collective-permute-start.12 = (bf16[1,256,512]{2,1,0:T(8,128)(2,1)S(1)}, bf16[1,256,512]{2,1,0:T(8,128)(2,1)S(1)}, u32[]{:S(2)}, u32[]{:S(2)}) collective-permute-start(bf16[1,256,512]{2,1,0:T(8,128)(2,1)S(1)} %add.45), channel_id=1, source_target_pairs={{0,12},{1,5},{2,6},{3,15},{4,0},{5,9},{6,10},{7,3},{8,4},{9,13},{1... | collective-permute-start | bytes 786440 | tf_op jit(solution)/shard_map/ppermute | solution.py:393
  99.3 1.9 %collective-permute-start.13 = (bf16[1,256,512]{2,1,0:T(8,128)(2,1)S(1)}, bf16[1,256,512]{2,1,0:T(8,128)(2,1)S(1)}, u32[]{:S(2)}, u32[]{:S(2)}) collective-permute-start(bf16[1,256,512]{2,1,0:T(8,128)(2,1)S(1)} %add.46), channel_id=1, source_target_pairs={{0,14},{1,3},{2,4},{3,1},{4,2},{5,7},{6,8},{7,5},{8,6},{9,11},{10,... | collective-permute-start | bytes 786440 | tf_op jit(solution)/shard_map/ppermute | solution.py:394
  102.4 4.0 %collective-permute-done.12 = bf16[1,256,512]{2,1,0:T(8,128)(2,1)S(1)} collective-permute-done((bf16[1,256,512]{2,1,0:T(8,128)(2,1)S(1)}, bf16[1,256,512]{2,1,0:T(8,128)(2,1)S(1)}, u32[]{:S(2)}, u32[]{:S(2)}) %collective-permute-start.12) | collective-permute-done | bytes 262176 | tf_op jit(solution)/shard_map/ppermute | solution.py:393
  106.4 2.4 %collective-permute-done.13 = bf16[1,256,512]{2,1,0:T(8,128)(2,1)S(1)} collective-permute-done((bf16[1,256,512]{2,1,0:T(8,128)(2,1)S(1)}, bf16[1,256,512]{2,1,0:T(8,128)(2,1)S(1)}, u32[]{:S(2)}, u32[]{:S(2)}) %collective-permute-start.13) | collective-permute-done | bytes 262176 | tf_op jit(solution)/shard_map/ppermute | solution.py:394
  (35 shorter events, 12.6 us)
Async XLA Ops:
  0.0 42.5 %copy-start.1 = (bf16[1,256,512]{2,1,0:T(8,128)(2,1)S(1)}, bf16[1,256,512]{2,1,0:T(8,128)(2,1)}, u32[]{:S(2)}) copy-start(bf16[1,256,512]{2,1,0:T(8,128)(2,1)} %param.7) | copy-start | bytes 786436
  0.0 54.3 %copy-start.3 = (s32[32]{0:T(128)S(1)}, s32[32]{0:T(128)}, u32[]{:S(2)}) copy-start(s32[32]{0:T(128)} %spans.5) | copy-start | bytes 388
  0.0 54.3 %copy-start.2 = (s32[1,4096]{1,0:T(1,128)S(1)}, s32[1,4096]{1,0:T(1,128)}, u32[]{:S(2)}) copy-start(s32[1,4096]{1,0:T(1,128)} %param.11) | copy-start | bytes 49156
  0.0 66.7 %copy-start = (bf16[512,8192]{1,0:T(8,128)(2,1)S(1)}, bf16[512,8192]{1,0:T(8,128)(2,1)}, u32[]{:S(2)}) copy-start(bf16[512,8192]{1,0:T(8,128)(2,1)} %w_ref.5) | copy-start | bytes 25165828
  2.4 64.3 %collective-permute-start.7 = (bf16[8,512,512]{2,1,0:T(8,128)(2,1)S(1)}, bf16[8,512,512]{2,1,0:T(8,128)(2,1)S(1)}, u32[]{:S(2)}, u32[]{:S(2)}) collective-permute-start(bf16[8,512,512]{2,1,0:T(8,128)(2,1)S(1)} %pack.1), channel_id=1, source_target_pairs={{0,1},{1,0},{2,3},{3,2},{4,5},{5,4},{6,7},{7,6},{8,9},{9,8},{10,11... | collective-permute-start | bytes 12582920 | tf_op jit(solution)/shard_map/ppermute | solution.py:375
  15.9 8.1 %collective-permute-start = (bf16[136,256]{1,0:T(8,128)(2,1)S(1)}, bf16[136,256]{1,0:T(8,128)(2,1)S(1)}, u32[]{:S(2)}, u32[]{:S(2)}) collective-permute-start(bf16[136,256]{1,0:T(8,128)(2,1)S(1)} %prepare.1), channel_id=1, source_target_pairs={{0,16},{1,49},{2,18},{3,51},{4,20},{5,53},{6,22},{7,55},{8,24},{9,... | collective-permute-start | bytes 208904 | tf_op jit(solution)/shard_map/ppermute | solution.py:370
  24.0 8.0 %collective-permute-start.1 = (bf16[272,256]{1,0:T(8,128)(2,1)S(1)}, bf16[272,256]{1,0:T(8,128)(2,1)S(1)}, u32[]{:S(2)}, u32[]{:S(2)}) collective-permute-start(bf16[272,256]{1,0:T(8,128)(2,1)S(1)} %pad_maximum_fusion.1), channel_id=1, source_target_pairs={{0,48},{1,17},{2,50},{3,19},{4,52},{5,21},{6,54},{7,23},{8,56},{9,... | collective-permute-start | bytes 417800 | tf_op jit(solution)/shard_map/ppermute | solution.py:374
  32.0 8.5 %collective-permute-start.2 = (bf16[544,256]{1,0:T(8,128)(2,1)S(1)}, bf16[544,256]{1,0:T(8,128)(2,1)S(1)}, u32[]{:S(2)}, u32[]{:S(2)}) collective-permute-start(bf16[544,256]{1,0:T(8,128)(2,1)S(1)} %pad_maximum_fusion.blocks_ref), channel_id=1, source_target_pairs={{0,64},{1,193},{2,66},{3,195},{4,68},{5,197},{6,70},{7,199},{8,72}... | collective-permute-start | bytes 835592 | tf_op jit(solution)/shard_map/ppermute | solution.py:377
  35.1 21.5 %collective-permute-start.5 = (bf16[544,256]{1,0:T(8,128)(2,1)S(1)}, bf16[544,256]{1,0:T(8,128)(2,1)S(1)}, u32[]{:S(2)}, u32[]{:S(2)}) collective-permute-start(bf16[544,256]{1,0:T(8,128)(2,1)S(1)} %pad_maximum_fusion.blocks_ref), channel_id=1, source_target_pairs={{0,192},{1,65},{2,194},{3,67},{4,196},{5,69},{6,198},{7,71},{8,200... | collective-permute-start | bytes 835592 | tf_op jit(solution)/shard_map/ppermute | solution.py:378
  40.5 19.2 %collective-permute-start.3 = (bf16[544,256]{1,0:T(8,128)(2,1)S(1)}, bf16[544,256]{1,0:T(8,128)(2,1)S(1)}, u32[]{:S(2)}, u32[]{:S(2)}) collective-permute-start(bf16[544,256]{1,0:T(8,128)(2,1)S(1)} %collective-permute-done.2.a_ref), channel_id=1, source_target_pairs={{0,192},{1,65},{2,194},{3,67},{4,196},{5,69},{6,198},{7,71},{8,200... | collective-permute-start | bytes 835592 | tf_op jit(solution)/shard_map/ppermute | solution.py:379
  42.5 11.8 %collective-permute-start.4 = (bf16[256,512]{1,0:T(8,128)(2,1)S(1)}, bf16[256,512]{1,0:T(8,128)(2,1)S(1)}, u32[]{:S(2)}, u32[]{:S(2)}) collective-permute-start(bf16[256,512]{1,0:T(8,128)(2,1)S(1)} %bitcast.21), channel_id=1, source_target_pairs={{0,1},{1,0},{2,3},{3,2},{4,5},{5,4},{6,7},{7,6},{8,9},{9,8},{10,11... | collective-permute-start | bytes 786440 | tf_op jit(solution)/shard_map/ppermute | solution.py:371
  61.5 5.2 %collective-permute-start.6 = (bf16[136,2048]{1,0:T(8,128)(2,1)S(1)}, bf16[136,2048]{1,0:T(8,128)(2,1)S(1)}, u32[]{:S(2)}, u32[]{:S(2)}) collective-permute-start(bf16[136,2048]{1,0:T(8,128)(2,1)S(1)} %get-tuple-element.36.mine_ref), channel_id=1, source_target_pairs={{0,1},{1,0},{2,3},{3,2},{4,5},{5,4},{6,7},{7,6},{8,9},{9,8},{10,11... | collective-permute-start | bytes 1671176 | tf_op jit(solution)/shard_map/ppermute | solution.py:381
  67.7 7.4 %collective-permute-start.8 = (bf16[256,512]{1,0:T(8,128)(2,1)S(1)}, bf16[256,512]{1,0:T(8,128)(2,1)S(1)}, u32[]{:S(2)}, u32[]{:S(2)}) collective-permute-start(bf16[256,512]{1,0:T(8,128)(2,1)S(1)} %get-tuple-element.40), channel_id=1, source_target_pairs={{0,14},{1,3},{2,4},{3,1},{4,2},{5,7},{6,8},{7,5},{8,6},{9,11},{10,... | collective-permute-start | bytes 786440 | tf_op jit(solution)/shard_map/ppermute | solution.py:386
  70.9 9.4 %collective-permute-start.10 = (bf16[256,512]{1,0:T(8,128)(2,1)S(1)}, bf16[256,512]{1,0:T(8,128)(2,1)S(1)}, u32[]{:S(2)}, u32[]{:S(2)}) collective-permute-start(bf16[256,512]{1,0:T(8,128)(2,1)S(1)} %get-tuple-element.44), channel_id=1, source_target_pairs={{0,14},{1,3},{2,4},{3,1},{4,2},{5,7},{6,8},{7,5},{8,6},{9,11},{10,... | collective-permute-start | bytes 786440 | tf_op jit(solution)/shard_map/ppermute | solution.py:385
  73.0 28.8 %copy-start.4 = (s32[1,256]{1,0:T(1,128)S(1)}, s32[1,256]{1,0:T(1,128)}, u32[]{:S(2)}) copy-start(s32[1,256]{1,0:T(1,128)} %mask_hbm.1) | copy-start | bytes 3076
  75.2 24.1 %collective-permute-start.9 = (bf16[2,256,512]{2,1,0:T(8,128)(2,1)S(1)}, bf16[2,256,512]{2,1,0:T(8,128)(2,1)S(1)}, u32[]{:S(2)}, u32[]{:S(2)}) collective-permute-start(bf16[2,256,512]{2,1,0:T(8,128)(2,1)S(1)} %add.43), channel_id=1, source_target_pairs={{0,2},{1,15},{2,0},{3,5},{4,6},{5,3},{6,4},{7,9},{8,10},{9,7},{10,... | collective-permute-start | bytes 1572872 | tf_op jit(solution)/shard_map/ppermute | solution.py:392
  80.3 13.9 %collective-permute-start.11 = (bf16[1,256,512]{2,1,0:T(8,128)(2,1)S(1)}, bf16[1,256,512]{2,1,0:T(8,128)(2,1)S(1)}, u32[]{:S(2)}, u32[]{:S(2)}) collective-permute-start(bf16[1,256,512]{2,1,0:T(8,128)(2,1)S(1)} %add.44), channel_id=1, source_target_pairs={{0,2},{1,15},{2,0},{3,5},{4,6},{5,3},{6,4},{7,9},{8,10},{9,7},{10,... | collective-permute-start | bytes 786440 | tf_op jit(solution)/shard_map/ppermute | solution.py:391
  83.2 4.6 %collective-permute-start.14 = (f32[8,128]{1,0:T(8,128)S(1)}, f32[8,128]{1,0:T(8,128)S(1)}, u32[]{:S(2)}, u32[]{:S(2)}) collective-permute-start(f32[8,128]{1,0:T(8,128)S(1)} %get-tuple-element.46), channel_id=1, source_target_pairs={{0,256},{1,513},{2,258},{3,515},{4,260},{5,517},{6,262},{7,519},{8... | collective-permute-start | bytes 12296 | tf_op jit(solution)/shard_map/ppermute | solution.py:389
  87.9 13.3 %collective-permute-start.15 = (f32[8,128]{1,0:T(8,128)S(1)}, f32[8,128]{1,0:T(8,128)S(1)}, u32[]{:S(2)}, u32[]{:S(2)}) collective-permute-start(f32[8,128]{1,0:T(8,128)S(1)} %collective-permute-done.14), channel_id=1, source_target_pairs={{0,1},{1,0},{2,3},{3,2},{4,5},{5,4},{6,7},{7,6},{8,9},{9,8},{10,11... | collective-permute-start | bytes 12296 | tf_op jit(solution)/shard_map/ppermute | solution.py:390
  94.3 12.1 %collective-permute-start.12 = (bf16[1,256,512]{2,1,0:T(8,128)(2,1)S(1)}, bf16[1,256,512]{2,1,0:T(8,128)(2,1)S(1)}, u32[]{:S(2)}, u32[]{:S(2)}) collective-permute-start(bf16[1,256,512]{2,1,0:T(8,128)(2,1)S(1)} %add.45), channel_id=1, source_target_pairs={{0,12},{1,5},{2,6},{3,15},{4,0},{5,9},{6,10},{7,3},{8,4},{9,13},{1... | collective-permute-start | bytes 786440 | tf_op jit(solution)/shard_map/ppermute | solution.py:393
  99.3 9.5 %collective-permute-start.13 = (bf16[1,256,512]{2,1,0:T(8,128)(2,1)S(1)}, bf16[1,256,512]{2,1,0:T(8,128)(2,1)S(1)}, u32[]{:S(2)}, u32[]{:S(2)}) collective-permute-start(bf16[1,256,512]{2,1,0:T(8,128)(2,1)S(1)} %add.46), channel_id=1, source_target_pairs={{0,14},{1,3},{2,4},{3,1},{4,2},{5,7},{6,8},{7,5},{8,6},{9,11},{10,... | collective-permute-start | bytes 786440 | tf_op jit(solution)/shard_map/ppermute | solution.py:394
